TPU v7x, 256 devices: a whole 4x4x8 slice. The times are simulated.
256 devices in a mesh: var: 32 (over y, z_hi, core), smp: 8 (over z_lo, x).
Axes of the slice: x: 4, y: 4, z: 8 (z_hi: 4, z_lo: 2; z = z_hi * 2 + z_lo), core: 2. Of those that a mesh axis runs over, the one named last changes fastest.
Arguments:
- genotype: bfloat16 [65536, 16384], P('var', 'smp'), may hold values from 0 to 2
- labels: int32 [65536], P('var'), may hold values from 0 to 7, as said below
- probes: bfloat16 [20, 16384], P(None, 'smp'), may hold values from -6 to 6
- phenotype: bfloat16 [16384], P('smp'), may hold values from -6 to 6
Outputs:
- moments: float32 [8, 21, 8, 2048], P(None, None, 'smp', 'var')
Inputs may be any that keep to these rules, and one draw needn't show every extreme that they name: Within each aligned block of 2048 variants the labels never fall, and every one of the 8 components appears in every block.
All inputs are finite; a program needn't handle non-finite values.
Results may differ from a plain program's by a relative error of at most 0.0039.
Values sent between devices are 32-bit elements; how exact they have to be, the bound alone decides.
No kernel may reach another device: no remote copies, remote signals or barrier semaphores. Data moves between devices by JAX's collectives and lax.ppermute only.
A program may use at most 64 MiB of HBM per device.

v0:
```python
import jax
import jax.numpy as jnp
from jax import lax
from jax.sharding import PartitionSpec as P

QDEV = 1
K = 8
NV = 21


EPS = 1e-06


def sent_to_all(array, axis):
    copies = jnp.broadcast_to(array, (lax.axis_size(axis), *array.shape))
    return lax.all_to_all(copies, axis, split_axis=0, concat_axis=0, tiled=True)


def over_copies(array, axis):
    return sent_to_all(array, axis).sum(axis=0)


def in_blocks(array, dim, devices):
    dims = array.shape
    tiles = array.reshape(*dims[:dim], devices, dims[dim] // devices, *dims[dim + 1 :])
    return jnp.moveaxis(tiles, dim, 0)


def sent_and_summed(array, axis, dim):
    tiles = in_blocks(array, dim, lax.axis_size(axis))
    arrived = lax.all_to_all(tiles, axis, split_axis=0, concat_axis=0, tiled=True)
    return arrived.sum(axis=0)


def body(genotype, labels, probes, phenotype):
    variants = genotype.shape[0]
    samples = genotype.shape[1]
    total = samples * lax.axis_size("smp")
    member = (labels[None, :] == jnp.arange(K, dtype=jnp.int32)[:, None]).astype(jnp.float32)
    counts = over_copies(jnp.sum(member, axis=1), "var")
    dosage = genotype.astype(jnp.float32)
    sums = over_copies(jnp.sum(dosage, axis=1), "smp")
    centered = dosage - (sums / total)[:, None]
    squares = over_copies(jnp.sum(centered * centered, axis=1), "smp")
    scaled = (centered * lax.rsqrt(squares / total + EPS)[:, None]).astype(jnp.bfloat16)
    vectors = jnp.concatenate([probes, phenotype[None, :]], axis=0)
    partial_value = lax.dot_general(
        vectors, scaled, (((1,), (1,)), ((), ())), preferred_element_type=jnp.float32
    )
    projected = over_copies(partial_value, "smp")
    weights = (projected[None, :, :] * member[:, None, :] / counts[:, None, None]).astype(
        jnp.bfloat16
    )
    weights = weights.reshape(K * NV, variants)
    terms = jnp.dot(weights, scaled, preferred_element_type=jnp.float32)
    terms = terms.reshape(K, NV, QDEV, samples // QDEV)
    return sent_and_summed(terms, "var", 3)


def solution(mesh):
    placed = (P("var", "smp"), P("var"), P(None, "smp"), P("smp"))
    return jax.shard_map(
        body, mesh=mesh, in_specs=placed, out_specs=P(None, None, "smp", "var"), check_vma=False
    )
```

profile of v0, /device:TPU:6, one launch (start us, length us, event | category | flops | bytes accessed | tf_op | source)
XLA Modules:
  0.0 160.3 jit_solution(135499815257199648)
XLA Ops:
  0.0 12.3 %copy.18 = bf16[2048,2048]{0,1:T(8,128)(2,1)} copy(bf16[2048,2048]{1,0:T(8,128)(2,1)} %param.4) | data formatting | bytes 16777216 | tf_op args[0]
  12.3 0.0 copy-start.2
  12.3 0.0 copy-start.1
  12.3 4.8 %convert_reduce_fusion = f32[2048]{0:T(1024)S(1)} fusion(bf16[2048,2048]{0,1:T(8,128)(2,1)} %copy.18), kind=kLoop, calls=%fused_computation.1 | loop fusion | flops 8386560 | bytes 8396800 | tf_op jit(solution)/shard_map/reduce_sum | solution.py:42
  17.1 10.2 %all_to_all.28 = f32[8,1,2048]{2,1,0:T(1,128)S(1)} all-to-all(f32[8,1,2048]{2,1,0:T(1,128)S(1)} %broadcast_in_dim.11), channel_id=1, replica_groups=mesh['var'=32,'smp'=8] {'smp'}, dimensions={0} | all-to-all | bytes 131072 | tf_op jit(solution)/shard_map/all_to_all | solution.py:16
  27.3 0.1 reduce_sum.75
  27.4 5.6 %fusion.2 = f32[2048]{0:T(1024)S(1)} fusion(bf16[2048,2048]{0,1:T(8,128)(2,1)} %copy.18, f32[2048]{0:T(1024)S(1)} %broadcast_multiply_fusion), kind=kLoop, calls=%fused_computation.4 | loop fusion | flops 16775168 | bytes 8404992 | tf_op jit(solution)/shard_map/reduce_sum | solution.py:44
  33.0 0.7 broadcast_in_dim.24
  33.7 5.3 %all-to-all-start.1 = ((f32[8,1,2048]{2,1,0:T(1,128)}), f32[8,1,2048]{2,1,0:T(1,128)S(1)}, u32[]{:S(2)}, u32[]{:S(2)}) async-start(f32[8,1,2048]{2,1,0:T(1,128)} %broadcast_in_dim.24), calls=%async_computation.1 | async-start | bytes 131072 | tf_op jit(solution)/shard_map/all_to_all | solution.py:16
  39.0 0.0 copy-done.2
  39.0 0.0 copy-done.1
  39.0 0.1 fusion.14
  39.2 4.1 %all-to-all-done.1 = f32[8,1,2048]{2,1,0:T(1,128)S(1)} async-done(((f32[8,1,2048]{2,1,0:T(1,128)}), f32[8,1,2048]{2,1,0:T(1,128)S(1)}, u32[]{:S(2)}, u32[]{:S(2)}) %all-to-all-start.1) | async-done | bytes 65568 | tf_op jit(solution)/shard_map/all_to_all | solution.py:16
  43.3 0.6 broadcast_in_dim.26
  43.9 10.6 %all-to-all-start.3 = ((f32[32,1,8]{2,1,0:T(1,128)}), f32[32,1,8]{2,1,0:T(1,128)S(1)}, u32[]{:S(2)}, u32[]{:S(2)}) async-start(f32[32,1,8]{2,1,0:T(1,128)} %broadcast_in_dim.26), calls=%async_computation.3 | async-start | bytes 32768 | tf_op jit(solution)/shard_map/all_to_all | solution.py:16
  54.5 0.1 reduce_sum.77
  54.6 0.0 copy-start
  54.6 9.8 %fusion.3 = bf16[2048,2048]{0,1:T(8,128)(2,1)} fusion(bf16[2048,2048]{0,1:T(8,128)(2,1)} %copy.18, f32[2048]{0:T(1024)S(1)} %add_rsqrt_fusion, f32[2048]{0:T(1024)S(1)} %broadcast_multiply_fusion), kind=kLoop, calls=%fused_computation.5 | loop fusion | flops 16777216 | bytes 16793600 | tf_op jit(solution)/shard_map/convert_element_type | solution.py:45
  64.4 0.0 copy-done
  64.4 4.6 %fusion.9 = f32[21,2048]{1,0:T(8,128)S(1)} fusion(bf16[2048,2048]{0,1:T(8,128)(2,1)} %fusion.3, bf16[1,2048]{1,0:T(2,128)(2,1)S(1)} %broadcast_in_dim.10, bf16[20,2048]{1,0:T(8,128)(2,1)S(1)} %copy-done), kind=kOutput, calls=%fused_computation.12 | convolution fusion | flops 176332800 | bytes 8646656 | tf_op jit(solution)/shard_map/dot_general | solution.py:47
  69.0 0.0 all-to-all-done.3
  69.0 1.4 broadcast_in_dim.25
  70.5 5.6 %all-to-all-start.2 = ((f32[8,21,2048]{2,1,0:T(8,128)}), f32[8,21,2048]{2,1,0:T(8,128)S(1)}, u32[]{:S(2)}, u32[]{:S(2)}) async-start(f32[8,21,2048]{2,1,0:T(8,128)} %broadcast_in_dim.25), calls=%async_computation.2 | async-start | bytes 3145728 | tf_op jit(solution)/shard_map/all_to_all | solution.py:16
  76.0 0.1 reduce_sum.80
  76.1 19.7 %all-to-all-done.2 = f32[8,21,2048]{2,1,0:T(8,128)S(1)} async-done(((f32[8,21,2048]{2,1,0:T(8,128)}), f32[8,21,2048]{2,1,0:T(8,128)S(1)}, u32[]{:S(2)}, u32[]{:S(2)}) %all-to-all-start.2) | async-done | bytes 1376288 | tf_op jit(solution)/shard_map/all_to_all | solution.py:16
  95.8 0.1 reduce_sum.78
  95.9 5.9 %convolution_bitcast_fusion = f32[32,8,21,1,64]{4,2,0,1,3:T(8,128)S(1)} fusion(bf16[32,64,2048,1]{2,1,0,3:T(8,128)(2,1)} %bitcast.24, f32[8]{0:T(128)S(1)} %reduce_sum.80, f32[8,2048]{1,0:T(8,128)S(1)} %fusion.13, f32[21,2048]{1,0:T(8,128)S(1)} %reduce_sum.78), kind=kOutput, calls=%fused_computation.6 | convolution fusion | flops 1410318336 | bytes 10002464 | tf_op jit(solution)/shard_map/dot_general | solution.py:55
  101.8 1.6 copy.38
  103.4 2.8 %reshape.63 = f32[32,1,10752]{2,1,0:T(1,128)} reshape(f32[32,21,1,8,64]{4,3,2,1,0:T(8,128)S(1)} %bitcast.25) | data formatting | bytes 2752512
  106.2 45.6 %all_to_all.29 = f32[32,1,10752]{2,1,0:T(1,128)S(1)} all-to-all(f32[32,1,10752]{2,1,0:T(1,128)} %reshape.63), channel_id=1, replica_groups=mesh['var'=32,'smp'=8] {'var'}, dimensions={0} | all-to-all | bytes 2752512 | tf_op jit(solution)/shard_map/all_to_all | solution.py:31
  151.7 0.5 broadcast.59
  152.3 5.3 %reduce.4 = f32[32,10752]{1,0:T(8,128)} reduce(f32[32,1,10752]{2,1,0:T(1,128)S(1)} %all_to_all.29, f32[]{:T(128)} %broadcast.59), dimensions={1}, to_apply=%all_to_all.22.reduce_sub_computation | reduce | bytes 2752516 | tf_op jit(solution)/shard_map/all_to_all | solution.py:31
  157.5 1.9 %reshape.64 = f32[32,21,1,8,64]{4,3,2,1,0:T(8,128)S(1)} reshape(f32[32,10752]{1,0:T(8,128)} %reduce.4) | data formatting | bytes 2752512
  159.4 0.2 bitcast_reduce_fusion
  159.6 0.7 copy.26
  (6 shorter events, 0.1 us)
Async XLA Ops:
  12.3 26.7 %copy-start.2 = (bf16[2048]{0:T(1024)(128)(2,1)S(1)}, bf16[2048]{0:T(1024)(128)(2,1)}, u32[]{:S(2)}) copy-start(bf16[2048]{0:T(1024)(128)(2,1)} %param.7) | copy-start | bytes 12292
  12.3 26.7 %copy-start.1 = (s32[2048]{0:T(1024)S(1)}, s32[2048]{0:T(1024)}, u32[]{:S(2)}) copy-start(s32[2048]{0:T(1024)} %param.5) | copy-start | bytes 24580
  33.7 9.6 %all-to-all-start.1 = ((f32[8,1,2048]{2,1,0:T(1,128)}), f32[8,1,2048]{2,1,0:T(1,128)S(1)}, u32[]{:S(2)}, u32[]{:S(2)}) async-start(f32[8,1,2048]{2,1,0:T(1,128)} %broadcast_in_dim.24), calls=%async_computation.1 | async-start | bytes 131072 | tf_op jit(solution)/shard_map/all_to_all | solution.py:16
  43.9 25.1 %all-to-all-start.3 = ((f32[32,1,8]{2,1,0:T(1,128)}), f32[32,1,8]{2,1,0:T(1,128)S(1)}, u32[]{:S(2)}, u32[]{:S(2)}) async-start(f32[32,1,8]{2,1,0:T(1,128)} %broadcast_in_dim.26), calls=%async_computation.3 | async-start | bytes 32768 | tf_op jit(solution)/shard_map/all_to_all | solution.py:16
  54.6 9.9 %copy-start = (bf16[20,2048]{1,0:T(8,128)(2,1)S(1)}, bf16[20,2048]{1,0:T(8,128)(2,1)}, u32[]{:S(2)}) copy-start(bf16[20,2048]{1,0:T(8,128)(2,1)} %param.6) | copy-start | bytes 245764
  70.5 25.3 %all-to-all-start.2 = ((f32[8,21,2048]{2,1,0:T(8,128)}), f32[8,21,2048]{2,1,0:T(8,128)S(1)}, u32[]{:S(2)}, u32[]{:S(2)}) async-start(f32[8,21,2048]{2,1,0:T(8,128)} %broadcast_in_dim.25), calls=%async_computation.2 | async-start | bytes 3145728 | tf_op jit(solution)/shard_map/all_to_all | solution.py:16
where the time goes:
time: 163 us; the launch traced here: 160 us
  blocking collectives  55.8 us (34%)
  other arithmetic  26.1 us (16%)
  waiting for transfers between devices  23.8 us (15%)
  local copies, waits for them, and re-layouts  22.6 us (14%)
  starting transfers between devices  21.5 us (13%)
  matrix products  10.5 us (6%)
    all_to_all x1, blocking collectives, sent_and_summed(): lax.all_to_all(tiles, axis, split_axis=0, concat_axis=0, tiled=True)  45.6 us
    all_to_all x3, waiting for transfers between devices, sent_to_all(): return lax.all_to_all(copies, axis, split_axis=0, concat_axis=0, tiled=True)  23.8 us
    all_to_all x3, starting transfers between devices, sent_to_all(): return lax.all_to_all(copies, axis, split_axis=0, concat_axis=0, tiled=True)  21.5 us
    unnamed x10, local copies, waits for them, and re-layouts  17 us
    all_to_all x1, blocking collectives, sent_to_all(): return lax.all_to_all(copies, axis, split_axis=0, concat_axis=0, tiled=True)  10.2 us
    convert_element_type x1, other arithmetic, body(): (centered * lax.rsqrt(squares / total + EPS)[:, None]).astype(jnp.bfloat16)  9.84 us
    dot_general x1, matrix products, body(): terms = jnp.dot(weights, scaled, preferred_element_type=jnp.float32)  5.91 us
    reduce_sum x1, other arithmetic, body(): squares = over_copies(jnp.sum(centered * centered, axis=1), 'smp')  5.61 us
  transfers between devices with their start and end apart: 3, of which 2 were waited for; matrix products, arithmetic and copies ran while one was open for 9% of the time, Pallas kernels for 0%

commit v1 on v0

v1 whole, which is shorter than its diff:
```python
import jax
import jax.numpy as jnp
from jax import lax
from jax.experimental import pallas as pl
from jax.experimental.pallas import tpu as pltpu
from jax.sharding import PartitionSpec as P

K = 8
NV = 21
EPS = 1e-06
N = 16384

MEAN, SQUARES, VSUM = 21, 22, 23
ROWS = 24
STEP = 256


def shifted(array, axis, perm):
    return lax.ppermute(array, axis, perm)


ZLO_SWAP = [(i, i ^ 4) for i in range(8)]
X_UP = [(i, (i & 4) | ((i + 1) & 3)) for i in range(8)]
X_DOWN = [(i, (i & 4) | ((i - 1) & 3)) for i in range(8)]
CORE_SWAP = [(i, i ^ 1) for i in range(32)]
Y_UP = [(i, (i + 8) % 32) for i in range(32)]
Y_ACROSS = [(i, (i + 16) % 32) for i in range(32)]
Y_DOWN = [(i, (i - 8) % 32) for i in range(32)]
Z_UP = [(i, (i & 25) | ((i + 2) & 6)) for i in range(32)]
Z_ACROSS = [(i, i ^ 4) for i in range(32)]
Z_DOWN = [(i, (i & 25) | ((i - 2) & 6)) for i in range(32)]


def stats_kernel(probes, phenotype, genotype, out, vec, vsum):
    samples = genotype.shape[1]
    step = pl.program_id(0)

    @pl.when(step == 0)
    def _():
        row = lax.broadcasted_iota(jnp.int32, (32, samples), 0)
        low = jnp.concatenate([probes[...].astype(jnp.float32), jnp.zeros((12, samples), jnp.float32)], axis=0)
        low = jnp.where(row == NV - 1, phenotype[...], jnp.where(row == MEAN, 1.0, low))
        full = jnp.concatenate([low, jnp.zeros((96, samples), jnp.float32)], axis=0)
        vec[...] = jnp.transpose(full).astype(jnp.bfloat16)
        vsum[...] = jnp.dot(jnp.ones((8, samples), jnp.bfloat16), vec[...], preferred_element_type=jnp.float32)

    acc = jnp.dot(genotype[...], vec[...], preferred_element_type=jnp.float32)
    squares, bases = [], []
    for r in range(0, STEP, 64):
        base = jnp.broadcast_to(genotype[r : r + 64, 0:128].astype(jnp.float32)[:, 0:1], (64, 128))
        sq = jnp.zeros((64, 128), jnp.float32)
        for c in range(0, samples, 128):
            dev = genotype[r : r + 64, c : c + 128].astype(jnp.float32) - base
            sq = sq + dev * dev
        squares.append(jnp.sum(sq, axis=1, keepdims=True))
        bases.append(base)
    lane = lax.broadcasted_iota(jnp.int32, acc.shape, 1)
    acc = jnp.where(lane == SQUARES, jnp.concatenate(squares, axis=0), acc)
    acc = jnp.where(lane == VSUM, jnp.concatenate(bases, axis=0), acc)
    flat = jnp.transpose(acc)[0:ROWS, :]
    mean = flat[MEAN : MEAN + 1] / samples
    apart = mean - flat[VSUM : VSUM + 1]
    spread = jnp.maximum(flat[SQUARES : SQUARES + 1] - samples * apart * apart, 0.0)
    row = lax.broadcasted_iota(jnp.int32, flat.shape, 0)
    total = jnp.concatenate([vsum[0:1, :]] * (STEP // 128), axis=1)
    flat = jnp.where(row == MEAN, mean, jnp.where(row == SQUARES, spread, flat))
    out[0] = jnp.where(row == VSUM, total, flat)


def local_stats(probes, phenotype, genotype):
    variants, samples = genotype.shape
    half = variants // 2 // STEP
    return pl.pallas_call(
        stats_kernel,
        grid=(variants // STEP,),
        in_specs=[
            pl.BlockSpec((NV - 1, samples), lambda i: (0, 0)),
            pl.BlockSpec((1, samples), lambda i: (0, 0)),
            pl.BlockSpec((STEP, samples), lambda i: (i, 0)),
        ],
        out_specs=pl.BlockSpec((1, ROWS, STEP), lambda i: (i // half, 0, i % half)),
        out_shape=jax.ShapeDtypeStruct((2, ROWS, variants // 2), jnp.float32),
        scratch_shapes=[pltpu.VMEM((samples, 128), jnp.bfloat16), pltpu.VMEM((8, 128), jnp.float32)],
        compiler_params=pltpu.CompilerParams(vmem_limit_bytes=56 * 1024 * 1024),
        name="local_stats",
    )(probes, phenotype, genotype)


def merged(pieces, each):
    total = sum(pieces[1:], pieces[0])
    mean = total[MEAN : MEAN + 1] * (1.0 / len(pieces))
    apart = sum((p[MEAN : MEAN + 1] - mean) ** 2 for p in pieces) * each
    row = lax.broadcasted_iota(jnp.int32, total.shape, 0)
    return jnp.where(row == MEAN, mean, jnp.where(row == SQUARES, total + apart, total))


def over_samples(stats, samples):
    zlo = lax.axis_index("smp") // 4
    mine = lax.dynamic_index_in_dim(stats, zlo, 0, keepdims=False)
    other = lax.dynamic_index_in_dim(stats, 1 - zlo, 0, keepdims=False)
    own = merged([mine, shifted(other, "smp", ZLO_SWAP)], samples)
    below = shifted(own, "smp", X_UP)
    above = shifted(own, "smp", X_DOWN)
    cut = own.shape[1] // 2
    far_low = shifted(below[:, :cut], "smp", X_UP)
    far_high = shifted(above[:, cut:], "smp", X_DOWN)
    far = jnp.concatenate([far_low, far_high], axis=1)
    own = merged([own, below, above, far], 2 * samples)
    back = shifted(own, "smp", ZLO_SWAP)
    return jnp.where(zlo == 0, own, back), jnp.where(zlo == 0, back, own)


PAIRS = NV // 2
PACK = 88


def terms_kernel(place, low, high, labels, genotype, keep, give, weights, shift):
    variants, samples = genotype.shape
    stats = jnp.concatenate([low[...], high[...]], axis=1)
    mean = stats[MEAN : MEAN + 1]
    scale = lax.rsqrt(stats[SQUARES : SQUARES + 1] / N + EPS)
    sub = lax.broadcasted_iota(jnp.int32, (ROWS, 128), 0)
    lane = lax.broadcasted_iota(jnp.int32, (ROWS, 128), 1)
    vsum = jnp.sum(jnp.where(sub == lane, stats[VSUM : VSUM + 1, 0:128], 0.0), axis=1, keepdims=True)
    projected = (stats - vsum * mean) * scale
    weight = projected * scale
    comp = lax.broadcasted_iota(jnp.int32, (K, variants), 0)
    member = comp == labels[...]
    counts = jnp.sum(jnp.where(member, 1.0, 0.0), axis=1, keepdims=True)

    def rows_of(array, j):
        return jnp.where(member, array[j : j + 1], 0.0)

    for pair in range(PAIRS + 1):
        first = rows_of(weight, 2 * pair)
        second = rows_of(weight, 2 * pair + 1) if pair < PAIRS else jnp.zeros_like(first)
        weights[16 * pair : 16 * pair + 16, :] = jnp.concatenate([first, second], axis=0).astype(jnp.bfloat16)
    for r in range(0, 2 * PACK, 16):
        held = weights[r : r + 16, :].astype(jnp.float32)
        shift[r : r + 16, :] = jnp.broadcast_to(jnp.sum(held * mean, axis=1, keepdims=True), (16, 128))
    shift[K * NV :, :] = jnp.broadcast_to(-counts, (K, 128))

    spot = place[0]
    y, z, core = spot // 8, (spot // 2) % 4, spot % 2
    low_lanes = lax.broadcasted_iota(jnp.int32, (PACK, 128), 1) < 64
    for c in range(samples // 256):
        block = jnp.dot(weights[...], genotype[:, 256 * c : 256 * c + 256], preferred_element_type=jnp.float32)
        for h in range(2):
            t = 2 * c + h
            tile = block[:, 128 * h : 128 * h + 128] - shift[...]
            a, b = tile[:PACK], tile[PACK:]
            ra, rb = pltpu.roll(a, 64, 1), pltpu.roll(b, 64, 1)
            zero = jnp.where(low_lanes, a, rb)
            one = jnp.where(low_lanes, ra, b)
            ky, kz = (t // 4 - y + 4) % 4, (t % 4 - z + 4) % 4
            keep[ky, kz] = jnp.where(core == 0, zero, one)
            give[ky, kz] = jnp.where(core == 0, one, zero)


def local_terms(place, low, high, labels, genotype):
    vmem = pl.BlockSpec(memory_space=pltpu.VMEM)
    tiles = jax.ShapeDtypeStruct((4, 4, PACK, 128), jnp.float32)
    variants = genotype.shape[0]
    return pl.pallas_call(
        terms_kernel,
        in_specs=[pl.BlockSpec(memory_space=pltpu.SMEM), vmem, vmem, vmem, vmem],
        out_specs=(vmem, vmem),
        out_shape=(tiles, tiles),
        scratch_shapes=[pltpu.VMEM((2 * PACK, variants), jnp.bfloat16), pltpu.VMEM((2 * PACK, 128), jnp.float32)],
        compiler_params=pltpu.CompilerParams(vmem_limit_bytes=16 * 1024 * 1024),
        name="local_terms",
    )(place, low, high, labels, genotype)


def direct_sum(parts, axis, up, across, down):
    here, above, far, below = parts
    return here + shifted(above, axis, up) + shifted(below, axis, down) + shifted(far, axis, across)


def over_variants(keep, give):
    whole = keep + shifted(give, "var", CORE_SWAP)
    column = direct_sum([whole[k] for k in range(4)], "var", Y_UP, Y_ACROSS, Y_DOWN)
    return direct_sum([column[k] for k in range(4)], "var", Z_UP, Z_ACROSS, Z_DOWN)


def body(genotype, labels, probes, phenotype):
    variants, samples = genotype.shape
    stats = local_stats(probes, phenotype.astype(jnp.float32).reshape(1, samples), genotype)
    low, high = over_samples(stats, samples)
    place = lax.axis_index("var").astype(jnp.int32).reshape(1)
    keep, give = local_terms(place, low, high, labels.reshape(1, variants), genotype)
    packed = over_variants(keep, give)
    rows = jnp.concatenate([packed[:, :64], packed[:, 64:]], axis=0).reshape(NV + 1, K, 64)
    out = rows[:NV] / rows[NV:]
    return jnp.transpose(out, (1, 0, 2)).reshape(K, NV, 1, 64)


def solution(mesh):
    placed = (P("var", "smp"), P("var"), P(None, "smp"), P("smp"))
    return jax.shard_map(
        body, mesh=mesh, in_specs=placed, out_specs=P(None, None, "smp", "var"), check_vma=False
    )
```

time: 163 us -> 71.4 us (0.44); the launches traced: 160 us -> 70.9 us
  blocking collectives: 55.8 us -> 0 us
  other arithmetic: 26.1 us -> 3.54 us
  local copies, waits for them, and re-layouts: 22.6 us -> 5.22 us
  Pallas kernels: 0 us -> 12.1 us
  matrix products: 10.5 us -> 0 us
  waiting for transfers between devices: 23.8 us -> 28 us
    all_to_all x2 -> x0, blocking collectives: 55.8 us -> none  [the longest x1 45.6 us: sent_and_summed(): lax.all_to_all(tiles, axis, split_axis=0, concat_axis=0, tiled=True)]
    ppermute x0 -> x13, waiting for transfers between devices: none -> 28 us  [shifted(): return lax.ppermute(array, axis, perm)]
    all_to_all x3 -> x0, waiting for transfers between devices: 23.8 us -> none  [sent_to_all(): return lax.all_to_all(copies, axis, split_axis=0, concat_axis=0, tiled=True)]
    ppermute x0 -> x13, starting transfers between devices: none -> 22.1 us  [shifted(): return lax.ppermute(array, axis, perm)]
    all_to_all x3 -> x0, starting transfers between devices: 21.5 us -> none  [sent_to_all(): return lax.all_to_all(copies, axis, split_axis=0, concat_axis=0, tiled=True)]
    unnamed x10 -> x5, local copies, waits for them, and re-layouts: 17 us -> 3.38 us
    pallas_call x0 -> x2, Pallas kernels: none -> 12.1 us  [the longest x1 9.8 us: local_stats(): pl.pallas_call(stats_kernel, grid=(variants // STEP,), in_specs=[pl.Block...]
    reduce_sum x8 -> x0, other arithmetic: 10.9 us -> none  [the longest x1 5.61 us: body(): squares = over_copies(jnp.sum(centered * centered, axis=1), 'smp')]
  transfers between devices with their start and end apart: 3 -> 13, of which waited for: 2 -> 11; matrix products, arithmetic and copies ran while one was open for 9% -> 0% of each run, Pallas kernels for 0% -> 0%
where the time goes in v1:
time: 71.4 us; the launch traced here: 70.9 us
  waiting for transfers between devices  28 us (39%)
  starting transfers between devices  22.1 us (31%)
  Pallas kernels  12.1 us (17%)
  local copies, waits for them, and re-layouts  5.22 us (7%)
  other arithmetic  3.54 us (5%)
    ppermute x13, waiting for transfers between devices, shifted(): return lax.ppermute(array, axis, perm)  28 us
    ppermute x13, starting transfers between devices, shifted(): return lax.ppermute(array, axis, perm)  22.1 us
    pallas_call x1, Pallas kernels, local_stats(): pl.pallas_call(stats_kernel, grid=(variants // STEP,), in_specs=[pl.Block...  9.8 us
    unnamed x5, local copies, waits for them, and re-layouts  3.38 us
    pallas_call x1, Pallas kernels, local_terms(): pl.pallas_call(terms_kernel, in_specs=[pl.BlockSpec(memory_space=pltpu.SM...  2.26 us
  transfers between devices with their start and end apart: 13, of which 11 were waited for; matrix products, arithmetic and copies ran while one was open for 0% of the time, Pallas kernels for 0%

profile of v1, /device:TPU:6, one launch (start us, length us, event | category | flops | bytes accessed | tf_op | source)
XLA Modules:
  0.0 70.9 jit_solution(17689209404006747308)
XLA Ops:
  0.0 0.0 copy-start.1
  0.0 1.3 %reshape.24 = f32[2048]{0:T(1024)} convert(bf16[2048]{0:T(1024)(128)(2,1)} %param.7) | non-fusion elementwise | flops 2048 | bytes 12288 | tf_op jit(solution)/shard_map/reshape | solution.py:188
  1.3 9.8 %local_stats.1 = f32[2,24,1024]{2,1,0:T(8,128)} custom-call(bf16[20,2048]{1,0:T(8,128)(2,1)} %probes.1, f32[1,2048]{1,0:T(1,128)} %bitcast.68, bf16[2048,2048]{1,0:T(8,128)(2,1)} %genotype.3), custom_call_target="tpu_custom_call" | custom-call | tf_op jit(solution)/shard_map/local_stats/pallas_call | solution.py:73
  11.1 0.9 %dynamic-slice_bitcast_fusion = f32[24,1024]{1,0:T(8,128)S(1)} fusion(f32[2,24,1024]{2,1,0:T(8,128)} %local_stats.1, s32[]{:T(128)S(6)} %select_n.41), kind=kLoop, calls=%fused_computation.13 | loop fusion | bytes 196612 | tf_op jit(solution)/shard_map/jit(dynamic_index_in_dim)/squeeze | solution.py:100
  12.0 1.9 %collective-permute-start = (f32[24,1024]{1,0:T(8,128)S(1)}, f32[24,1024]{1,0:T(8,128)S(1)}, u32[]{:S(2)}, u32[]{:S(2)}) collective-permute-start(f32[24,1024]{1,0:T(8,128)S(1)} %dynamic-slice_bitcast_fusion), channel_id=1, source_target_pairs={{0,4},{1,5},{2,6},{3,7},{4,0},{5,1},{6,2},{7,3},{8,12},{9,13},{10,... | collective-permute-start | bytes 294920 | tf_op jit(solution)/shard_map/ppermute | solution.py:19
  13.9 2.8 %collective-permute-done = f32[24,1024]{1,0:T(8,128)S(1)} collective-permute-done((f32[24,1024]{1,0:T(8,128)S(1)}, f32[24,1024]{1,0:T(8,128)S(1)}, u32[]{:S(2)}, u32[]{:S(2)}) %collective-permute-start) | collective-permute-done | bytes 98336 | tf_op jit(solution)/shard_map/ppermute | solution.py:19
  16.7 0.9 %bitcast_add_fusion = f32[24,1024]{1,0:T(8,128)S(1)} fusion(f32[24,1024]{1,0:T(8,128)S(1)} %collective-permute-done, f32[2,24,1024]{2,1,0:T(8,128)} %local_stats.1, s32[]{:T(128)S(6)} %select_n.40), kind=kLoop, calls=%fused_computation.11 | loop fusion | flops 24576 | bytes 294916 | tf_op jit(solution)/shard_map/add | solution.py:90
  17.6 0.8 %slice_multiply_fusion.1 = (f32[1,1024]{1,0:T(1,128)S(1)}, f32[1,1024]{1,0:T(1,128)S(1)}) fusion(f32[24,1024]{1,0:T(8,128)S(1)} %bitcast_add_fusion, f32[24,1024]{1,0:T(8,128)S(1)} %collective-permute-done, f32[2,24,1024]{2,1,0:T(8,128)} %local_stats.1, s32[]{:T(128)S(6)} %select_n.40, s32[]{:T(128)S(6)} %add.97), kind=kLoop, calls=%fused_computation.47 | loop fusion | flops 7168 | bytes 20488 | tf_op jit(solution)/shard_map/mul | solution.py:91
  18.4 0.1 fusion.3
  18.5 2.2 %collective-permute-start.1 = (f32[24,1024]{1,0:T(8,128)S(1)}, f32[24,1024]{1,0:T(8,128)S(1)}, u32[]{:S(2)}, u32[]{:S(2)}) collective-permute-start(f32[24,1024]{1,0:T(8,128)S(1)} %fusion.3), channel_id=1, source_target_pairs={{0,1},{1,2},{2,3},{3,0},{4,5},{5,6},{6,7},{7,4},{8,9},{9,10},{10,1... | collective-permute-start | bytes 294920 | tf_op jit(solution)/shard_map/ppermute | solution.py:19
  20.7 0.0 collective-permute-start.2
  20.7 2.5 %collective-permute-done.1 = f32[24,1024]{1,0:T(8,128)S(1)} collective-permute-done((f32[24,1024]{1,0:T(8,128)S(1)}, f32[24,1024]{1,0:T(8,128)S(1)}, u32[]{:S(2)}, u32[]{:S(2)}) %collective-permute-start.1) | collective-permute-done | bytes 98336 | tf_op jit(solution)/shard_map/ppermute | solution.py:19
  23.2 3.3 %collective-permute-start.3 = (f32[24,512]{1,0:T(8,128)S(1)}, f32[24,512]{1,0:T(8,128)S(1)}, u32[]{:S(2)}, u32[]{:S(2)}) collective-permute-start(f32[24,512]{1,0:T(8,128)S(1)} %slice.101), channel_id=1, source_target_pairs={{0,1},{1,2},{2,3},{3,0},{4,5},{5,6},{6,7},{7,4},{8,9},{9,10},{10,1... | collective-permute-start | bytes 147464 | tf_op jit(solution)/shard_map/ppermute | solution.py:19
  26.5 0.2 collective-permute-done.2
  26.7 0.0 collective-permute-start.4
  26.7 1.6 %collective-permute-done.3 = f32[24,512]{1,0:T(8,128)S(1)} collective-permute-done((f32[24,512]{1,0:T(8,128)S(1)}, f32[24,512]{1,0:T(8,128)S(1)}, u32[]{:S(2)}, u32[]{:S(2)}) %collective-permute-start.3) | collective-permute-done | bytes 49184 | tf_op jit(solution)/shard_map/ppermute | solution.py:19
  28.3 3.7 %collective-permute-done.4 = f32[24,512]{1,0:T(8,128)S(1)} collective-permute-done((f32[24,512]{1,0:T(8,128)S(1)}, f32[24,512]{1,0:T(8,128)S(1)}, u32[]{:S(2)}, u32[]{:S(2)}) %collective-permute-start.4) | collective-permute-done | bytes 49184 | tf_op jit(solution)/shard_map/ppermute | solution.py:19
  32.0 0.1 add_add_fusion
  32.1 0.1 fusion.4
  32.2 0.2 collective-permute-start.5
  32.4 4.5 %collective-permute-done.5 = f32[24,1024]{1,0:T(8,128)S(1)} collective-permute-done((f32[24,1024]{1,0:T(8,128)S(1)}, f32[24,1024]{1,0:T(8,128)S(1)}, u32[]{:S(2)}, u32[]{:S(2)}) %collective-permute-start.5) | collective-permute-done | bytes 98336 | tf_op jit(solution)/shard_map/ppermute | solution.py:19
  36.9 0.1 broadcast_select_fusion
  37.0 0.0 copy-done.1
  37.0 0.0 copy-start
  37.0 3.4 %copy-done = bf16[2048,2048]{1,0:T(8,128)(2,1)S(1)} copy-done((bf16[2048,2048]{1,0:T(8,128)(2,1)S(1)}, bf16[2048,2048]{1,0:T(8,128)(2,1)}, u32[]{:S(2)}) %copy-start) | copy-done | bytes 8388632
  40.4 2.3 %local_terms.1 = (f32[4,4,88,128]{3,2,1,0:T(8,128)S(1)}, f32[4,4,88,128]{3,2,1,0:T(8,128)S(1)}) custom-call(s32[1]{0:T(128)} %bitcast.place, f32[24,1024]{1,0:T(8,128)S(1)} %get-tuple-element.13.low, f32[24,1024]{1,0:T(8,128)S(1)} %get-tuple-element.12.high, s32[1,2048]{1,0:T(1,128)S(1)} %bitcast.59, bf16[2048,2048]{1,0:T(8,128)(2,1)S(1)} %copy-done), custom_call_target="tpu_custom_call" | custom-call | tf_op jit(solution)/shard_map/local_terms/pallas_call | solution.py:164
  42.7 0.1 collective-permute-start.6
  42.8 2.2 %collective-permute-done.6 = f32[4,4,88,128]{3,2,1,0:T(8,128)S(1)} collective-permute-done((f32[4,4,88,128]{3,2,1,0:T(8,128)S(1)}, f32[4,4,88,128]{3,2,1,0:T(8,128)S(1)}, u32[]{:S(2)}, u32[]{:S(2)}) %collective-permute-start.6) | collective-permute-done | bytes 720928 | tf_op jit(solution)/shard_map/ppermute | solution.py:19
  45.0 0.1 add.90
  45.1 0.1 collective-permute-start.7
  45.2 2.7 %collective-permute-start.9 = (f32[4,88,128]{2,1,0:T(8,128)S(1)}, f32[4,88,128]{2,1,0:T(8,128)S(1)}, u32[]{:S(2)}, u32[]{:S(2)}) collective-permute-start(f32[4,88,128]{2,1,0:T(8,128)S(1)} %get-tuple-element.10), channel_id=1, source_target_pairs={{0,128},{8,136},{16,144},{24,152},{32,160},{40,168},{48,176},{56,1... | collective-permute-start | bytes 540680 | tf_op jit(solution)/shard_map/ppermute | solution.py:19
  47.9 1.3 %collective-permute-start.8 = (f32[4,88,128]{2,1,0:T(8,128)S(1)}, f32[4,88,128]{2,1,0:T(8,128)S(1)}, u32[]{:S(2)}, u32[]{:S(2)}) collective-permute-start(f32[4,88,128]{2,1,0:T(8,128)S(1)} %get-tuple-element.11), channel_id=1, source_target_pairs={{0,192},{8,200},{16,208},{24,216},{32,224},{40,232},{48,240},{56,2... | collective-permute-start | bytes 540680 | tf_op jit(solution)/shard_map/ppermute | solution.py:19
  49.3 7.6 %collective-permute-done.7 = f32[4,88,128]{2,1,0:T(8,128)S(1)} collective-permute-done((f32[4,88,128]{2,1,0:T(8,128)S(1)}, f32[4,88,128]{2,1,0:T(8,128)S(1)}, u32[]{:S(2)}, u32[]{:S(2)}) %collective-permute-start.7) | collective-permute-done | bytes 180256 | tf_op jit(solution)/shard_map/ppermute | solution.py:19
  56.8 0.0 collective-permute-done.9
  56.8 0.6 collective-permute-done.8
  57.5 2.2 %collective-permute-start.10 = (f32[88,128]{1,0:T(8,128)S(1)}, f32[88,128]{1,0:T(8,128)S(1)}, u32[]{:S(2)}, u32[]{:S(2)}) collective-permute-start(f32[88,128]{1,0:T(8,128)S(1)} %get-tuple-element.14), channel_id=1, source_target_pairs={{0,16},{8,24},{16,32},{24,40},{32,48},{40,56},{48,0},{56,8},{64,80... | collective-permute-start | bytes 135176 | tf_op jit(solution)/shard_map/ppermute | solution.py:19
  59.8 5.3 %collective-permute-start.12 = (f32[88,128]{1,0:T(8,128)S(1)}, f32[88,128]{1,0:T(8,128)S(1)}, u32[]{:S(2)}, u32[]{:S(2)}) collective-permute-start(f32[88,128]{1,0:T(8,128)S(1)} %get-tuple-element.15), channel_id=1, source_target_pairs={{0,32},{8,40},{16,48},{24,56},{32,0},{40,8},{48,16},{56,24},{64,96... | collective-permute-start | bytes 135176 | tf_op jit(solution)/shard_map/ppermute | solution.py:19
  65.1 2.7 %collective-permute-start.11 = (f32[88,128]{1,0:T(8,128)S(1)}, f32[88,128]{1,0:T(8,128)S(1)}, u32[]{:S(2)}, u32[]{:S(2)}) collective-permute-start(f32[88,128]{1,0:T(8,128)S(1)} %get-tuple-element.16), channel_id=1, source_target_pairs={{0,48},{8,56},{16,0},{24,8},{32,16},{40,24},{48,32},{56,40},{64,11... | collective-permute-start | bytes 135176 | tf_op jit(solution)/shard_map/ppermute | solution.py:19
  67.7 0.0 collective-permute-done.10
  67.7 0.4 collective-permute-done.12
  68.1 1.9 %collective-permute-done.11 = f32[88,128]{1,0:T(8,128)S(1)} collective-permute-done((f32[88,128]{1,0:T(8,128)S(1)}, f32[88,128]{1,0:T(8,128)S(1)}, u32[]{:S(2)}, u32[]{:S(2)}) %collective-permute-start.11) | collective-permute-done | bytes 45088 | tf_op jit(solution)/shard_map/ppermute | solution.py:19
  70.0 0.1 slice.118
  70.1 0.1 fusion.24
  70.2 0.7 %copy.6 = f32[8,21,1,64]{3,2,1,0:T(1,128)} copy(f32[8,21,1,64]{3,0,2,1:T(8,128)S(1)} %fusion.7) | data formatting | bytes 86016 | tf_op jit(solution)/shard_map/reshape | solution.py:195
  (11 shorter events, 0.2 us)
Async XLA Ops:
  0.0 37.0 %copy-start.1 = (s32[2048]{0:T(1024)S(1)}, s32[2048]{0:T(1024)}, u32[]{:S(2)}) copy-start(s32[2048]{0:T(1024)} %param.5) | copy-start | bytes 24580
  12.0 4.7 %collective-permute-start = (f32[24,1024]{1,0:T(8,128)S(1)}, f32[24,1024]{1,0:T(8,128)S(1)}, u32[]{:S(2)}, u32[]{:S(2)}) collective-permute-start(f32[24,1024]{1,0:T(8,128)S(1)} %dynamic-slice_bitcast_fusion), channel_id=1, source_target_pairs={{0,4},{1,5},{2,6},{3,7},{4,0},{5,1},{6,2},{7,3},{8,12},{9,13},{10,... | collective-permute-start | bytes 294920 | tf_op jit(solution)/shard_map/ppermute | solution.py:19
  18.5 4.7 %collective-permute-start.1 = (f32[24,1024]{1,0:T(8,128)S(1)}, f32[24,1024]{1,0:T(8,128)S(1)}, u32[]{:S(2)}, u32[]{:S(2)}) collective-permute-start(f32[24,1024]{1,0:T(8,128)S(1)} %fusion.3), channel_id=1, source_target_pairs={{0,1},{1,2},{2,3},{3,0},{4,5},{5,6},{6,7},{7,4},{8,9},{9,10},{10,1... | collective-permute-start | bytes 294920 | tf_op jit(solution)/shard_map/ppermute | solution.py:19
  20.7 6.0 %collective-permute-start.2 = (f32[24,1024]{1,0:T(8,128)S(1)}, f32[24,1024]{1,0:T(8,128)S(1)}, u32[]{:S(2)}, u32[]{:S(2)}) collective-permute-start(f32[24,1024]{1,0:T(8,128)S(1)} %fusion.3), channel_id=1, source_target_pairs={{0,3},{1,0},{2,1},{3,2},{4,7},{5,4},{6,5},{7,6},{8,11},{9,8},{10,9... | collective-permute-start | bytes 294920 | tf_op jit(solution)/shard_map/ppermute | solution.py:19
  23.2 5.1 %collective-permute-start.3 = (f32[24,512]{1,0:T(8,128)S(1)}, f32[24,512]{1,0:T(8,128)S(1)}, u32[]{:S(2)}, u32[]{:S(2)}) collective-permute-start(f32[24,512]{1,0:T(8,128)S(1)} %slice.101), channel_id=1, source_target_pairs={{0,1},{1,2},{2,3},{3,0},{4,5},{5,6},{6,7},{7,4},{8,9},{9,10},{10,1... | collective-permute-start | bytes 147464 | tf_op jit(solution)/shard_map/ppermute | solution.py:19
  26.7 5.3 %collective-permute-start.4 = (f32[24,512]{1,0:T(8,128)S(1)}, f32[24,512]{1,0:T(8,128)S(1)}, u32[]{:S(2)}, u32[]{:S(2)}) collective-permute-start(f32[24,512]{1,0:T(8,128)S(1)} %slice.102), channel_id=1, source_target_pairs={{0,3},{1,0},{2,1},{3,2},{4,7},{5,4},{6,5},{7,6},{8,11},{9,8},{10,9... | collective-permute-start | bytes 147464 | tf_op jit(solution)/shard_map/ppermute | solution.py:19
  32.2 4.7 %collective-permute-start.5 = (f32[24,1024]{1,0:T(8,128)S(1)}, f32[24,1024]{1,0:T(8,128)S(1)}, u32[]{:S(2)}, u32[]{:S(2)}) collective-permute-start(f32[24,1024]{1,0:T(8,128)S(1)} %fusion.4), channel_id=1, source_target_pairs={{0,4},{1,5},{2,6},{3,7},{4,0},{5,1},{6,2},{7,3},{8,12},{9,13},{10,... | collective-permute-start | bytes 294920 | tf_op jit(solution)/shard_map/ppermute | solution.py:19
  37.0 3.4 %copy-start = (bf16[2048,2048]{1,0:T(8,128)(2,1)S(1)}, bf16[2048,2048]{1,0:T(8,128)(2,1)}, u32[]{:S(2)}) copy-start(bf16[2048,2048]{1,0:T(8,128)(2,1)} %genotype.3) | copy-start | bytes 25165828
  42.7 2.3 %collective-permute-start.6 = (f32[4,4,88,128]{3,2,1,0:T(8,128)S(1)}, f32[4,4,88,128]{3,2,1,0:T(8,128)S(1)}, u32[]{:S(2)}, u32[]{:S(2)}) collective-permute-start(f32[4,4,88,128]{3,2,1,0:T(8,128)S(1)} %get-tuple-element.8), channel_id=1, source_target_pairs={{0,8},{8,0},{16,24},{24,16},{32,40},{40,32},{48,56},{56,48},{64,72... | collective-permute-start | bytes 2162696 | tf_op jit(solution)/shard_map/ppermute | solution.py:19
  45.1 11.7 %collective-permute-start.7 = (f32[4,88,128]{2,1,0:T(8,128)S(1)}, f32[4,88,128]{2,1,0:T(8,128)S(1)}, u32[]{:S(2)}, u32[]{:S(2)}) collective-permute-start(f32[4,88,128]{2,1,0:T(8,128)S(1)} %get-tuple-element.9), channel_id=1, source_target_pairs={{0,64},{8,72},{16,80},{24,88},{32,96},{40,104},{48,112},{56,120},{... | collective-permute-start | bytes 540680 | tf_op jit(solution)/shard_map/ppermute | solution.py:19
  45.2 11.7 %collective-permute-start.9 = (f32[4,88,128]{2,1,0:T(8,128)S(1)}, f32[4,88,128]{2,1,0:T(8,128)S(1)}, u32[]{:S(2)}, u32[]{:S(2)}) collective-permute-start(f32[4,88,128]{2,1,0:T(8,128)S(1)} %get-tuple-element.10), channel_id=1, source_target_pairs={{0,128},{8,136},{16,144},{24,152},{32,160},{40,168},{48,176},{56,1... | collective-permute-start | bytes 540680 | tf_op jit(solution)/shard_map/ppermute | solution.py:19
  47.9 9.5 %collective-permute-start.8 = (f32[4,88,128]{2,1,0:T(8,128)S(1)}, f32[4,88,128]{2,1,0:T(8,128)S(1)}, u32[]{:S(2)}, u32[]{:S(2)}) collective-permute-start(f32[4,88,128]{2,1,0:T(8,128)S(1)} %get-tuple-element.11), channel_id=1, source_target_pairs={{0,192},{8,200},{16,208},{24,216},{32,224},{40,232},{48,240},{56,2... | collective-permute-start | bytes 540680 | tf_op jit(solution)/shard_map/ppermute | solution.py:19
  57.5 10.2 %collective-permute-start.10 = (f32[88,128]{1,0:T(8,128)S(1)}, f32[88,128]{1,0:T(8,128)S(1)}, u32[]{:S(2)}, u32[]{:S(2)}) collective-permute-start(f32[88,128]{1,0:T(8,128)S(1)} %get-tuple-element.14), channel_id=1, source_target_pairs={{0,16},{8,24},{16,32},{24,40},{32,48},{40,56},{48,0},{56,8},{64,80... | collective-permute-start | bytes 135176 | tf_op jit(solution)/shard_map/ppermute | solution.py:19
  59.8 8.4 %collective-permute-start.12 = (f32[88,128]{1,0:T(8,128)S(1)}, f32[88,128]{1,0:T(8,128)S(1)}, u32[]{:S(2)}, u32[]{:S(2)}) collective-permute-start(f32[88,128]{1,0:T(8,128)S(1)} %get-tuple-element.15), channel_id=1, source_target_pairs={{0,32},{8,40},{16,48},{24,56},{32,0},{40,8},{48,16},{56,24},{64,96... | collective-permute-start | bytes 135176 | tf_op jit(solution)/shard_map/ppermute | solution.py:19
  65.1 5.0 %collective-permute-start.11 = (f32[88,128]{1,0:T(8,128)S(1)}, f32[88,128]{1,0:T(8,128)S(1)}, u32[]{:S(2)}, u32[]{:S(2)}) collective-permute-start(f32[88,128]{1,0:T(8,128)S(1)} %get-tuple-element.16), channel_id=1, source_target_pairs={{0,48},{8,56},{16,0},{24,8},{32,16},{40,24},{48,32},{56,40},{64,11... | collective-permute-start | bytes 135176 | tf_op jit(solution)/shard_map/ppermute | solution.py:19

commit v2 on v1

v2 whole, which is shorter than its diff:
```python
import jax
import jax.numpy as jnp
from jax import lax
from jax.experimental import pallas as pl
from jax.experimental.pallas import tpu as pltpu
from jax.sharding import PartitionSpec as P

K = 8
NV = 21
EPS = 1e-06
N = 16384

MEAN, SQUARES, VSUM = 21, 22, 23
ROWS = 24
STEP = 256


def shifted(array, axis, perm):
    return lax.ppermute(array, axis, perm)


ZLO_SWAP = [(i, i ^ 4) for i in range(8)]
X_UP = [(i, (i & 4) | ((i + 1) & 3)) for i in range(8)]
X_DOWN = [(i, (i & 4) | ((i - 1) & 3)) for i in range(8)]
CORE_SWAP = [(i, i ^ 1) for i in range(32)]
Y_UP = [(i, (i + 8) % 32) for i in range(32)]
Y_ACROSS = [(i, (i + 16) % 32) for i in range(32)]
Y_DOWN = [(i, (i - 8) % 32) for i in range(32)]
Z_UP = [(i, (i & 25) | ((i + 2) & 6)) for i in range(32)]
Z_ACROSS = [(i, i ^ 4) for i in range(32)]
Z_DOWN = [(i, (i & 25) | ((i - 2) & 6)) for i in range(32)]


def stats_kernel(place, probes, phenotype, genotype, held, mine, other, vec, vsum, arrived):
    variants, samples = genotype.shape
    steps = variants // STEP
    zlo = (place[0] // 4) % 2

    def copy(i):
        rows = pl.ds(pl.multiple_of(i * STEP, STEP), STEP)
        return pltpu.make_async_copy(genotype.at[rows], held.at[rows], arrived.at[i])

    for i in range(steps):
        copy(i).start()
    row = lax.broadcasted_iota(jnp.int32, (32, samples), 0)
    low = jnp.concatenate([probes[...].astype(jnp.float32), jnp.zeros((12, samples), jnp.float32)], axis=0)
    phen = phenotype[...].astype(jnp.float32).reshape(1, samples)
    low = jnp.where(row == NV - 1, phen, jnp.where(row == MEAN, 1.0, low))
    full = jnp.concatenate([low, jnp.zeros((96, samples), jnp.float32)], axis=0)
    vec[...] = jnp.transpose(full).astype(jnp.bfloat16)
    vsum[...] = jnp.dot(jnp.ones((8, samples), jnp.bfloat16), vec[...], preferred_element_type=jnp.float32)

    def step(i, carry):
        copy(i).wait()
        rows = pl.ds(pl.multiple_of(i * STEP, STEP), STEP)
        acc = jnp.dot(held[rows, :], vec[...], preferred_element_type=jnp.float32)
        squares, bases = [], []
        for r in range(0, STEP, 64):
            part = pl.ds(pl.multiple_of(i * STEP + r, 64), 64)
            base = jnp.broadcast_to(held[part, 0:128].astype(jnp.float32)[:, 0:1], (64, 128))
            sq = jnp.zeros((64, 128), jnp.float32)
            for c in range(0, samples, 128):
                dev = held[part, c : c + 128].astype(jnp.float32) - base
                sq = sq + dev * dev
            squares.append(jnp.sum(sq, axis=1, keepdims=True))
            bases.append(base)
        lane = lax.broadcasted_iota(jnp.int32, acc.shape, 1)
        acc = jnp.where(lane == SQUARES, jnp.concatenate(squares, axis=0), acc)
        acc = jnp.where(lane == VSUM, jnp.concatenate(bases, axis=0), acc)
        flat = jnp.transpose(acc)[0:ROWS, :]
        mean = flat[MEAN : MEAN + 1] / samples
        apart = mean - flat[VSUM : VSUM + 1]
        spread = jnp.maximum(flat[SQUARES : SQUARES + 1] - samples * apart * apart, 0.0)
        row = lax.broadcasted_iota(jnp.int32, flat.shape, 0)
        total = jnp.concatenate([vsum[0:1, :]] * (STEP // 128), axis=1)
        flat = jnp.where(row == MEAN, mean, jnp.where(row == SQUARES, spread, flat))
        flat = jnp.where(row == VSUM, total, flat)
        half = steps // 2
        spot = pl.ds(pl.multiple_of((i % half) * STEP, STEP), STEP)
        own = (i // half) == zlo

        @pl.when(own)
        def _():
            mine[:, spot] = flat

        @pl.when(jnp.logical_not(own))
        def _():
            other[:, spot] = flat

        return carry

    lax.fori_loop(0, steps, step, 0)


def local_stats(place, probes, phenotype, genotype):
    variants, samples = genotype.shape
    vmem = pl.BlockSpec(memory_space=pltpu.VMEM)
    block = jax.ShapeDtypeStruct((ROWS, variants // 2), jnp.float32)
    return pl.pallas_call(
        stats_kernel,
        in_specs=[pl.BlockSpec(memory_space=pltpu.SMEM), vmem, vmem, pl.BlockSpec(memory_space=pltpu.HBM)],
        out_specs=(vmem, vmem, vmem),
        out_shape=(jax.ShapeDtypeStruct(genotype.shape, genotype.dtype), block, block),
        scratch_shapes=[
            pltpu.VMEM((samples, 128), jnp.bfloat16),
            pltpu.VMEM((8, 128), jnp.float32),
            pltpu.SemaphoreType.DMA((variants // STEP,)),
        ],
        compiler_params=pltpu.CompilerParams(vmem_limit_bytes=40 * 1024 * 1024),
        name="local_stats",
    )(place, probes, phenotype, genotype)


def merged(pieces, each):
    total = sum(pieces[1:], pieces[0])
    mean = total[MEAN : MEAN + 1] * (1.0 / len(pieces))
    apart = sum((p[MEAN : MEAN + 1] - mean) ** 2 for p in pieces) * each
    row = lax.broadcasted_iota(jnp.int32, total.shape, 0)
    return jnp.where(row == MEAN, mean, jnp.where(row == SQUARES, total + apart, total))


def over_samples(mine, other, samples):
    own = merged([mine, shifted(other, "smp", ZLO_SWAP)], samples)
    below = shifted(own, "smp", X_UP)
    above = shifted(own, "smp", X_DOWN)
    cut = own.shape[1] // 2
    far_low = shifted(below[:, :cut], "smp", X_UP)
    far_high = shifted(above[:, cut:], "smp", X_DOWN)
    far = jnp.concatenate([far_low, far_high], axis=1)
    own = merged([own, below, above, far], 2 * samples)
    return own, shifted(own, "smp", ZLO_SWAP)


PAIRS = NV // 2
PACK = 88


def terms_kernel(place, own, back, labels, genotype, keep, give, weights, shift):
    variants, samples = genotype.shape
    lower = (place[0] // 4) % 2 == 0
    stats = jnp.concatenate(
        [jnp.where(lower, own[...], back[...]), jnp.where(lower, back[...], own[...])], axis=1
    )
    mean = stats[MEAN : MEAN + 1]
    scale = lax.rsqrt(stats[SQUARES : SQUARES + 1] / N + EPS)
    sub = lax.broadcasted_iota(jnp.int32, (ROWS, 128), 0)
    lane = lax.broadcasted_iota(jnp.int32, (ROWS, 128), 1)
    vsum = jnp.sum(jnp.where(sub == lane, stats[VSUM : VSUM + 1, 0:128], 0.0), axis=1, keepdims=True)
    projected = (stats - vsum * mean) * scale
    weight = projected * scale
    comp = lax.broadcasted_iota(jnp.int32, (K, variants), 0)
    member = comp == labels[...]
    counts = jnp.sum(jnp.where(member, 1.0, 0.0), axis=1, keepdims=True)

    def rows_of(array, j):
        return jnp.where(member, array[j : j + 1], 0.0)

    for pair in range(PAIRS + 1):
        first = rows_of(weight, 2 * pair)
        second = rows_of(weight, 2 * pair + 1) if pair < PAIRS else jnp.zeros_like(first)
        weights[16 * pair : 16 * pair + 16, :] = jnp.concatenate([first, second], axis=0).astype(jnp.bfloat16)
    for r in range(0, 2 * PACK, 16):
        held = weights[r : r + 16, :].astype(jnp.float32)
        shift[r : r + 16, :] = jnp.broadcast_to(jnp.sum(held * mean, axis=1, keepdims=True), (16, 128))
    shift[K * NV :, :] = jnp.broadcast_to(-counts, (K, 128))

    spot = place[0] // 8
    y, z, core = spot // 8, (spot // 2) % 4, spot % 2
    low_lanes = lax.broadcasted_iota(jnp.int32, (PACK, 128), 1) < 64
    for c in range(samples // 256):
        block = jnp.dot(weights[...], genotype[:, 256 * c : 256 * c + 256], preferred_element_type=jnp.float32)
        for h in range(2):
            t = 2 * c + h
            tile = block[:, 128 * h : 128 * h + 128] - shift[...]
            a, b = tile[:PACK], tile[PACK:]
            ra, rb = pltpu.roll(a, 64, 1), pltpu.roll(b, 64, 1)
            zero = jnp.where(low_lanes, a, rb)
            one = jnp.where(low_lanes, ra, b)
            ky, kz = (t // 4 - y + 4) % 4, (t % 4 - z + 4) % 4
            keep[ky, kz] = jnp.where(core == 0, zero, one)
            give[ky, kz] = jnp.where(core == 0, one, zero)


def local_terms(place, own, back, labels, genotype):
    vmem = pl.BlockSpec(memory_space=pltpu.VMEM)
    tiles = jax.ShapeDtypeStruct((4, 4, PACK, 128), jnp.float32)
    variants = genotype.shape[0]
    return pl.pallas_call(
        terms_kernel,
        in_specs=[pl.BlockSpec(memory_space=pltpu.SMEM), vmem, vmem, vmem, vmem],
        out_specs=(vmem, vmem),
        out_shape=(tiles, tiles),
        scratch_shapes=[pltpu.VMEM((2 * PACK, variants), jnp.bfloat16), pltpu.VMEM((2 * PACK, 128), jnp.float32)],
        compiler_params=pltpu.CompilerParams(vmem_limit_bytes=16 * 1024 * 1024),
        name="local_terms",
    )(place, own, back, labels, genotype)


def direct_sum(parts, axis, up, across, down):
    here, above, far, below = parts
    return here + shifted(above, axis, up) + shifted(below, axis, down) + shifted(far, axis, across)


def over_variants(keep, give):
    whole = keep + shifted(give, "var", CORE_SWAP)
    column = direct_sum([whole[k] for k in range(4)], "var", Y_UP, Y_ACROSS, Y_DOWN)
    return direct_sum([column[k] for k in range(4)], "var", Z_UP, Z_ACROSS, Z_DOWN)


def body(genotype, labels, probes, phenotype):
    variants, samples = genotype.shape
    place = lax.axis_index(("var", "smp")).astype(jnp.int32).reshape(1)
    held, mine, other = local_stats(place, probes, phenotype, genotype)
    own, back = over_samples(mine, other, samples)
    keep, give = local_terms(place, own, back, labels.reshape(1, variants), held)
    packed = over_variants(keep, give)
    rows = jnp.concatenate([packed[:, :64], packed[:, 64:]], axis=0).reshape(NV + 1, K, 64)
    out = rows[:NV] / rows[NV:]
    return jnp.transpose(out, (1, 0, 2)).reshape(K, NV, 1, 64)


def solution(mesh):
    placed = (P("var", "smp"), P("var"), P(None, "smp"), P("smp"))
    return jax.shard_map(
        body, mesh=mesh, in_specs=placed, out_specs=P(None, None, "smp", "var"), check_vma=False
    )
```

time: 71.4 us -> 62.9 us (0.88)
  other arithmetic: 3.54 us -> 0.51 us
  local copies, waits for them, and re-layouts: 5.22 us -> 2.54 us
  Pallas kernels: 12.1 us -> 9.51 us
    pallas_call x1, Pallas kernels: 9.8 us -> 7.25 us  [local_stats(): pl.pallas_call(stats_kernel, in_specs=[pl.BlockSpec(memory_space=pltpu.SM...]
    unnamed x5 -> x7, local copies, waits for them, and re-layouts: 3.38 us -> 1.6 us
    reshape x1 -> x0, other arithmetic: 1.3 us -> none  [body(): phenotype.astype(jnp.float32).reshape(1, samples)]
    add x2, other arithmetic: 1 us -> 0.1 us  [merged(): total = sum(pieces[1:], pieces[0])]
    squeeze x1 -> x0, local copies, waits for them, and re-layouts: 0.9 us -> none  [over_samples(): other = lax.dynamic_index_in_dim(stats, 1 - zlo, 0, keepdims=False)]
    mul x2, other arithmetic: 0.82 us -> 0.06 us  [merged(): mean = total[MEAN:MEAN + 1] * (1.0 / len(pieces))]
where the time goes in v2:
time: 62.9 us; the launch traced here: 62.8 us
  waiting for transfers between devices  28 us (45%)
  starting transfers between devices  22.1 us (35%)
  Pallas kernels  9.51 us (15%)
  local copies, waits for them, and re-layouts  2.54 us (4%)
    ppermute x13, waiting for transfers between devices, shifted(): return lax.ppermute(array, axis, perm)  28 us
    ppermute x13, starting transfers between devices, shifted(): return lax.ppermute(array, axis, perm)  22.1 us
    pallas_call x1, Pallas kernels, local_stats(): pl.pallas_call(stats_kernel, in_specs=[pl.BlockSpec(memory_space=pltpu.SM...  7.25 us
    pallas_call x1, Pallas kernels, local_terms(): pl.pallas_call(terms_kernel, in_specs=[pl.BlockSpec(memory_space=pltpu.SM...  2.26 us
    unnamed x7, local copies, waits for them, and re-layouts  1.6 us
  transfers between devices with their start and end apart: 13, of which 11 were waited for; matrix products, arithmetic and copies ran while one was open for 0% of the time, Pallas kernels for 0%

profile of v2, /device:TPU:6, one launch (start us, length us, event | category | flops | bytes accessed | tf_op | source)
XLA Modules:
  0.0 62.8 jit_solution(6651830807000593010)
XLA Ops:
  0.0 0.0 copy-start.1
  0.0 0.0 copy-start
  0.0 0.9 %copy-done = bf16[20,2048]{1,0:T(8,128)(2,1)S(1)} copy-done((bf16[20,2048]{1,0:T(8,128)(2,1)S(1)}, bf16[20,2048]{1,0:T(8,128)(2,1)}, u32[]{:S(2)}) %copy-start) | copy-done | bytes 81944
  0.9 0.0 copy-start.2
  0.9 0.7 %copy-done.2 = bf16[2048]{0:T(1024)(128)(2,1)S(1)} copy-done((bf16[2048]{0:T(1024)(128)(2,1)S(1)}, bf16[2048]{0:T(1024)(128)(2,1)}, u32[]{:S(2)}) %copy-start.2) | copy-done | bytes 4120
  1.6 7.3 %local_stats.1 = (bf16[2048,2048]{1,0:T(8,128)(2,1)S(1)}, f32[24,1024]{1,0:T(8,128)S(1)}, f32[24,1024]{1,0:T(8,128)S(1)}) custom-call(s32[1]{0:T(128)} %bitcast.place, bf16[20,2048]{1,0:T(8,128)(2,1)S(1)} %copy-done, bf16[2048]{0:T(1024)(128)(2,1)S(1)} %copy-done.2, bf16[2048,2048]{1,0:T(8,128)(2,1)} %genotype.1), custom_call_target="tpu_custom_call" | custom-call | tf_op jit(solution)/shard_map/local_stats/pallas_call | solution.py:99
  8.9 2.0 %collective-permute-start = (f32[24,1024]{1,0:T(8,128)S(1)}, f32[24,1024]{1,0:T(8,128)S(1)}, u32[]{:S(2)}, u32[]{:S(2)}) collective-permute-start(f32[24,1024]{1,0:T(8,128)S(1)} %get-tuple-element.11), channel_id=1, source_target_pairs={{0,4},{1,5},{2,6},{3,7},{4,0},{5,1},{6,2},{7,3},{8,12},{9,13},{10,... | collective-permute-start | bytes 294920 | tf_op jit(solution)/shard_map/ppermute | solution.py:19
  10.9 2.8 %collective-permute-done = f32[24,1024]{1,0:T(8,128)S(1)} collective-permute-done((f32[24,1024]{1,0:T(8,128)S(1)}, f32[24,1024]{1,0:T(8,128)S(1)}, u32[]{:S(2)}, u32[]{:S(2)}) %collective-permute-start) | collective-permute-done | bytes 98336 | tf_op jit(solution)/shard_map/ppermute | solution.py:19
  13.7 0.1 fusion.3
  13.8 2.2 %collective-permute-start.1 = (f32[24,1024]{1,0:T(8,128)S(1)}, f32[24,1024]{1,0:T(8,128)S(1)}, u32[]{:S(2)}, u32[]{:S(2)}) collective-permute-start(f32[24,1024]{1,0:T(8,128)S(1)} %fusion.3), channel_id=1, source_target_pairs={{0,1},{1,2},{2,3},{3,0},{4,5},{5,6},{6,7},{7,4},{8,9},{9,10},{10,1... | collective-permute-start | bytes 294920 | tf_op jit(solution)/shard_map/ppermute | solution.py:19
  16.0 0.0 collective-permute-start.2
  16.0 2.5 %collective-permute-done.1 = f32[24,1024]{1,0:T(8,128)S(1)} collective-permute-done((f32[24,1024]{1,0:T(8,128)S(1)}, f32[24,1024]{1,0:T(8,128)S(1)}, u32[]{:S(2)}, u32[]{:S(2)}) %collective-permute-start.1) | collective-permute-done | bytes 98336 | tf_op jit(solution)/shard_map/ppermute | solution.py:19
  18.5 3.3 %collective-permute-start.3 = (f32[24,512]{1,0:T(8,128)S(1)}, f32[24,512]{1,0:T(8,128)S(1)}, u32[]{:S(2)}, u32[]{:S(2)}) collective-permute-start(f32[24,512]{1,0:T(8,128)S(1)} %slice.97), channel_id=1, source_target_pairs={{0,1},{1,2},{2,3},{3,0},{4,5},{5,6},{6,7},{7,4},{8,9},{9,10},{10,1... | collective-permute-start | bytes 147464 | tf_op jit(solution)/shard_map/ppermute | solution.py:19
  21.8 0.2 collective-permute-done.2
  22.0 0.0 collective-permute-start.4
  22.0 1.5 %collective-permute-done.3 = f32[24,512]{1,0:T(8,128)S(1)} collective-permute-done((f32[24,512]{1,0:T(8,128)S(1)}, f32[24,512]{1,0:T(8,128)S(1)}, u32[]{:S(2)}, u32[]{:S(2)}) %collective-permute-start.3) | collective-permute-done | bytes 49184 | tf_op jit(solution)/shard_map/ppermute | solution.py:19
  23.6 3.7 %collective-permute-done.4 = f32[24,512]{1,0:T(8,128)S(1)} collective-permute-done((f32[24,512]{1,0:T(8,128)S(1)}, f32[24,512]{1,0:T(8,128)S(1)}, u32[]{:S(2)}, u32[]{:S(2)}) %collective-permute-start.4) | collective-permute-done | bytes 49184 | tf_op jit(solution)/shard_map/ppermute | solution.py:19
  27.3 0.1 add_add_fusion
  27.4 0.1 fusion.4.own
  27.5 0.2 collective-permute-start.5
  27.7 4.5 %collective-permute-done.5.back = f32[24,1024]{1,0:T(8,128)S(1)} collective-permute-done((f32[24,1024]{1,0:T(8,128)S(1)}, f32[24,1024]{1,0:T(8,128)S(1)}, u32[]{:S(2)}, u32[]{:S(2)}) %collective-permute-start.5) | collective-permute-done | bytes 98336 | tf_op jit(solution)/shard_map/ppermute | solution.py:19
  32.2 0.0 copy-done.1
  32.2 2.3 %local_terms.1 = (f32[4,4,88,128]{3,2,1,0:T(8,128)S(1)}, f32[4,4,88,128]{3,2,1,0:T(8,128)S(1)}) custom-call(s32[1]{0:T(128)} %bitcast.place, f32[24,1024]{1,0:T(8,128)S(1)} %fusion.4.own, f32[24,1024]{1,0:T(8,128)S(1)} %collective-permute-done.5.back, s32[1,2048]{1,0:T(1,128)S(1)} %bitcast.44, bf16[2048,2048]{1,0:T(8,128)(2,1)S(1)} %get-tuple-element.12.genotype), custom_call_target="tpu_custom_call" | custom-call | tf_op jit(solution)/shard_map/local_terms/pallas_call | solution.py:188
  34.5 0.1 collective-permute-start.6
  34.6 2.2 %collective-permute-done.6 = f32[4,4,88,128]{3,2,1,0:T(8,128)S(1)} collective-permute-done((f32[4,4,88,128]{3,2,1,0:T(8,128)S(1)}, f32[4,4,88,128]{3,2,1,0:T(8,128)S(1)}, u32[]{:S(2)}, u32[]{:S(2)}) %collective-permute-start.6) | collective-permute-done | bytes 720928 | tf_op jit(solution)/shard_map/ppermute | solution.py:19
  36.8 0.1 add.83
  36.9 0.1 collective-permute-start.7
  37.0 2.7 %collective-permute-start.9 = (f32[4,88,128]{2,1,0:T(8,128)S(1)}, f32[4,88,128]{2,1,0:T(8,128)S(1)}, u32[]{:S(2)}, u32[]{:S(2)}) collective-permute-start(f32[4,88,128]{2,1,0:T(8,128)S(1)} %get-tuple-element.16), channel_id=1, source_target_pairs={{0,128},{8,136},{16,144},{24,152},{32,160},{40,168},{48,176},{56,1... | collective-permute-start | bytes 540680 | tf_op jit(solution)/shard_map/ppermute | solution.py:19
  39.7 1.3 %collective-permute-start.8 = (f32[4,88,128]{2,1,0:T(8,128)S(1)}, f32[4,88,128]{2,1,0:T(8,128)S(1)}, u32[]{:S(2)}, u32[]{:S(2)}) collective-permute-start(f32[4,88,128]{2,1,0:T(8,128)S(1)} %get-tuple-element.17), channel_id=1, source_target_pairs={{0,192},{8,200},{16,208},{24,216},{32,224},{40,232},{48,240},{56,2... | collective-permute-start | bytes 540680 | tf_op jit(solution)/shard_map/ppermute | solution.py:19
  41.1 7.6 %collective-permute-done.7 = f32[4,88,128]{2,1,0:T(8,128)S(1)} collective-permute-done((f32[4,88,128]{2,1,0:T(8,128)S(1)}, f32[4,88,128]{2,1,0:T(8,128)S(1)}, u32[]{:S(2)}, u32[]{:S(2)}) %collective-permute-start.7) | collective-permute-done | bytes 180256 | tf_op jit(solution)/shard_map/ppermute | solution.py:19
  48.7 0.0 collective-permute-done.9
  48.7 0.6 collective-permute-done.8
  49.4 2.2 %collective-permute-start.10 = (f32[88,128]{1,0:T(8,128)S(1)}, f32[88,128]{1,0:T(8,128)S(1)}, u32[]{:S(2)}, u32[]{:S(2)}) collective-permute-start(f32[88,128]{1,0:T(8,128)S(1)} %get-tuple-element.18), channel_id=1, source_target_pairs={{0,16},{8,24},{16,32},{24,40},{32,48},{40,56},{48,0},{56,8},{64,80... | collective-permute-start | bytes 135176 | tf_op jit(solution)/shard_map/ppermute | solution.py:19
  51.6 5.3 %collective-permute-start.12 = (f32[88,128]{1,0:T(8,128)S(1)}, f32[88,128]{1,0:T(8,128)S(1)}, u32[]{:S(2)}, u32[]{:S(2)}) collective-permute-start(f32[88,128]{1,0:T(8,128)S(1)} %get-tuple-element.19), channel_id=1, source_target_pairs={{0,32},{8,40},{16,48},{24,56},{32,0},{40,8},{48,16},{56,24},{64,96... | collective-permute-start | bytes 135176 | tf_op jit(solution)/shard_map/ppermute | solution.py:19
  56.9 2.7 %collective-permute-start.11 = (f32[88,128]{1,0:T(8,128)S(1)}, f32[88,128]{1,0:T(8,128)S(1)}, u32[]{:S(2)}, u32[]{:S(2)}) collective-permute-start(f32[88,128]{1,0:T(8,128)S(1)} %get-tuple-element.20), channel_id=1, source_target_pairs={{0,48},{8,56},{16,0},{24,8},{32,16},{40,24},{48,32},{56,40},{64,11... | collective-permute-start | bytes 135176 | tf_op jit(solution)/shard_map/ppermute | solution.py:19
  59.5 0.0 collective-permute-done.10
  59.5 0.4 collective-permute-done.12
  59.9 1.9 %collective-permute-done.11 = f32[88,128]{1,0:T(8,128)S(1)} collective-permute-done((f32[88,128]{1,0:T(8,128)S(1)}, f32[88,128]{1,0:T(8,128)S(1)}, u32[]{:S(2)}, u32[]{:S(2)}) %collective-permute-start.11) | collective-permute-done | bytes 45088 | tf_op jit(solution)/shard_map/ppermute | solution.py:19
  61.9 0.1 slice.114
  61.9 0.1 fusion.22
  62.0 0.7 %copy.6 = f32[8,21,1,64]{3,2,1,0:T(1,128)} copy(f32[8,21,1,64]{3,0,2,1:T(8,128)S(1)} %fusion.7) | data formatting | bytes 86016 | tf_op jit(solution)/shard_map/reshape | solution.py:219
  (13 shorter events, 0.2 us)
Async XLA Ops:
  0.0 32.2 %copy-start.1 = (s32[2048]{0:T(1024)S(1)}, s32[2048]{0:T(1024)}, u32[]{:S(2)}) copy-start(s32[2048]{0:T(1024)} %param.5) | copy-start | bytes 24580
  0.0 0.9 %copy-start = (bf16[20,2048]{1,0:T(8,128)(2,1)S(1)}, bf16[20,2048]{1,0:T(8,128)(2,1)}, u32[]{:S(2)}) copy-start(bf16[20,2048]{1,0:T(8,128)(2,1)} %probes.1) | copy-start | bytes 245764
  0.9 0.7 %copy-start.2 = (bf16[2048]{0:T(1024)(128)(2,1)S(1)}, bf16[2048]{0:T(1024)(128)(2,1)}, u32[]{:S(2)}) copy-start(bf16[2048]{0:T(1024)(128)(2,1)} %phenotype.1) | copy-start | bytes 12292
  8.9 4.8 %collective-permute-start = (f32[24,1024]{1,0:T(8,128)S(1)}, f32[24,1024]{1,0:T(8,128)S(1)}, u32[]{:S(2)}, u32[]{:S(2)}) collective-permute-start(f32[24,1024]{1,0:T(8,128)S(1)} %get-tuple-element.11), channel_id=1, source_target_pairs={{0,4},{1,5},{2,6},{3,7},{4,0},{5,1},{6,2},{7,3},{8,12},{9,13},{10,... | collective-permute-start | bytes 294920 | tf_op jit(solution)/shard_map/ppermute | solution.py:19
  13.8 4.7 %collective-permute-start.1 = (f32[24,1024]{1,0:T(8,128)S(1)}, f32[24,1024]{1,0:T(8,128)S(1)}, u32[]{:S(2)}, u32[]{:S(2)}) collective-permute-start(f32[24,1024]{1,0:T(8,128)S(1)} %fusion.3), channel_id=1, source_target_pairs={{0,1},{1,2},{2,3},{3,0},{4,5},{5,6},{6,7},{7,4},{8,9},{9,10},{10,1... | collective-permute-start | bytes 294920 | tf_op jit(solution)/shard_map/ppermute | solution.py:19
  16.0 6.0 %collective-permute-start.2 = (f32[24,1024]{1,0:T(8,128)S(1)}, f32[24,1024]{1,0:T(8,128)S(1)}, u32[]{:S(2)}, u32[]{:S(2)}) collective-permute-start(f32[24,1024]{1,0:T(8,128)S(1)} %fusion.3), channel_id=1, source_target_pairs={{0,3},{1,0},{2,1},{3,2},{4,7},{5,4},{6,5},{7,6},{8,11},{9,8},{10,9... | collective-permute-start | bytes 294920 | tf_op jit(solution)/shard_map/ppermute | solution.py:19
  18.5 5.1 %collective-permute-start.3 = (f32[24,512]{1,0:T(8,128)S(1)}, f32[24,512]{1,0:T(8,128)S(1)}, u32[]{:S(2)}, u32[]{:S(2)}) collective-permute-start(f32[24,512]{1,0:T(8,128)S(1)} %slice.97), channel_id=1, source_target_pairs={{0,1},{1,2},{2,3},{3,0},{4,5},{5,6},{6,7},{7,4},{8,9},{9,10},{10,1... | collective-permute-start | bytes 147464 | tf_op jit(solution)/shard_map/ppermute | solution.py:19
  22.0 5.3 %collective-permute-start.4 = (f32[24,512]{1,0:T(8,128)S(1)}, f32[24,512]{1,0:T(8,128)S(1)}, u32[]{:S(2)}, u32[]{:S(2)}) collective-permute-start(f32[24,512]{1,0:T(8,128)S(1)} %slice.98), channel_id=1, source_target_pairs={{0,3},{1,0},{2,1},{3,2},{4,7},{5,4},{6,5},{7,6},{8,11},{9,8},{10,9... | collective-permute-start | bytes 147464 | tf_op jit(solution)/shard_map/ppermute | solution.py:19
  27.5 4.7 %collective-permute-start.5 = (f32[24,1024]{1,0:T(8,128)S(1)}, f32[24,1024]{1,0:T(8,128)S(1)}, u32[]{:S(2)}, u32[]{:S(2)}) collective-permute-start(f32[24,1024]{1,0:T(8,128)S(1)} %fusion.4.own), channel_id=1, source_target_pairs={{0,4},{1,5},{2,6},{3,7},{4,0},{5,1},{6,2},{7,3},{8,12},{9,13},{10,... | collective-permute-start | bytes 294920 | tf_op jit(solution)/shard_map/ppermute | solution.py:19
  34.5 2.3 %collective-permute-start.6 = (f32[4,4,88,128]{3,2,1,0:T(8,128)S(1)}, f32[4,4,88,128]{3,2,1,0:T(8,128)S(1)}, u32[]{:S(2)}, u32[]{:S(2)}) collective-permute-start(f32[4,4,88,128]{3,2,1,0:T(8,128)S(1)} %get-tuple-element.14), channel_id=1, source_target_pairs={{0,8},{8,0},{16,24},{24,16},{32,40},{40,32},{48,56},{56,48},{64,72... | collective-permute-start | bytes 2162696 | tf_op jit(solution)/shard_map/ppermute | solution.py:19
  36.9 11.7 %collective-permute-start.7 = (f32[4,88,128]{2,1,0:T(8,128)S(1)}, f32[4,88,128]{2,1,0:T(8,128)S(1)}, u32[]{:S(2)}, u32[]{:S(2)}) collective-permute-start(f32[4,88,128]{2,1,0:T(8,128)S(1)} %get-tuple-element.15), channel_id=1, source_target_pairs={{0,64},{8,72},{16,80},{24,88},{32,96},{40,104},{48,112},{56,120},{... | collective-permute-start | bytes 540680 | tf_op jit(solution)/shard_map/ppermute | solution.py:19
  37.0 11.7 %collective-permute-start.9 = (f32[4,88,128]{2,1,0:T(8,128)S(1)}, f32[4,88,128]{2,1,0:T(8,128)S(1)}, u32[]{:S(2)}, u32[]{:S(2)}) collective-permute-start(f32[4,88,128]{2,1,0:T(8,128)S(1)} %get-tuple-element.16), channel_id=1, source_target_pairs={{0,128},{8,136},{16,144},{24,152},{32,160},{40,168},{48,176},{56,1... | collective-permute-start | bytes 540680 | tf_op jit(solution)/shard_map/ppermute | solution.py:19
  39.7 9.5 %collective-permute-start.8 = (f32[4,88,128]{2,1,0:T(8,128)S(1)}, f32[4,88,128]{2,1,0:T(8,128)S(1)}, u32[]{:S(2)}, u32[]{:S(2)}) collective-permute-start(f32[4,88,128]{2,1,0:T(8,128)S(1)} %get-tuple-element.17), channel_id=1, source_target_pairs={{0,192},{8,200},{16,208},{24,216},{32,224},{40,232},{48,240},{56,2... | collective-permute-start | bytes 540680 | tf_op jit(solution)/shard_map/ppermute | solution.py:19
  49.4 10.2 %collective-permute-start.10 = (f32[88,128]{1,0:T(8,128)S(1)}, f32[88,128]{1,0:T(8,128)S(1)}, u32[]{:S(2)}, u32[]{:S(2)}) collective-permute-start(f32[88,128]{1,0:T(8,128)S(1)} %get-tuple-element.18), channel_id=1, source_target_pairs={{0,16},{8,24},{16,32},{24,40},{32,48},{40,56},{48,0},{56,8},{64,80... | collective-permute-start | bytes 135176 | tf_op jit(solution)/shard_map/ppermute | solution.py:19
  51.6 8.3 %collective-permute-start.12 = (f32[88,128]{1,0:T(8,128)S(1)}, f32[88,128]{1,0:T(8,128)S(1)}, u32[]{:S(2)}, u32[]{:S(2)}) collective-permute-start(f32[88,128]{1,0:T(8,128)S(1)} %get-tuple-element.19), channel_id=1, source_target_pairs={{0,32},{8,40},{16,48},{24,56},{32,0},{40,8},{48,16},{56,24},{64,96... | collective-permute-start | bytes 135176 | tf_op jit(solution)/shard_map/ppermute | solution.py:19
  56.9 5.0 %collective-permute-start.11 = (f32[88,128]{1,0:T(8,128)S(1)}, f32[88,128]{1,0:T(8,128)S(1)}, u32[]{:S(2)}, u32[]{:S(2)}) collective-permute-start(f32[88,128]{1,0:T(8,128)S(1)} %get-tuple-element.20), channel_id=1, source_target_pairs={{0,48},{8,56},{16,0},{24,8},{32,16},{40,24},{48,32},{56,40},{64,11... | collective-permute-start | bytes 135176 | tf_op jit(solution)/shard_map/ppermute | solution.py:19

commit v3 on v2

--- a/solution.py
+++ b/solution.py
@@ -20,8 +20,8 @@
 
 
 ZLO_SWAP = [(i, i ^ 4) for i in range(8)]
-X_UP = [(i, (i & 4) | ((i + 1) & 3)) for i in range(8)]
-X_DOWN = [(i, (i & 4) | ((i - 1) & 3)) for i in range(8)]
+X_SWAP = [(i, i ^ 1) for i in range(8)]
+X_TURN = [(i, i ^ 3) for i in range(8)]
 CORE_SWAP = [(i, i ^ 1) for i in range(32)]
 Y_UP = [(i, (i + 8) % 32) for i in range(32)]
 Y_ACROSS = [(i, (i + 16) % 32) for i in range(32)]
@@ -121,21 +121,17 @@
 
 def over_samples(mine, other, samples):
     own = merged([mine, shifted(other, "smp", ZLO_SWAP)], samples)
-    below = shifted(own, "smp", X_UP)
-    above = shifted(own, "smp", X_DOWN)
-    cut = own.shape[1] // 2
-    far_low = shifted(below[:, :cut], "smp", X_UP)
-    far_high = shifted(above[:, cut:], "smp", X_DOWN)
-    far = jnp.concatenate([far_low, far_high], axis=1)
-    own = merged([own, below, above, far], 2 * samples)
+    own = merged([own, shifted(own, "smp", X_SWAP)], 2 * samples)
+    own = merged([own, shifted(own, "smp", X_TURN)], 4 * samples)
     return own, shifted(own, "smp", ZLO_SWAP)
 
 
 PAIRS = NV // 2
 PACK = 88
-
-
-def terms_kernel(place, own, back, labels, genotype, keep, give, weights, shift):
+CUT = 48
+
+
+def terms_kernel(place, own, back, labels, genotype, keep_a, keep_b, give_a, give_b, weights, shift):
     variants, samples = genotype.shape
     lower = (place[0] // 4) % 2 == 0
     stats = jnp.concatenate(
@@ -177,19 +173,22 @@
             zero = jnp.where(low_lanes, a, rb)
             one = jnp.where(low_lanes, ra, b)
             ky, kz = (t // 4 - y + 4) % 4, (t % 4 - z + 4) % 4
-            keep[ky, kz] = jnp.where(core == 0, zero, one)
-            give[ky, kz] = jnp.where(core == 0, one, zero)
+            keep = jnp.where(core == 0, zero, one)
+            give = jnp.where(core == 0, one, zero)
+            keep_a[ky, kz], keep_b[ky, kz] = keep[:CUT], keep[CUT:]
+            give_a[ky, kz], give_b[ky, kz] = give[:CUT], give[CUT:]
 
 
 def local_terms(place, own, back, labels, genotype):
     vmem = pl.BlockSpec(memory_space=pltpu.VMEM)
-    tiles = jax.ShapeDtypeStruct((4, 4, PACK, 128), jnp.float32)
+    upper = jax.ShapeDtypeStruct((4, 4, CUT, 128), jnp.float32)
+    lower = jax.ShapeDtypeStruct((4, 4, PACK - CUT, 128), jnp.float32)
     variants = genotype.shape[0]
     return pl.pallas_call(
         terms_kernel,
         in_specs=[pl.BlockSpec(memory_space=pltpu.SMEM), vmem, vmem, vmem, vmem],
-        out_specs=(vmem, vmem),
-        out_shape=(tiles, tiles),
+        out_specs=(vmem, vmem, vmem, vmem),
+        out_shape=(upper, lower, upper, lower),
         scratch_shapes=[pltpu.VMEM((2 * PACK, variants), jnp.bfloat16), pltpu.VMEM((2 * PACK, 128), jnp.float32)],
         compiler_params=pltpu.CompilerParams(vmem_limit_bytes=16 * 1024 * 1024),
         name="local_terms",
@@ -212,8 +211,8 @@
     place = lax.axis_index(("var", "smp")).astype(jnp.int32).reshape(1)
     held, mine, other = local_stats(place, probes, phenotype, genotype)
     own, back = over_samples(mine, other, samples)
-    keep, give = local_terms(place, own, back, labels.reshape(1, variants), held)
-    packed = over_variants(keep, give)
+    keep_a, keep_b, give_a, give_b = local_terms(place, own, back, labels.reshape(1, variants), held)
+    packed = jnp.concatenate([over_variants(keep_a, give_a), over_variants(keep_b, give_b)], axis=0)
     rows = jnp.concatenate([packed[:, :64], packed[:, 64:]], axis=0).reshape(NV + 1, K, 64)
     out = rows[:NV] / rows[NV:]
     return jnp.transpose(out, (1, 0, 2)).reshape(K, NV, 1, 64)

time: 62.9 us -> 64.8 us (1.030)
  starting transfers between devices: 22.1 us -> 33.5 us
  waiting for transfers between devices: 28 us -> 18.2 us
    ppermute x13 -> x18, starting transfers between devices: 22.1 us -> 33.5 us  [shifted(): return lax.ppermute(array, axis, perm)]
    ppermute x13 -> x18, waiting for transfers between devices: 28 us -> 18.2 us  [shifted(): return lax.ppermute(array, axis, perm)]
    unnamed x7 -> x6, local copies, waits for them, and re-layouts: 1.6 us -> 1.6 us
  transfers between devices with their start and end apart: 13 -> 18, of which waited for: 11 -> 9; matrix products, arithmetic and copies ran while one was open for 0% -> 0% of each run, Pallas kernels for 0% -> 0%
where the time goes in v3:
time: 64.8 us; the launch traced here: 64.6 us
  starting transfers between devices  33.5 us (52%)
  waiting for transfers between devices  18.2 us (28%)
  Pallas kernels  9.51 us (15%)
  local copies, waits for them, and re-layouts  2.45 us (4%)
  other arithmetic  0.75 us (1%)
    ppermute x18, starting transfers between devices, shifted(): return lax.ppermute(array, axis, perm)  33.5 us
    ppermute x18, waiting for transfers between devices, shifted(): return lax.ppermute(array, axis, perm)  18.2 us
    pallas_call x1, Pallas kernels, local_stats(): pl.pallas_call(stats_kernel, in_specs=[pl.BlockSpec(memory_space=pltpu.SM...  7.27 us
    pallas_call x1, Pallas kernels, local_terms(): pl.pallas_call(terms_kernel, in_specs=[pl.BlockSpec(memory_space=pltpu.SM...  2.24 us
    unnamed x6, local copies, waits for them, and re-layouts  1.6 us
  transfers between devices with their start and end apart: 18, of which 9 were waited for; matrix products, arithmetic and copies ran while one was open for 0% of the time, Pallas kernels for 0%

profile of v3, /device:TPU:6, one launch (start us, length us, event | category | flops | bytes accessed | tf_op | source)
XLA Modules:
  0.0 64.6 jit_solution(12288958964550778086)
XLA Ops:
  0.0 0.0 copy-start.1
  0.0 0.0 copy-start
  0.0 0.9 %copy-done = bf16[20,2048]{1,0:T(8,128)(2,1)S(1)} copy-done((bf16[20,2048]{1,0:T(8,128)(2,1)S(1)}, bf16[20,2048]{1,0:T(8,128)(2,1)}, u32[]{:S(2)}) %copy-start) | copy-done | bytes 81944
  0.9 0.0 copy-start.2
  0.9 0.7 %copy-done.2 = bf16[2048]{0:T(1024)(128)(2,1)S(1)} copy-done((bf16[2048]{0:T(1024)(128)(2,1)S(1)}, bf16[2048]{0:T(1024)(128)(2,1)}, u32[]{:S(2)}) %copy-start.2) | copy-done | bytes 4120
  1.6 7.3 %local_stats.1 = (bf16[2048,2048]{1,0:T(8,128)(2,1)S(1)}, f32[24,1024]{1,0:T(8,128)S(1)}, f32[24,1024]{1,0:T(8,128)S(1)}) custom-call(s32[1]{0:T(128)} %bitcast.place, bf16[20,2048]{1,0:T(8,128)(2,1)S(1)} %copy-done, bf16[2048]{0:T(1024)(128)(2,1)S(1)} %copy-done.2, bf16[2048,2048]{1,0:T(8,128)(2,1)} %genotype.1), custom_call_target="tpu_custom_call" | custom-call | tf_op jit(solution)/shard_map/local_stats/pallas_call | solution.py:99
  8.9 2.0 %collective-permute-start = (f32[24,1024]{1,0:T(8,128)S(1)}, f32[24,1024]{1,0:T(8,128)S(1)}, u32[]{:S(2)}, u32[]{:S(2)}) collective-permute-start(f32[24,1024]{1,0:T(8,128)S(1)} %get-tuple-element.13), channel_id=1, source_target_pairs={{0,4},{1,5},{2,6},{3,7},{4,0},{5,1},{6,2},{7,3},{8,12},{9,13},{10,... | collective-permute-start | bytes 294920 | tf_op jit(solution)/shard_map/ppermute | solution.py:19
  10.9 2.8 %collective-permute-done = f32[24,1024]{1,0:T(8,128)S(1)} collective-permute-done((f32[24,1024]{1,0:T(8,128)S(1)}, f32[24,1024]{1,0:T(8,128)S(1)}, u32[]{:S(2)}, u32[]{:S(2)}) %collective-permute-start) | collective-permute-done | bytes 98336 | tf_op jit(solution)/shard_map/ppermute | solution.py:19
  13.7 0.1 fusion
  13.8 0.9 %collective-permute-start.1 = (f32[24,1024]{1,0:T(8,128)S(1)}, f32[24,1024]{1,0:T(8,128)S(1)}, u32[]{:S(2)}, u32[]{:S(2)}) collective-permute-start(f32[24,1024]{1,0:T(8,128)S(1)} %fusion), channel_id=1, source_target_pairs={{0,1},{1,0},{2,3},{3,2},{4,5},{5,4},{6,7},{7,6},{8,9},{9,8},{10,11... | collective-permute-start | bytes 294920 | tf_op jit(solution)/shard_map/ppermute | solution.py:19
  14.7 3.8 %collective-permute-done.1 = f32[24,1024]{1,0:T(8,128)S(1)} collective-permute-done((f32[24,1024]{1,0:T(8,128)S(1)}, f32[24,1024]{1,0:T(8,128)S(1)}, u32[]{:S(2)}, u32[]{:S(2)}) %collective-permute-start.1) | collective-permute-done | bytes 98336 | tf_op jit(solution)/shard_map/ppermute | solution.py:19
  18.5 0.1 fusion.30
  18.6 0.1 fusion.1
  18.7 2.2 %collective-permute-start.2 = (f32[24,1024]{1,0:T(8,128)S(1)}, f32[24,1024]{1,0:T(8,128)S(1)}, u32[]{:S(2)}, u32[]{:S(2)}) collective-permute-start(f32[24,1024]{1,0:T(8,128)S(1)} %fusion.1), channel_id=1, source_target_pairs={{0,3},{1,2},{2,1},{3,0},{4,7},{5,6},{6,5},{7,4},{8,11},{9,10},{10,... | collective-permute-start | bytes 294920 | tf_op jit(solution)/shard_map/ppermute | solution.py:19
  20.9 3.7 %collective-permute-done.2 = f32[24,1024]{1,0:T(8,128)S(1)} collective-permute-done((f32[24,1024]{1,0:T(8,128)S(1)}, f32[24,1024]{1,0:T(8,128)S(1)}, u32[]{:S(2)}, u32[]{:S(2)}) %collective-permute-start.2) | collective-permute-done | bytes 98336 | tf_op jit(solution)/shard_map/ppermute | solution.py:19
  24.6 0.1 fusion.29
  24.7 0.1 fusion.2.own
  24.8 1.9 %collective-permute-start.3 = (f32[24,1024]{1,0:T(8,128)S(1)}, f32[24,1024]{1,0:T(8,128)S(1)}, u32[]{:S(2)}, u32[]{:S(2)}) collective-permute-start(f32[24,1024]{1,0:T(8,128)S(1)} %fusion.2.own), channel_id=1, source_target_pairs={{0,4},{1,5},{2,6},{3,7},{4,0},{5,1},{6,2},{7,3},{8,12},{9,13},{10,... | collective-permute-start | bytes 294920 | tf_op jit(solution)/shard_map/ppermute | solution.py:19
  26.7 2.8 %collective-permute-done.3.back = f32[24,1024]{1,0:T(8,128)S(1)} collective-permute-done((f32[24,1024]{1,0:T(8,128)S(1)}, f32[24,1024]{1,0:T(8,128)S(1)}, u32[]{:S(2)}, u32[]{:S(2)}) %collective-permute-start.3) | collective-permute-done | bytes 98336 | tf_op jit(solution)/shard_map/ppermute | solution.py:19
  29.5 0.0 copy-done.1
  29.5 2.2 %local_terms.1 = (f32[4,4,48,128]{3,2,1,0:T(8,128)S(1)}, f32[4,4,40,128]{3,2,1,0:T(8,128)S(1)}, f32[4,4,48,128]{3,2,1,0:T(8,128)S(1)}, f32[4,4,40,128]{3,2,1,0:T(8,128)S(1)}) custom-call(s32[1]{0:T(128)} %bitcast.place, f32[24,1024]{1,0:T(8,128)S(1)} %fusion.2.own, f32[24,1024]{1,0:T(8,128)S(1)} %collective-permute-done.3.back, s32[1,2048]{1,0:T(1,128)S(1)} %bitcast.74, ...), custom_call_target="tpu_custom_call" | custom-call | tf_op jit(solution)/shard_map/local_terms/pallas_call | solution.py:187
  31.8 0.1 collective-permute-start.11
  31.9 0.5 collective-permute-start.4
  32.4 1.1 %collective-permute-done.11 = f32[4,4,40,128]{3,2,1,0:T(8,128)S(1)} collective-permute-done((f32[4,4,40,128]{3,2,1,0:T(8,128)S(1)}, f32[4,4,40,128]{3,2,1,0:T(8,128)S(1)}, u32[]{:S(2)}, u32[]{:S(2)}) %collective-permute-start.11) | collective-permute-done | bytes 327712 | tf_op jit(solution)/shard_map/ppermute | solution.py:19
  33.6 1.6 %collective-permute-start.12 = (f32[4,40,128]{2,1,0:T(8,128)S(1)}, f32[4,40,128]{2,1,0:T(8,128)S(1)}, u32[]{:S(2)}, u32[]{:S(2)}) collective-permute-start(f32[4,40,128]{2,1,0:T(8,128)S(1)} %get-tuple-element.22), channel_id=1, source_target_pairs={{0,64},{8,72},{16,80},{24,88},{32,96},{40,104},{48,112},{56,120},{... | collective-permute-start | bytes 245768 | tf_op jit(solution)/shard_map/ppermute | solution.py:19
  35.2 2.9 %collective-permute-start.14 = (f32[4,40,128]{2,1,0:T(8,128)S(1)}, f32[4,40,128]{2,1,0:T(8,128)S(1)}, u32[]{:S(2)}, u32[]{:S(2)}) collective-permute-start(f32[4,40,128]{2,1,0:T(8,128)S(1)} %get-tuple-element.23), channel_id=1, source_target_pairs={{0,128},{8,136},{16,144},{24,152},{32,160},{40,168},{48,176},{56,1... | collective-permute-start | bytes 245768 | tf_op jit(solution)/shard_map/ppermute | solution.py:19
  38.1 1.3 %collective-permute-start.13 = (f32[4,40,128]{2,1,0:T(8,128)S(1)}, f32[4,40,128]{2,1,0:T(8,128)S(1)}, u32[]{:S(2)}, u32[]{:S(2)}) collective-permute-start(f32[4,40,128]{2,1,0:T(8,128)S(1)} %get-tuple-element.24), channel_id=1, source_target_pairs={{0,192},{8,200},{16,208},{24,216},{32,224},{40,232},{48,240},{56,2... | collective-permute-start | bytes 245768 | tf_op jit(solution)/shard_map/ppermute | solution.py:19
  39.5 0.0 collective-permute-done.4
  39.5 0.1 add.109
  39.6 0.8 %collective-permute-start.5 = (f32[4,48,128]{2,1,0:T(8,128)S(1)}, f32[4,48,128]{2,1,0:T(8,128)S(1)}, u32[]{:S(2)}, u32[]{:S(2)}) collective-permute-start(f32[4,48,128]{2,1,0:T(8,128)S(1)} %get-tuple-element.19), channel_id=1, source_target_pairs={{0,64},{8,72},{16,80},{24,88},{32,96},{40,104},{48,112},{56,120},{... | collective-permute-start | bytes 294920 | tf_op jit(solution)/shard_map/ppermute | solution.py:19
  40.3 0.8 %collective-permute-start.7 = (f32[4,48,128]{2,1,0:T(8,128)S(1)}, f32[4,48,128]{2,1,0:T(8,128)S(1)}, u32[]{:S(2)}, u32[]{:S(2)}) collective-permute-start(f32[4,48,128]{2,1,0:T(8,128)S(1)} %get-tuple-element.20), channel_id=1, source_target_pairs={{0,128},{8,136},{16,144},{24,152},{32,160},{40,168},{48,176},{56,1... | collective-permute-start | bytes 294920 | tf_op jit(solution)/shard_map/ppermute | solution.py:19
  41.1 0.0 collective-permute-done.12
  41.1 2.0 %collective-permute-start.6 = (f32[4,48,128]{2,1,0:T(8,128)S(1)}, f32[4,48,128]{2,1,0:T(8,128)S(1)}, u32[]{:S(2)}, u32[]{:S(2)}) collective-permute-start(f32[4,48,128]{2,1,0:T(8,128)S(1)} %get-tuple-element.21), channel_id=1, source_target_pairs={{0,192},{8,200},{16,208},{24,216},{32,224},{40,232},{48,240},{56,2... | collective-permute-start | bytes 294920 | tf_op jit(solution)/shard_map/ppermute | solution.py:19
  43.1 0.1 collective-permute-done.14
  43.2 0.0 collective-permute-done.13
  43.2 3.3 %collective-permute-start.15 = (f32[40,128]{1,0:T(8,128)S(1)}, f32[40,128]{1,0:T(8,128)S(1)}, u32[]{:S(2)}, u32[]{:S(2)}) collective-permute-start(f32[40,128]{1,0:T(8,128)S(1)} %get-tuple-element.34), channel_id=1, source_target_pairs={{0,16},{8,24},{16,32},{24,40},{32,48},{40,56},{48,0},{56,8},{64,80... | collective-permute-start | bytes 61448 | tf_op jit(solution)/shard_map/ppermute | solution.py:19
  46.5 5.3 %collective-permute-start.17 = (f32[40,128]{1,0:T(8,128)S(1)}, f32[40,128]{1,0:T(8,128)S(1)}, u32[]{:S(2)}, u32[]{:S(2)}) collective-permute-start(f32[40,128]{1,0:T(8,128)S(1)} %get-tuple-element.35), channel_id=1, source_target_pairs={{0,32},{8,40},{16,48},{24,56},{32,0},{40,8},{48,16},{56,24},{64,96... | collective-permute-start | bytes 61448 | tf_op jit(solution)/shard_map/ppermute | solution.py:19
  51.8 0.0 collective-permute-done.5
  51.9 2.6 %collective-permute-start.16 = (f32[40,128]{1,0:T(8,128)S(1)}, f32[40,128]{1,0:T(8,128)S(1)}, u32[]{:S(2)}, u32[]{:S(2)}) collective-permute-start(f32[40,128]{1,0:T(8,128)S(1)} %get-tuple-element.36), channel_id=1, source_target_pairs={{0,48},{8,56},{16,0},{24,8},{32,16},{40,24},{48,32},{56,40},{64,11... | collective-permute-start | bytes 61448 | tf_op jit(solution)/shard_map/ppermute | solution.py:19
  54.5 0.0 collective-permute-done.7
  54.5 0.0 collective-permute-done.6
  54.5 0.4 collective-permute-start.8
  54.9 2.4 %collective-permute-start.10 = (f32[48,128]{1,0:T(8,128)S(1)}, f32[48,128]{1,0:T(8,128)S(1)}, u32[]{:S(2)}, u32[]{:S(2)}) collective-permute-start(f32[48,128]{1,0:T(8,128)S(1)} %get-tuple-element.26), channel_id=1, source_target_pairs={{0,32},{8,40},{16,48},{24,56},{32,0},{40,8},{48,16},{56,24},{64,96... | collective-permute-start | bytes 73736 | tf_op jit(solution)/shard_map/ppermute | solution.py:19
  57.3 0.0 collective-permute-done.15
  57.3 2.5 %collective-permute-start.9 = (f32[48,128]{1,0:T(8,128)S(1)}, f32[48,128]{1,0:T(8,128)S(1)}, u32[]{:S(2)}, u32[]{:S(2)}) collective-permute-start(f32[48,128]{1,0:T(8,128)S(1)} %get-tuple-element.27), channel_id=1, source_target_pairs={{0,48},{8,56},{16,0},{24,8},{32,16},{40,24},{48,32},{56,40},{64,11... | collective-permute-start | bytes 73736 | tf_op jit(solution)/shard_map/ppermute | solution.py:19
  59.8 0.0 collective-permute-done.17
  59.8 0.0 collective-permute-done.16
  59.8 0.1 slice.150
  59.9 0.7 %collective-permute-done.8 = f32[48,128]{1,0:T(8,128)S(1)} collective-permute-done((f32[48,128]{1,0:T(8,128)S(1)}, f32[48,128]{1,0:T(8,128)S(1)}, u32[]{:S(2)}, u32[]{:S(2)}) %collective-permute-start.8) | collective-permute-done | bytes 24608 | tf_op jit(solution)/shard_map/ppermute | solution.py:19
  60.6 2.2 %collective-permute-done.10 = f32[48,128]{1,0:T(8,128)S(1)} collective-permute-done((f32[48,128]{1,0:T(8,128)S(1)}, f32[48,128]{1,0:T(8,128)S(1)}, u32[]{:S(2)}, u32[]{:S(2)}) %collective-permute-start.10) | collective-permute-done | bytes 24608 | tf_op jit(solution)/shard_map/ppermute | solution.py:19
  62.8 0.9 %collective-permute-done.9 = f32[48,128]{1,0:T(8,128)S(1)} collective-permute-done((f32[48,128]{1,0:T(8,128)S(1)}, f32[48,128]{1,0:T(8,128)S(1)}, u32[]{:S(2)}, u32[]{:S(2)}) %collective-permute-start.9) | collective-permute-done | bytes 24608 | tf_op jit(solution)/shard_map/ppermute | solution.py:19
  63.7 0.1 fusion.8
  63.8 0.7 %copy.6 = f32[8,21,1,64]{3,2,1,0:T(1,128)} copy(f32[8,21,1,64]{3,0,2,1:T(8,128)S(1)} %fusion.8) | data formatting | bytes 86016 | tf_op jit(solution)/shard_map/reshape | solution.py:218
  (15 shorter events, 0.3 us)
Async XLA Ops:
  0.0 29.5 %copy-start.1 = (s32[2048]{0:T(1024)S(1)}, s32[2048]{0:T(1024)}, u32[]{:S(2)}) copy-start(s32[2048]{0:T(1024)} %param.5) | copy-start | bytes 24580
  0.0 0.9 %copy-start = (bf16[20,2048]{1,0:T(8,128)(2,1)S(1)}, bf16[20,2048]{1,0:T(8,128)(2,1)}, u32[]{:S(2)}) copy-start(bf16[20,2048]{1,0:T(8,128)(2,1)} %probes.1) | copy-start | bytes 245764
  0.9 0.7 %copy-start.2 = (bf16[2048]{0:T(1024)(128)(2,1)S(1)}, bf16[2048]{0:T(1024)(128)(2,1)}, u32[]{:S(2)}) copy-start(bf16[2048]{0:T(1024)(128)(2,1)} %phenotype.1) | copy-start | bytes 12292
  8.9 4.8 %collective-permute-start = (f32[24,1024]{1,0:T(8,128)S(1)}, f32[24,1024]{1,0:T(8,128)S(1)}, u32[]{:S(2)}, u32[]{:S(2)}) collective-permute-start(f32[24,1024]{1,0:T(8,128)S(1)} %get-tuple-element.13), channel_id=1, source_target_pairs={{0,4},{1,5},{2,6},{3,7},{4,0},{5,1},{6,2},{7,3},{8,12},{9,13},{10,... | collective-permute-start | bytes 294920 | tf_op jit(solution)/shard_map/ppermute | solution.py:19
  13.8 4.7 %collective-permute-start.1 = (f32[24,1024]{1,0:T(8,128)S(1)}, f32[24,1024]{1,0:T(8,128)S(1)}, u32[]{:S(2)}, u32[]{:S(2)}) collective-permute-start(f32[24,1024]{1,0:T(8,128)S(1)} %fusion), channel_id=1, source_target_pairs={{0,1},{1,0},{2,3},{3,2},{4,5},{5,4},{6,7},{7,6},{8,9},{9,8},{10,11... | collective-permute-start | bytes 294920 | tf_op jit(solution)/shard_map/ppermute | solution.py:19
  18.7 5.9 %collective-permute-start.2 = (f32[24,1024]{1,0:T(8,128)S(1)}, f32[24,1024]{1,0:T(8,128)S(1)}, u32[]{:S(2)}, u32[]{:S(2)}) collective-permute-start(f32[24,1024]{1,0:T(8,128)S(1)} %fusion.1), channel_id=1, source_target_pairs={{0,3},{1,2},{2,1},{3,0},{4,7},{5,6},{6,5},{7,4},{8,11},{9,10},{10,... | collective-permute-start | bytes 294920 | tf_op jit(solution)/shard_map/ppermute | solution.py:19
  24.8 4.7 %collective-permute-start.3 = (f32[24,1024]{1,0:T(8,128)S(1)}, f32[24,1024]{1,0:T(8,128)S(1)}, u32[]{:S(2)}, u32[]{:S(2)}) collective-permute-start(f32[24,1024]{1,0:T(8,128)S(1)} %fusion.2.own), channel_id=1, source_target_pairs={{0,4},{1,5},{2,6},{3,7},{4,0},{5,1},{6,2},{7,3},{8,12},{9,13},{10,... | collective-permute-start | bytes 294920 | tf_op jit(solution)/shard_map/ppermute | solution.py:19
  31.8 1.7 %collective-permute-start.11 = (f32[4,4,40,128]{3,2,1,0:T(8,128)S(1)}, f32[4,4,40,128]{3,2,1,0:T(8,128)S(1)}, u32[]{:S(2)}, u32[]{:S(2)}) collective-permute-start(f32[4,4,40,128]{3,2,1,0:T(8,128)S(1)} %get-tuple-element.18), channel_id=1, source_target_pairs={{0,8},{8,0},{16,24},{24,16},{32,40},{40,32},{48,56},{56,48},{64,72... | collective-permute-start | bytes 983048 | tf_op jit(solution)/shard_map/ppermute | solution.py:19
  31.9 7.6 %collective-permute-start.4 = (f32[4,4,48,128]{3,2,1,0:T(8,128)S(1)}, f32[4,4,48,128]{3,2,1,0:T(8,128)S(1)}, u32[]{:S(2)}, u32[]{:S(2)}) collective-permute-start(f32[4,4,48,128]{3,2,1,0:T(8,128)S(1)} %get-tuple-element.16), channel_id=1, source_target_pairs={{0,8},{8,0},{16,24},{24,16},{32,40},{40,32},{48,56},{56,48},{64,72... | collective-permute-start | bytes 1179656 | tf_op jit(solution)/shard_map/ppermute | solution.py:19
  33.6 7.6 %collective-permute-start.12 = (f32[4,40,128]{2,1,0:T(8,128)S(1)}, f32[4,40,128]{2,1,0:T(8,128)S(1)}, u32[]{:S(2)}, u32[]{:S(2)}) collective-permute-start(f32[4,40,128]{2,1,0:T(8,128)S(1)} %get-tuple-element.22), channel_id=1, source_target_pairs={{0,64},{8,72},{16,80},{24,88},{32,96},{40,104},{48,112},{56,120},{... | collective-permute-start | bytes 245768 | tf_op jit(solution)/shard_map/ppermute | solution.py:19
  35.2 8.0 %collective-permute-start.14 = (f32[4,40,128]{2,1,0:T(8,128)S(1)}, f32[4,40,128]{2,1,0:T(8,128)S(1)}, u32[]{:S(2)}, u32[]{:S(2)}) collective-permute-start(f32[4,40,128]{2,1,0:T(8,128)S(1)} %get-tuple-element.23), channel_id=1, source_target_pairs={{0,128},{8,136},{16,144},{24,152},{32,160},{40,168},{48,176},{56,1... | collective-permute-start | bytes 245768 | tf_op jit(solution)/shard_map/ppermute | solution.py:19
  38.1 5.0 %collective-permute-start.13 = (f32[4,40,128]{2,1,0:T(8,128)S(1)}, f32[4,40,128]{2,1,0:T(8,128)S(1)}, u32[]{:S(2)}, u32[]{:S(2)}) collective-permute-start(f32[4,40,128]{2,1,0:T(8,128)S(1)} %get-tuple-element.24), channel_id=1, source_target_pairs={{0,192},{8,200},{16,208},{24,216},{32,224},{40,232},{48,240},{56,2... | collective-permute-start | bytes 245768 | tf_op jit(solution)/shard_map/ppermute | solution.py:19
  39.6 12.3 %collective-permute-start.5 = (f32[4,48,128]{2,1,0:T(8,128)S(1)}, f32[4,48,128]{2,1,0:T(8,128)S(1)}, u32[]{:S(2)}, u32[]{:S(2)}) collective-permute-start(f32[4,48,128]{2,1,0:T(8,128)S(1)} %get-tuple-element.19), channel_id=1, source_target_pairs={{0,64},{8,72},{16,80},{24,88},{32,96},{40,104},{48,112},{56,120},{... | collective-permute-start | bytes 294920 | tf_op jit(solution)/shard_map/ppermute | solution.py:19
  40.3 14.2 %collective-permute-start.7 = (f32[4,48,128]{2,1,0:T(8,128)S(1)}, f32[4,48,128]{2,1,0:T(8,128)S(1)}, u32[]{:S(2)}, u32[]{:S(2)}) collective-permute-start(f32[4,48,128]{2,1,0:T(8,128)S(1)} %get-tuple-element.20), channel_id=1, source_target_pairs={{0,128},{8,136},{16,144},{24,152},{32,160},{40,168},{48,176},{56,1... | collective-permute-start | bytes 294920 | tf_op jit(solution)/shard_map/ppermute | solution.py:19
  41.1 13.4 %collective-permute-start.6 = (f32[4,48,128]{2,1,0:T(8,128)S(1)}, f32[4,48,128]{2,1,0:T(8,128)S(1)}, u32[]{:S(2)}, u32[]{:S(2)}) collective-permute-start(f32[4,48,128]{2,1,0:T(8,128)S(1)} %get-tuple-element.21), channel_id=1, source_target_pairs={{0,192},{8,200},{16,208},{24,216},{32,224},{40,232},{48,240},{56,2... | collective-permute-start | bytes 294920 | tf_op jit(solution)/shard_map/ppermute | solution.py:19
  43.2 14.1 %collective-permute-start.15 = (f32[40,128]{1,0:T(8,128)S(1)}, f32[40,128]{1,0:T(8,128)S(1)}, u32[]{:S(2)}, u32[]{:S(2)}) collective-permute-start(f32[40,128]{1,0:T(8,128)S(1)} %get-tuple-element.34), channel_id=1, source_target_pairs={{0,16},{8,24},{16,32},{24,40},{32,48},{40,56},{48,0},{56,8},{64,80... | collective-permute-start | bytes 61448 | tf_op jit(solution)/shard_map/ppermute | solution.py:19
  46.5 13.3 %collective-permute-start.17 = (f32[40,128]{1,0:T(8,128)S(1)}, f32[40,128]{1,0:T(8,128)S(1)}, u32[]{:S(2)}, u32[]{:S(2)}) collective-permute-start(f32[40,128]{1,0:T(8,128)S(1)} %get-tuple-element.35), channel_id=1, source_target_pairs={{0,32},{8,40},{16,48},{24,56},{32,0},{40,8},{48,16},{56,24},{64,96... | collective-permute-start | bytes 61448 | tf_op jit(solution)/shard_map/ppermute | solution.py:19
  51.9 7.9 %collective-permute-start.16 = (f32[40,128]{1,0:T(8,128)S(1)}, f32[40,128]{1,0:T(8,128)S(1)}, u32[]{:S(2)}, u32[]{:S(2)}) collective-permute-start(f32[40,128]{1,0:T(8,128)S(1)} %get-tuple-element.36), channel_id=1, source_target_pairs={{0,48},{8,56},{16,0},{24,8},{32,16},{40,24},{48,32},{56,40},{64,11... | collective-permute-start | bytes 61448 | tf_op jit(solution)/shard_map/ppermute | solution.py:19
  54.5 6.0 %collective-permute-start.8 = (f32[48,128]{1,0:T(8,128)S(1)}, f32[48,128]{1,0:T(8,128)S(1)}, u32[]{:S(2)}, u32[]{:S(2)}) collective-permute-start(f32[48,128]{1,0:T(8,128)S(1)} %get-tuple-element.25), channel_id=1, source_target_pairs={{0,16},{8,24},{16,32},{24,40},{32,48},{40,56},{48,0},{56,8},{64,80... | collective-permute-start | bytes 73736 | tf_op jit(solution)/shard_map/ppermute | solution.py:19
  54.9 7.9 %collective-permute-start.10 = (f32[48,128]{1,0:T(8,128)S(1)}, f32[48,128]{1,0:T(8,128)S(1)}, u32[]{:S(2)}, u32[]{:S(2)}) collective-permute-start(f32[48,128]{1,0:T(8,128)S(1)} %get-tuple-element.26), channel_id=1, source_target_pairs={{0,32},{8,40},{16,48},{24,56},{32,0},{40,8},{48,16},{56,24},{64,96... | collective-permute-start | bytes 73736 | tf_op jit(solution)/shard_map/ppermute | solution.py:19
  57.3 6.4 %collective-permute-start.9 = (f32[48,128]{1,0:T(8,128)S(1)}, f32[48,128]{1,0:T(8,128)S(1)}, u32[]{:S(2)}, u32[]{:S(2)}) collective-permute-start(f32[48,128]{1,0:T(8,128)S(1)} %get-tuple-element.27), channel_id=1, source_target_pairs={{0,48},{8,56},{16,0},{24,8},{32,16},{40,24},{48,32},{56,40},{64,11... | collective-permute-start | bytes 73736 | tf_op jit(solution)/shard_map/ppermute | solution.py:19

commit v4 on v2

--- a/solution.py
+++ b/solution.py
@@ -20,8 +20,8 @@
 
 
 ZLO_SWAP = [(i, i ^ 4) for i in range(8)]
-X_UP = [(i, (i & 4) | ((i + 1) & 3)) for i in range(8)]
-X_DOWN = [(i, (i & 4) | ((i - 1) & 3)) for i in range(8)]
+X_SWAP = [(i, i ^ 1) for i in range(8)]
+X_TURN = [(i, i ^ 3) for i in range(8)]
 CORE_SWAP = [(i, i ^ 1) for i in range(32)]
 Y_UP = [(i, (i + 8) % 32) for i in range(32)]
 Y_ACROSS = [(i, (i + 16) % 32) for i in range(32)]
@@ -31,16 +31,45 @@
 Z_DOWN = [(i, (i & 25) | ((i - 2) & 6)) for i in range(32)]
 
 
-def stats_kernel(place, probes, phenotype, genotype, held, mine, other, vec, vsum, arrived):
+def block_stats(held, first, vec, vsum):
+    samples = held.shape[1]
+    rows = pl.ds(pl.multiple_of(first, STEP), STEP)
+    acc = jnp.dot(held[rows, :], vec[...], preferred_element_type=jnp.float32)
+    squares, bases = [], []
+    for r in range(0, STEP, 64):
+        part = pl.ds(pl.multiple_of(first + r, 64), 64)
+        base = jnp.broadcast_to(held[part, 0:128].astype(jnp.float32)[:, 0:1], (64, 128))
+        sq = jnp.zeros((64, 128), jnp.float32)
+        for c in range(0, samples, 128):
+            dev = held[part, c : c + 128].astype(jnp.float32) - base
+            sq = sq + dev * dev
+        squares.append(jnp.sum(sq, axis=1, keepdims=True))
+        bases.append(base)
+    lane = lax.broadcasted_iota(jnp.int32, acc.shape, 1)
+    acc = jnp.where(lane == SQUARES, jnp.concatenate(squares, axis=0), acc)
+    acc = jnp.where(lane == VSUM, jnp.concatenate(bases, axis=0), acc)
+    flat = jnp.transpose(acc)[0:ROWS, :]
+    mean = flat[MEAN : MEAN + 1] / samples
+    apart = mean - flat[VSUM : VSUM + 1]
+    spread = jnp.maximum(flat[SQUARES : SQUARES + 1] - samples * apart * apart, 0.0)
+    row = lax.broadcasted_iota(jnp.int32, flat.shape, 0)
+    total = jnp.concatenate([vsum[0:1, :]] * (STEP // 128), axis=1)
+    flat = jnp.where(row == MEAN, mean, jnp.where(row == SQUARES, spread, flat))
+    return jnp.where(row == VSUM, total, flat)
+
+
+def first_kernel(place, probes, phenotype, genotype, held, other, vec, vsum, arrived):
     variants, samples = genotype.shape
     steps = variants // STEP
-    zlo = (place[0] // 4) % 2
+    ahead = steps // 2
+    away = (1 - (place[0] // 4) % 2) * ahead
 
     def copy(i):
-        rows = pl.ds(pl.multiple_of(i * STEP, STEP), STEP)
-        return pltpu.make_async_copy(genotype.at[rows], held.at[rows], arrived.at[i])
-
-    for i in range(steps):
+        source = pl.ds(pl.multiple_of(((i + away) % steps) * STEP, STEP), STEP)
+        target = pl.ds(pl.multiple_of(i * STEP, STEP), STEP)
+        return pltpu.make_async_copy(genotype.at[source], held.at[target], arrived.at[i])
+
+    for i in range(ahead):
         copy(i).start()
     row = lax.broadcasted_iota(jnp.int32, (32, samples), 0)
     low = jnp.concatenate([probes[...].astype(jnp.float32), jnp.zeros((12, samples), jnp.float32)], axis=0)
@@ -52,63 +81,53 @@
 
     def step(i, carry):
         copy(i).wait()
-        rows = pl.ds(pl.multiple_of(i * STEP, STEP), STEP)
-        acc = jnp.dot(held[rows, :], vec[...], preferred_element_type=jnp.float32)
-        squares, bases = [], []
-        for r in range(0, STEP, 64):
-            part = pl.ds(pl.multiple_of(i * STEP + r, 64), 64)
-            base = jnp.broadcast_to(held[part, 0:128].astype(jnp.float32)[:, 0:1], (64, 128))
-            sq = jnp.zeros((64, 128), jnp.float32)
-            for c in range(0, samples, 128):
-                dev = held[part, c : c + 128].astype(jnp.float32) - base
-                sq = sq + dev * dev
-            squares.append(jnp.sum(sq, axis=1, keepdims=True))
-            bases.append(base)
-        lane = lax.broadcasted_iota(jnp.int32, acc.shape, 1)
-        acc = jnp.where(lane == SQUARES, jnp.concatenate(squares, axis=0), acc)
-        acc = jnp.where(lane == VSUM, jnp.concatenate(bases, axis=0), acc)
-        flat = jnp.transpose(acc)[0:ROWS, :]
-        mean = flat[MEAN : MEAN + 1] / samples
-        apart = mean - flat[VSUM : VSUM + 1]
-        spread = jnp.maximum(flat[SQUARES : SQUARES + 1] - samples * apart * apart, 0.0)
-        row = lax.broadcasted_iota(jnp.int32, flat.shape, 0)
-        total = jnp.concatenate([vsum[0:1, :]] * (STEP // 128), axis=1)
-        flat = jnp.where(row == MEAN, mean, jnp.where(row == SQUARES, spread, flat))
-        flat = jnp.where(row == VSUM, total, flat)
-        half = steps // 2
-        spot = pl.ds(pl.multiple_of((i % half) * STEP, STEP), STEP)
-        own = (i // half) == zlo
-
-        @pl.when(own)
-        def _():
-            mine[:, spot] = flat
-
-        @pl.when(jnp.logical_not(own))
-        def _():
-            other[:, spot] = flat
-
+        copy(i + ahead).start()
+        other[:, pl.ds(pl.multiple_of(i * STEP, STEP), STEP)] = block_stats(held, i * STEP, vec, vsum)
         return carry
 
-    lax.fori_loop(0, steps, step, 0)
+    lax.fori_loop(0, ahead, step, 0)
+    for i in range(ahead, steps):
+        copy(i).wait()
+
+
+def second_kernel(held, vec, vsum, mine):
+    half = held.shape[0] // 2
+
+    def step(i, carry):
+        mine[:, pl.ds(pl.multiple_of(i * STEP, STEP), STEP)] = block_stats(held, half + i * STEP, vec, vsum)
+        return carry
+
+    lax.fori_loop(0, half // STEP, step, 0)
 
 
 def local_stats(place, probes, phenotype, genotype):
     variants, samples = genotype.shape
     vmem = pl.BlockSpec(memory_space=pltpu.VMEM)
     block = jax.ShapeDtypeStruct((ROWS, variants // 2), jnp.float32)
-    return pl.pallas_call(
-        stats_kernel,
+    held, other, vec, vsum = pl.pallas_call(
+        first_kernel,
         in_specs=[pl.BlockSpec(memory_space=pltpu.SMEM), vmem, vmem, pl.BlockSpec(memory_space=pltpu.HBM)],
-        out_specs=(vmem, vmem, vmem),
-        out_shape=(jax.ShapeDtypeStruct(genotype.shape, genotype.dtype), block, block),
-        scratch_shapes=[
-            pltpu.VMEM((samples, 128), jnp.bfloat16),
-            pltpu.VMEM((8, 128), jnp.float32),
-            pltpu.SemaphoreType.DMA((variants // STEP,)),
-        ],
+        out_specs=(vmem, vmem, vmem, vmem),
+        out_shape=(
+            jax.ShapeDtypeStruct(genotype.shape, genotype.dtype),
+            block,
+            jax.ShapeDtypeStruct((samples, 128), jnp.bfloat16),
+            jax.ShapeDtypeStruct((8, 128), jnp.float32),
+        ),
+        scratch_shapes=[pltpu.SemaphoreType.DMA((variants // STEP,))],
         compiler_params=pltpu.CompilerParams(vmem_limit_bytes=40 * 1024 * 1024),
-        name="local_stats",
+        name="first_stats",
     )(place, probes, phenotype, genotype)
+    theirs = shifted(other, "smp", ZLO_SWAP)
+    mine = pl.pallas_call(
+        second_kernel,
+        in_specs=[vmem, vmem, vmem],
+        out_specs=vmem,
+        out_shape=block,
+        compiler_params=pltpu.CompilerParams(vmem_limit_bytes=16 * 1024 * 1024),
+        name="second_stats",
+    )(held, vec, vsum)
+    return held, mine, theirs
 
 
 def merged(pieces, each):
@@ -119,15 +138,10 @@
     return jnp.where(row == MEAN, mean, jnp.where(row == SQUARES, total + apart, total))
 
 
-def over_samples(mine, other, samples):
-    own = merged([mine, shifted(other, "smp", ZLO_SWAP)], samples)
-    below = shifted(own, "smp", X_UP)
-    above = shifted(own, "smp", X_DOWN)
-    cut = own.shape[1] // 2
-    far_low = shifted(below[:, :cut], "smp", X_UP)
-    far_high = shifted(above[:, cut:], "smp", X_DOWN)
-    far = jnp.concatenate([far_low, far_high], axis=1)
-    own = merged([own, below, above, far], 2 * samples)
+def over_samples(mine, theirs, samples):
+    own = merged([mine, theirs], samples)
+    own = merged([own, shifted(own, "smp", X_SWAP)], 2 * samples)
+    own = merged([own, shifted(own, "smp", X_TURN)], 4 * samples)
     return own, shifted(own, "smp", ZLO_SWAP)
 
 
@@ -137,10 +151,10 @@
 
 def terms_kernel(place, own, back, labels, genotype, keep, give, weights, shift):
     variants, samples = genotype.shape
+    half = variants // 2
+    stats = jnp.concatenate([back[...], own[...]], axis=1)
     lower = (place[0] // 4) % 2 == 0
-    stats = jnp.concatenate(
-        [jnp.where(lower, own[...], back[...]), jnp.where(lower, back[...], own[...])], axis=1
-    )
+    tags = jnp.where(lower, jnp.concatenate([labels[:, half:], labels[:, :half]], axis=1), labels[...])
     mean = stats[MEAN : MEAN + 1]
     scale = lax.rsqrt(stats[SQUARES : SQUARES + 1] / N + EPS)
     sub = lax.broadcasted_iota(jnp.int32, (ROWS, 128), 0)
@@ -149,7 +163,7 @@
     projected = (stats - vsum * mean) * scale
     weight = projected * scale
     comp = lax.broadcasted_iota(jnp.int32, (K, variants), 0)
-    member = comp == labels[...]
+    member = comp == tags
     counts = jnp.sum(jnp.where(member, 1.0, 0.0), axis=1, keepdims=True)
 
     def rows_of(array, j):
@@ -210,8 +224,8 @@
 def body(genotype, labels, probes, phenotype):
     variants, samples = genotype.shape
     place = lax.axis_index(("var", "smp")).astype(jnp.int32).reshape(1)
-    held, mine, other = local_stats(place, probes, phenotype, genotype)
-    own, back = over_samples(mine, other, samples)
+    held, mine, theirs = local_stats(place, probes, phenotype, genotype)
+    own, back = over_samples(mine, theirs, samples)
     keep, give = local_terms(place, own, back, labels.reshape(1, variants), held)
     packed = over_variants(keep, give)
     rows = jnp.concatenate([packed[:, :64], packed[:, 64:]], axis=0).reshape(NV + 1, K, 64)

time: 62.9 us -> 59.5 us (0.946)
  waiting for transfers between devices: 28 us -> 22.3 us
  starting transfers between devices: 22.1 us -> 23.7 us
    ppermute x13 -> x11, waiting for transfers between devices: 28 us -> 22.3 us  [shifted(): return lax.ppermute(array, axis, perm)]
    ppermute x13 -> x11, starting transfers between devices: 22.1 us -> 23.7 us  [shifted(): return lax.ppermute(array, axis, perm)]
    pallas_call x1 -> x2, Pallas kernels: 7.25 us -> 7.75 us  [the longest x1 4.79 us: local_stats(): pl.pallas_call(first_kernel, in_specs=[pl.BlockSpec(memory_space=pltpu.SM...]
    unnamed x7 -> x6, local copies, waits for them, and re-layouts: 1.6 us -> 1.58 us
  transfers between devices with their start and end apart: 13 -> 11, of which waited for: 11 -> 8; matrix products, arithmetic and copies ran while one was open for 0% -> 0% of each run, Pallas kernels for 0% -> 5%
where the time goes in v4:
time: 59.5 us; the launch traced here: 59.3 us
  starting transfers between devices  23.7 us (40%)
  waiting for transfers between devices  22.3 us (37%)
  Pallas kernels  10 us (17%)
  local copies, waits for them, and re-layouts  2.51 us (4%)
  other arithmetic  0.68 us (1%)
    ppermute x11, starting transfers between devices, shifted(): return lax.ppermute(array, axis, perm)  23.7 us
    ppermute x11, waiting for transfers between devices, shifted(): return lax.ppermute(array, axis, perm)  22.3 us
    pallas_call x1, Pallas kernels, local_stats(): pl.pallas_call(first_kernel, in_specs=[pl.BlockSpec(memory_space=pltpu.SM...  4.79 us
    pallas_call x1, Pallas kernels, local_stats(): pl.pallas_call(second_kernel, in_specs=[vmem, vmem, vmem], out_specs=vmem...  2.96 us
    pallas_call x1, Pallas kernels, local_terms(): pl.pallas_call(terms_kernel, in_specs=[pl.BlockSpec(memory_space=pltpu.SM...  2.26 us
    unnamed x6, local copies, waits for them, and re-layouts  1.58 us
  transfers between devices with their start and end apart: 11, of which 8 were waited for; matrix products, arithmetic and copies ran while one was open for 0% of the time, Pallas kernels for 5%

profile of v4, /device:TPU:6, one launch (start us, length us, event | category | flops | bytes accessed | tf_op | source)
XLA Modules:
  0.0 59.3 jit_solution(3975508357216562277)
XLA Ops:
  0.0 0.0 copy-start
  0.0 0.9 %copy-done = bf16[20,2048]{1,0:T(8,128)(2,1)S(1)} copy-done((bf16[20,2048]{1,0:T(8,128)(2,1)S(1)}, bf16[20,2048]{1,0:T(8,128)(2,1)}, u32[]{:S(2)}) %copy-start) | copy-done | bytes 81944
  0.9 0.0 copy-start.2
  0.9 0.7 %copy-done.2 = bf16[2048]{0:T(1024)(128)(2,1)S(1)} copy-done((bf16[2048]{0:T(1024)(128)(2,1)S(1)}, bf16[2048]{0:T(1024)(128)(2,1)}, u32[]{:S(2)}) %copy-start.2) | copy-done | bytes 4120
  1.6 0.0 copy-start.1
  1.6 4.8 %first_stats.1 = (bf16[2048,2048]{1,0:T(8,128)(2,1)S(1)}, f32[24,1024]{1,0:T(8,128)S(1)}, bf16[2048,128]{1,0:T(8,128)(2,1)S(1)}, f32[8,128]{1,0:T(8,128)S(1)}) custom-call(s32[1]{0:T(128)} %bitcast.place, bf16[20,2048]{1,0:T(8,128)(2,1)S(1)} %copy-done, bf16[2048]{0:T(1024)(128)(2,1)S(1)} %copy-done.2, bf16[2048,2048]{1,0:T(8,128)(2,1)} %genotype.1), custom_call_target="tpu_custom_call" | custom-call | tf_op jit(solution)/shard_map/first_stats/pallas_call | solution.py:107
  6.4 2.0 %collective-permute-start = (f32[24,1024]{1,0:T(8,128)S(1)}, f32[24,1024]{1,0:T(8,128)S(1)}, u32[]{:S(2)}, u32[]{:S(2)}) collective-permute-start(f32[24,1024]{1,0:T(8,128)S(1)} %get-tuple-element.14), channel_id=1, source_target_pairs={{0,4},{1,5},{2,6},{3,7},{4,0},{5,1},{6,2},{7,3},{8,12},{9,13},{10,... | collective-permute-start | bytes 294920 | tf_op jit(solution)/shard_map/ppermute | solution.py:19
  8.4 3.0 %second_stats.1 = f32[24,1024]{1,0:T(8,128)S(1)} custom-call(bf16[2048,2048]{1,0:T(8,128)(2,1)S(1)} %get-tuple-element.11.held.genotype, bf16[2048,128]{1,0:T(8,128)(2,1)S(1)} %get-tuple-element.12.vec, f32[8,128]{1,0:T(8,128)S(1)} %get-tuple-element.13.vsum), custom_call_target="tpu_custom_call" | custom-call | tf_op jit(solution)/shard_map/second_stats/pallas_call | solution.py:122
  11.4 0.0 collective-permute-done
  11.4 0.1 fusion.3
  11.5 0.9 %collective-permute-start.1 = (f32[24,1024]{1,0:T(8,128)S(1)}, f32[24,1024]{1,0:T(8,128)S(1)}, u32[]{:S(2)}, u32[]{:S(2)}) collective-permute-start(f32[24,1024]{1,0:T(8,128)S(1)} %fusion.3), channel_id=1, source_target_pairs={{0,1},{1,0},{2,3},{3,2},{4,5},{5,4},{6,7},{7,6},{8,9},{9,8},{10,11... | collective-permute-start | bytes 294920 | tf_op jit(solution)/shard_map/ppermute | solution.py:19
  12.4 3.8 %collective-permute-done.1 = f32[24,1024]{1,0:T(8,128)S(1)} collective-permute-done((f32[24,1024]{1,0:T(8,128)S(1)}, f32[24,1024]{1,0:T(8,128)S(1)}, u32[]{:S(2)}, u32[]{:S(2)}) %collective-permute-start.1) | collective-permute-done | bytes 98336 | tf_op jit(solution)/shard_map/ppermute | solution.py:19
  16.2 0.1 fusion.26
  16.3 0.1 fusion.4
  16.4 2.0 %collective-permute-start.2 = (f32[24,1024]{1,0:T(8,128)S(1)}, f32[24,1024]{1,0:T(8,128)S(1)}, u32[]{:S(2)}, u32[]{:S(2)}) collective-permute-start(f32[24,1024]{1,0:T(8,128)S(1)} %fusion.4), channel_id=1, source_target_pairs={{0,3},{1,2},{2,1},{3,0},{4,7},{5,6},{6,5},{7,4},{8,11},{9,10},{10,... | collective-permute-start | bytes 294920 | tf_op jit(solution)/shard_map/ppermute | solution.py:19
  18.4 3.9 %collective-permute-done.2 = f32[24,1024]{1,0:T(8,128)S(1)} collective-permute-done((f32[24,1024]{1,0:T(8,128)S(1)}, f32[24,1024]{1,0:T(8,128)S(1)}, u32[]{:S(2)}, u32[]{:S(2)}) %collective-permute-start.2) | collective-permute-done | bytes 98336 | tf_op jit(solution)/shard_map/ppermute | solution.py:19
  22.3 0.1 fusion.25
  22.4 0.1 fusion.5.own
  22.5 1.7 %collective-permute-start.3 = (f32[24,1024]{1,0:T(8,128)S(1)}, f32[24,1024]{1,0:T(8,128)S(1)}, u32[]{:S(2)}, u32[]{:S(2)}) collective-permute-start(f32[24,1024]{1,0:T(8,128)S(1)} %fusion.5.own), channel_id=1, source_target_pairs={{0,4},{1,5},{2,6},{3,7},{4,0},{5,1},{6,2},{7,3},{8,12},{9,13},{10,... | collective-permute-start | bytes 294920 | tf_op jit(solution)/shard_map/ppermute | solution.py:19
  24.2 3.0 %collective-permute-done.3.back = f32[24,1024]{1,0:T(8,128)S(1)} collective-permute-done((f32[24,1024]{1,0:T(8,128)S(1)}, f32[24,1024]{1,0:T(8,128)S(1)}, u32[]{:S(2)}, u32[]{:S(2)}) %collective-permute-start.3) | collective-permute-done | bytes 98336 | tf_op jit(solution)/shard_map/ppermute | solution.py:19
  27.2 0.0 copy-done.1
  27.2 2.3 %local_terms.1 = (f32[4,4,88,128]{3,2,1,0:T(8,128)S(1)}, f32[4,4,88,128]{3,2,1,0:T(8,128)S(1)}) custom-call(s32[1]{0:T(128)} %bitcast.place, f32[24,1024]{1,0:T(8,128)S(1)} %fusion.5.own, f32[24,1024]{1,0:T(8,128)S(1)} %collective-permute-done.3.back, s32[1,2048]{1,0:T(1,128)S(1)} %bitcast.46, bf16[2048,2048]{1,0:T(8,128)(2,1)S(1)} %get-tuple-element.11.held.genotype), custom_call_target="tpu_custom_call" | custom-call | tf_op jit(solution)/shard_map/local_terms/pallas_call | solution.py:202
  29.5 0.1 collective-permute-start.4
  29.6 2.2 %collective-permute-done.4 = f32[4,4,88,128]{3,2,1,0:T(8,128)S(1)} collective-permute-done((f32[4,4,88,128]{3,2,1,0:T(8,128)S(1)}, f32[4,4,88,128]{3,2,1,0:T(8,128)S(1)}, u32[]{:S(2)}, u32[]{:S(2)}) %collective-permute-start.4) | collective-permute-done | bytes 720928 | tf_op jit(solution)/shard_map/ppermute | solution.py:19
  31.8 0.1 add.88
  31.9 1.7 %collective-permute-start.5 = (f32[4,88,128]{2,1,0:T(8,128)S(1)}, f32[4,88,128]{2,1,0:T(8,128)S(1)}, u32[]{:S(2)}, u32[]{:S(2)}) collective-permute-start(f32[4,88,128]{2,1,0:T(8,128)S(1)} %get-tuple-element.17), channel_id=1, source_target_pairs={{0,64},{8,72},{16,80},{24,88},{32,96},{40,104},{48,112},{56,120},{... | collective-permute-start | bytes 540680 | tf_op jit(solution)/shard_map/ppermute | solution.py:19
  33.6 2.9 %collective-permute-start.7 = (f32[4,88,128]{2,1,0:T(8,128)S(1)}, f32[4,88,128]{2,1,0:T(8,128)S(1)}, u32[]{:S(2)}, u32[]{:S(2)}) collective-permute-start(f32[4,88,128]{2,1,0:T(8,128)S(1)} %get-tuple-element.18), channel_id=1, source_target_pairs={{0,128},{8,136},{16,144},{24,152},{32,160},{40,168},{48,176},{56,1... | collective-permute-start | bytes 540680 | tf_op jit(solution)/shard_map/ppermute | solution.py:19
  36.5 1.3 %collective-permute-start.6 = (f32[4,88,128]{2,1,0:T(8,128)S(1)}, f32[4,88,128]{2,1,0:T(8,128)S(1)}, u32[]{:S(2)}, u32[]{:S(2)}) collective-permute-start(f32[4,88,128]{2,1,0:T(8,128)S(1)} %get-tuple-element.19), channel_id=1, source_target_pairs={{0,192},{8,200},{16,208},{24,216},{32,224},{40,232},{48,240},{56,2... | collective-permute-start | bytes 540680 | tf_op jit(solution)/shard_map/ppermute | solution.py:19
  37.8 2.0 %collective-permute-done.5 = f32[4,88,128]{2,1,0:T(8,128)S(1)} collective-permute-done((f32[4,88,128]{2,1,0:T(8,128)S(1)}, f32[4,88,128]{2,1,0:T(8,128)S(1)}, u32[]{:S(2)}, u32[]{:S(2)}) %collective-permute-start.5) | collective-permute-done | bytes 180256 | tf_op jit(solution)/shard_map/ppermute | solution.py:19
  39.9 5.0 %collective-permute-done.7 = f32[4,88,128]{2,1,0:T(8,128)S(1)} collective-permute-done((f32[4,88,128]{2,1,0:T(8,128)S(1)}, f32[4,88,128]{2,1,0:T(8,128)S(1)}, u32[]{:S(2)}, u32[]{:S(2)}) %collective-permute-start.7) | collective-permute-done | bytes 180256 | tf_op jit(solution)/shard_map/ppermute | solution.py:19
  44.9 0.0 collective-permute-done.6
  45.0 3.3 %collective-permute-start.8 = (f32[88,128]{1,0:T(8,128)S(1)}, f32[88,128]{1,0:T(8,128)S(1)}, u32[]{:S(2)}, u32[]{:S(2)}) collective-permute-start(f32[88,128]{1,0:T(8,128)S(1)} %get-tuple-element.20), channel_id=1, source_target_pairs={{0,16},{8,24},{16,32},{24,40},{32,48},{40,56},{48,0},{56,8},{64,80... | collective-permute-start | bytes 135176 | tf_op jit(solution)/shard_map/ppermute | solution.py:19
  48.3 5.1 %collective-permute-start.10 = (f32[88,128]{1,0:T(8,128)S(1)}, f32[88,128]{1,0:T(8,128)S(1)}, u32[]{:S(2)}, u32[]{:S(2)}) collective-permute-start(f32[88,128]{1,0:T(8,128)S(1)} %get-tuple-element.21), channel_id=1, source_target_pairs={{0,32},{8,40},{16,48},{24,56},{32,0},{40,8},{48,16},{56,24},{64,96... | collective-permute-start | bytes 135176 | tf_op jit(solution)/shard_map/ppermute | solution.py:19
  53.4 2.7 %collective-permute-start.9 = (f32[88,128]{1,0:T(8,128)S(1)}, f32[88,128]{1,0:T(8,128)S(1)}, u32[]{:S(2)}, u32[]{:S(2)}) collective-permute-start(f32[88,128]{1,0:T(8,128)S(1)} %get-tuple-element.22), channel_id=1, source_target_pairs={{0,48},{8,56},{16,0},{24,8},{32,16},{40,24},{48,32},{56,40},{64,11... | collective-permute-start | bytes 135176 | tf_op jit(solution)/shard_map/ppermute | solution.py:19
  56.1 0.0 collective-permute-done.8
  56.1 0.4 collective-permute-done.10
  56.5 1.9 %collective-permute-done.9 = f32[88,128]{1,0:T(8,128)S(1)} collective-permute-done((f32[88,128]{1,0:T(8,128)S(1)}, f32[88,128]{1,0:T(8,128)S(1)}, u32[]{:S(2)}, u32[]{:S(2)}) %collective-permute-start.9) | collective-permute-done | bytes 45088 | tf_op jit(solution)/shard_map/ppermute | solution.py:19
  58.4 0.1 slice.110
  58.5 0.1 fusion.24
  58.6 0.7 %copy.6 = f32[8,21,1,64]{3,2,1,0:T(1,128)} copy(f32[8,21,1,64]{3,0,2,1:T(8,128)S(1)} %fusion.8) | data formatting | bytes 86016 | tf_op jit(solution)/shard_map/reshape | solution.py:233
  (10 shorter events, 0.2 us)
Async XLA Ops:
  0.0 0.9 %copy-start = (bf16[20,2048]{1,0:T(8,128)(2,1)S(1)}, bf16[20,2048]{1,0:T(8,128)(2,1)}, u32[]{:S(2)}) copy-start(bf16[20,2048]{1,0:T(8,128)(2,1)} %probes.1) | copy-start | bytes 245764
  0.9 0.7 %copy-start.2 = (bf16[2048]{0:T(1024)(128)(2,1)S(1)}, bf16[2048]{0:T(1024)(128)(2,1)}, u32[]{:S(2)}) copy-start(bf16[2048]{0:T(1024)(128)(2,1)} %phenotype.1) | copy-start | bytes 12292
  1.6 25.7 %copy-start.1 = (s32[2048]{0:T(1024)S(1)}, s32[2048]{0:T(1024)}, u32[]{:S(2)}) copy-start(s32[2048]{0:T(1024)} %param.5) | copy-start | bytes 24580
  6.4 5.0 %collective-permute-start = (f32[24,1024]{1,0:T(8,128)S(1)}, f32[24,1024]{1,0:T(8,128)S(1)}, u32[]{:S(2)}, u32[]{:S(2)}) collective-permute-start(f32[24,1024]{1,0:T(8,128)S(1)} %get-tuple-element.14), channel_id=1, source_target_pairs={{0,4},{1,5},{2,6},{3,7},{4,0},{5,1},{6,2},{7,3},{8,12},{9,13},{10,... | collective-permute-start | bytes 294920 | tf_op jit(solution)/shard_map/ppermute | solution.py:19
  11.5 4.7 %collective-permute-start.1 = (f32[24,1024]{1,0:T(8,128)S(1)}, f32[24,1024]{1,0:T(8,128)S(1)}, u32[]{:S(2)}, u32[]{:S(2)}) collective-permute-start(f32[24,1024]{1,0:T(8,128)S(1)} %fusion.3), channel_id=1, source_target_pairs={{0,1},{1,0},{2,3},{3,2},{4,5},{5,4},{6,7},{7,6},{8,9},{9,8},{10,11... | collective-permute-start | bytes 294920 | tf_op jit(solution)/shard_map/ppermute | solution.py:19
  16.4 5.9 %collective-permute-start.2 = (f32[24,1024]{1,0:T(8,128)S(1)}, f32[24,1024]{1,0:T(8,128)S(1)}, u32[]{:S(2)}, u32[]{:S(2)}) collective-permute-start(f32[24,1024]{1,0:T(8,128)S(1)} %fusion.4), channel_id=1, source_target_pairs={{0,3},{1,2},{2,1},{3,0},{4,7},{5,6},{6,5},{7,4},{8,11},{9,10},{10,... | collective-permute-start | bytes 294920 | tf_op jit(solution)/shard_map/ppermute | solution.py:19
  22.5 4.7 %collective-permute-start.3 = (f32[24,1024]{1,0:T(8,128)S(1)}, f32[24,1024]{1,0:T(8,128)S(1)}, u32[]{:S(2)}, u32[]{:S(2)}) collective-permute-start(f32[24,1024]{1,0:T(8,128)S(1)} %fusion.5.own), channel_id=1, source_target_pairs={{0,4},{1,5},{2,6},{3,7},{4,0},{5,1},{6,2},{7,3},{8,12},{9,13},{10,... | collective-permute-start | bytes 294920 | tf_op jit(solution)/shard_map/ppermute | solution.py:19
  29.5 2.3 %collective-permute-start.4 = (f32[4,4,88,128]{3,2,1,0:T(8,128)S(1)}, f32[4,4,88,128]{3,2,1,0:T(8,128)S(1)}, u32[]{:S(2)}, u32[]{:S(2)}) collective-permute-start(f32[4,4,88,128]{3,2,1,0:T(8,128)S(1)} %get-tuple-element.16), channel_id=1, source_target_pairs={{0,8},{8,0},{16,24},{24,16},{32,40},{40,32},{48,56},{56,48},{64,72... | collective-permute-start | bytes 2162696 | tf_op jit(solution)/shard_map/ppermute | solution.py:19
  31.9 7.9 %collective-permute-start.5 = (f32[4,88,128]{2,1,0:T(8,128)S(1)}, f32[4,88,128]{2,1,0:T(8,128)S(1)}, u32[]{:S(2)}, u32[]{:S(2)}) collective-permute-start(f32[4,88,128]{2,1,0:T(8,128)S(1)} %get-tuple-element.17), channel_id=1, source_target_pairs={{0,64},{8,72},{16,80},{24,88},{32,96},{40,104},{48,112},{56,120},{... | collective-permute-start | bytes 540680 | tf_op jit(solution)/shard_map/ppermute | solution.py:19
  33.6 11.3 %collective-permute-start.7 = (f32[4,88,128]{2,1,0:T(8,128)S(1)}, f32[4,88,128]{2,1,0:T(8,128)S(1)}, u32[]{:S(2)}, u32[]{:S(2)}) collective-permute-start(f32[4,88,128]{2,1,0:T(8,128)S(1)} %get-tuple-element.18), channel_id=1, source_target_pairs={{0,128},{8,136},{16,144},{24,152},{32,160},{40,168},{48,176},{56,1... | collective-permute-start | bytes 540680 | tf_op jit(solution)/shard_map/ppermute | solution.py:19
  36.5 8.4 %collective-permute-start.6 = (f32[4,88,128]{2,1,0:T(8,128)S(1)}, f32[4,88,128]{2,1,0:T(8,128)S(1)}, u32[]{:S(2)}, u32[]{:S(2)}) collective-permute-start(f32[4,88,128]{2,1,0:T(8,128)S(1)} %get-tuple-element.19), channel_id=1, source_target_pairs={{0,192},{8,200},{16,208},{24,216},{32,224},{40,232},{48,240},{56,2... | collective-permute-start | bytes 540680 | tf_op jit(solution)/shard_map/ppermute | solution.py:19
  45.0 11.1 %collective-permute-start.8 = (f32[88,128]{1,0:T(8,128)S(1)}, f32[88,128]{1,0:T(8,128)S(1)}, u32[]{:S(2)}, u32[]{:S(2)}) collective-permute-start(f32[88,128]{1,0:T(8,128)S(1)} %get-tuple-element.20), channel_id=1, source_target_pairs={{0,16},{8,24},{16,32},{24,40},{32,48},{40,56},{48,0},{56,8},{64,80... | collective-permute-start | bytes 135176 | tf_op jit(solution)/shard_map/ppermute | solution.py:19
  48.3 8.2 %collective-permute-start.10 = (f32[88,128]{1,0:T(8,128)S(1)}, f32[88,128]{1,0:T(8,128)S(1)}, u32[]{:S(2)}, u32[]{:S(2)}) collective-permute-start(f32[88,128]{1,0:T(8,128)S(1)} %get-tuple-element.21), channel_id=1, source_target_pairs={{0,32},{8,40},{16,48},{24,56},{32,0},{40,8},{48,16},{56,24},{64,96... | collective-permute-start | bytes 135176 | tf_op jit(solution)/shard_map/ppermute | solution.py:19
  53.4 5.0 %collective-permute-start.9 = (f32[88,128]{1,0:T(8,128)S(1)}, f32[88,128]{1,0:T(8,128)S(1)}, u32[]{:S(2)}, u32[]{:S(2)}) collective-permute-start(f32[88,128]{1,0:T(8,128)S(1)} %get-tuple-element.22), channel_id=1, source_target_pairs={{0,48},{8,56},{16,0},{24,8},{32,16},{40,24},{48,32},{56,40},{64,11... | collective-permute-start | bytes 135176 | tf_op jit(solution)/shard_map/ppermute | solution.py:19

commit v5 on v4

--- a/solution.py
+++ b/solution.py
@@ -149,12 +149,7 @@
 PACK = 88
 
 
-def terms_kernel(place, own, back, labels, genotype, keep, give, weights, shift):
-    variants, samples = genotype.shape
-    half = variants // 2
-    stats = jnp.concatenate([back[...], own[...]], axis=1)
-    lower = (place[0] // 4) % 2 == 0
-    tags = jnp.where(lower, jnp.concatenate([labels[:, half:], labels[:, :half]], axis=1), labels[...])
+def weigh(stats, tags, weights, shift):
     mean = stats[MEAN : MEAN + 1]
     scale = lax.rsqrt(stats[SQUARES : SQUARES + 1] / N + EPS)
     sub = lax.broadcasted_iota(jnp.int32, (ROWS, 128), 0)
@@ -162,30 +157,46 @@
     vsum = jnp.sum(jnp.where(sub == lane, stats[VSUM : VSUM + 1, 0:128], 0.0), axis=1, keepdims=True)
     projected = (stats - vsum * mean) * scale
     weight = projected * scale
-    comp = lax.broadcasted_iota(jnp.int32, (K, variants), 0)
-    member = comp == tags
+    member = lax.broadcasted_iota(jnp.int32, (K, stats.shape[1]), 0) == tags
     counts = jnp.sum(jnp.where(member, 1.0, 0.0), axis=1, keepdims=True)
 
-    def rows_of(array, j):
-        return jnp.where(member, array[j : j + 1], 0.0)
+    def rows_of(j):
+        return jnp.where(member, weight[j : j + 1], 0.0)
 
     for pair in range(PAIRS + 1):
-        first = rows_of(weight, 2 * pair)
-        second = rows_of(weight, 2 * pair + 1) if pair < PAIRS else jnp.zeros_like(first)
+        first = rows_of(2 * pair)
+        second = rows_of(2 * pair + 1) if pair < PAIRS else jnp.zeros_like(first)
         weights[16 * pair : 16 * pair + 16, :] = jnp.concatenate([first, second], axis=0).astype(jnp.bfloat16)
     for r in range(0, 2 * PACK, 16):
-        held = weights[r : r + 16, :].astype(jnp.float32)
-        shift[r : r + 16, :] = jnp.broadcast_to(jnp.sum(held * mean, axis=1, keepdims=True), (16, 128))
+        rows = weights[r : r + 16, :].astype(jnp.float32)
+        shift[r : r + 16, :] = jnp.broadcast_to(jnp.sum(rows * mean, axis=1, keepdims=True), (16, 128))
     shift[K * NV :, :] = jnp.broadcast_to(-counts, (K, 128))
 
+
+def own_kernel(place, own, labels, held, part, weights, shift):
+    samples = held.shape[1]
+    half = own.shape[1]
+    lower = (place[0] // 4) % 2 == 0
+    weigh(own[...], jnp.where(lower, labels[:, :half], labels[:, half:]), weights, shift)
+    for c in range(0, samples, 256):
+        block = jnp.dot(weights[...], held[half:, c : c + 256], preferred_element_type=jnp.float32)
+        for h in range(0, 256, 128):
+            part[:, c + h : c + h + 128] = block[:, h : h + 128] - shift[...]
+
+
+def terms_kernel(place, back, labels, held, part, keep, give, weights, shift):
+    samples = held.shape[1]
+    half = back.shape[1]
+    lower = (place[0] // 4) % 2 == 0
+    weigh(back[...], jnp.where(lower, labels[:, half:], labels[:, :half]), weights, shift)
     spot = place[0] // 8
     y, z, core = spot // 8, (spot // 2) % 4, spot % 2
     low_lanes = lax.broadcasted_iota(jnp.int32, (PACK, 128), 1) < 64
     for c in range(samples // 256):
-        block = jnp.dot(weights[...], genotype[:, 256 * c : 256 * c + 256], preferred_element_type=jnp.float32)
+        block = jnp.dot(weights[...], held[:half, 256 * c : 256 * c + 256], preferred_element_type=jnp.float32)
         for h in range(2):
             t = 2 * c + h
-            tile = block[:, 128 * h : 128 * h + 128] - shift[...]
+            tile = block[:, 128 * h : 128 * h + 128] + (part[:, 128 * t : 128 * t + 128] - shift[...])
             a, b = tile[:PACK], tile[PACK:]
             ra, rb = pltpu.roll(a, 64, 1), pltpu.roll(b, 64, 1)
             zero = jnp.where(low_lanes, a, rb)
@@ -195,19 +206,31 @@
             give[ky, kz] = jnp.where(core == 0, one, zero)
 
 
-def local_terms(place, own, back, labels, genotype):
+def local_terms(place, own, back, labels, held):
     vmem = pl.BlockSpec(memory_space=pltpu.VMEM)
+    smem = pl.BlockSpec(memory_space=pltpu.SMEM)
+    samples = held.shape[1]
     tiles = jax.ShapeDtypeStruct((4, 4, PACK, 128), jnp.float32)
-    variants = genotype.shape[0]
+    scratch = [pltpu.VMEM((2 * PACK, own.shape[1]), jnp.bfloat16), pltpu.VMEM((2 * PACK, 128), jnp.float32)]
+    params = pltpu.CompilerParams(vmem_limit_bytes=16 * 1024 * 1024)
+    part = pl.pallas_call(
+        own_kernel,
+        in_specs=[smem, vmem, vmem, vmem],
+        out_specs=vmem,
+        out_shape=jax.ShapeDtypeStruct((2 * PACK, samples), jnp.float32),
+        scratch_shapes=scratch,
+        compiler_params=params,
+        name="own_terms",
+    )(place, own, labels, held)
     return pl.pallas_call(
         terms_kernel,
-        in_specs=[pl.BlockSpec(memory_space=pltpu.SMEM), vmem, vmem, vmem, vmem],
+        in_specs=[smem, vmem, vmem, vmem, vmem],
         out_specs=(vmem, vmem),
         out_shape=(tiles, tiles),
-        scratch_shapes=[pltpu.VMEM((2 * PACK, variants), jnp.bfloat16), pltpu.VMEM((2 * PACK, 128), jnp.float32)],
-        compiler_params=pltpu.CompilerParams(vmem_limit_bytes=16 * 1024 * 1024),
+        scratch_shapes=scratch,
+        compiler_params=params,
         name="local_terms",
-    )(place, own, back, labels, genotype)
+    )(place, back, labels, held, part)
 
 
 def direct_sum(parts, axis, up, across, down):

time: 59.5 us -> 58.5 us (0.983)
  waiting for transfers between devices: 22.3 us -> 21.1 us
    ppermute x11, waiting for transfers between devices: 22.3 us -> 21.1 us  [shifted(): return lax.ppermute(array, axis, perm)]
    pallas_call x1 -> x2, Pallas kernels: 2.26 us -> 2.46 us  [the longest x1 1.34 us: local_terms(): pl.pallas_call(terms_kernel, in_specs=[smem, vmem, vmem, vmem, vmem], out...]
  transfers between devices with their start and end apart: 11 -> 11, of which waited for: 8 -> 8; matrix products, arithmetic and copies ran while one was open for 0% -> 0% of each run, Pallas kernels for 5% -> 7%
where the time goes in v5:
time: 58.5 us; the launch traced here: 58.4 us
  starting transfers between devices  23.7 us (41%)
  waiting for transfers between devices  21.1 us (36%)
  Pallas kernels  10.2 us (17%)
  local copies, waits for them, and re-layouts  2.51 us (4%)
  other arithmetic  0.68 us (1%)
    ppermute x11, starting transfers between devices, shifted(): return lax.ppermute(array, axis, perm)  23.7 us
    ppermute x11, waiting for transfers between devices, shifted(): return lax.ppermute(array, axis, perm)  21.1 us
    pallas_call x1, Pallas kernels, local_stats(): pl.pallas_call(first_kernel, in_specs=[pl.BlockSpec(memory_space=pltpu.SM...  4.79 us
    pallas_call x1, Pallas kernels, local_stats(): pl.pallas_call(second_kernel, in_specs=[vmem, vmem, vmem], out_specs=vmem...  2.96 us
    unnamed x6, local copies, waits for them, and re-layouts  1.58 us
    pallas_call x1, Pallas kernels, local_terms(): pl.pallas_call(terms_kernel, in_specs=[smem, vmem, vmem, vmem, vmem], out...  1.34 us
  transfers between devices with their start and end apart: 11, of which 8 were waited for; matrix products, arithmetic and copies ran while one was open for 0% of the time, Pallas kernels for 7%

profile of v5, /device:TPU:6, one launch (start us, length us, event | category | flops | bytes accessed | tf_op | source)
XLA Modules:
  0.0 58.4 jit_solution(2334401367748547275)
XLA Ops:
  0.0 0.0 copy-start
  0.0 0.9 %copy-done = bf16[20,2048]{1,0:T(8,128)(2,1)S(1)} copy-done((bf16[20,2048]{1,0:T(8,128)(2,1)S(1)}, bf16[20,2048]{1,0:T(8,128)(2,1)}, u32[]{:S(2)}) %copy-start) | copy-done | bytes 81944
  0.9 0.0 copy-start.2
  0.9 0.7 %copy-done.2 = bf16[2048]{0:T(1024)(128)(2,1)S(1)} copy-done((bf16[2048]{0:T(1024)(128)(2,1)S(1)}, bf16[2048]{0:T(1024)(128)(2,1)}, u32[]{:S(2)}) %copy-start.2) | copy-done | bytes 4120
  1.6 0.0 copy-start.1
  1.6 4.8 %first_stats.1 = (bf16[2048,2048]{1,0:T(8,128)(2,1)S(1)}, f32[24,1024]{1,0:T(8,128)S(1)}, bf16[2048,128]{1,0:T(8,128)(2,1)S(1)}, f32[8,128]{1,0:T(8,128)S(1)}) custom-call(s32[1]{0:T(128)} %bitcast.place, bf16[20,2048]{1,0:T(8,128)(2,1)S(1)} %copy-done, bf16[2048]{0:T(1024)(128)(2,1)S(1)} %copy-done.2, bf16[2048,2048]{1,0:T(8,128)(2,1)} %genotype.1), custom_call_target="tpu_custom_call" | custom-call | tf_op jit(solution)/shard_map/first_stats/pallas_call | solution.py:107
  6.4 2.0 %collective-permute-start = (f32[24,1024]{1,0:T(8,128)S(1)}, f32[24,1024]{1,0:T(8,128)S(1)}, u32[]{:S(2)}, u32[]{:S(2)}) collective-permute-start(f32[24,1024]{1,0:T(8,128)S(1)} %get-tuple-element.14), channel_id=1, source_target_pairs={{0,4},{1,5},{2,6},{3,7},{4,0},{5,1},{6,2},{7,3},{8,12},{9,13},{10,... | collective-permute-start | bytes 294920 | tf_op jit(solution)/shard_map/ppermute | solution.py:19
  8.4 3.0 %second_stats.1 = f32[24,1024]{1,0:T(8,128)S(1)} custom-call(bf16[2048,2048]{1,0:T(8,128)(2,1)S(1)} %get-tuple-element.11.held, bf16[2048,128]{1,0:T(8,128)(2,1)S(1)} %get-tuple-element.12.vec, f32[8,128]{1,0:T(8,128)S(1)} %get-tuple-element.13.vsum), custom_call_target="tpu_custom_call" | custom-call | tf_op jit(solution)/shard_map/second_stats/pallas_call | solution.py:122
  11.4 0.0 collective-permute-done
  11.4 0.1 fusion.3
  11.5 0.9 %collective-permute-start.1 = (f32[24,1024]{1,0:T(8,128)S(1)}, f32[24,1024]{1,0:T(8,128)S(1)}, u32[]{:S(2)}, u32[]{:S(2)}) collective-permute-start(f32[24,1024]{1,0:T(8,128)S(1)} %fusion.3), channel_id=1, source_target_pairs={{0,1},{1,0},{2,3},{3,2},{4,5},{5,4},{6,7},{7,6},{8,9},{9,8},{10,11... | collective-permute-start | bytes 294920 | tf_op jit(solution)/shard_map/ppermute | solution.py:19
  12.4 3.8 %collective-permute-done.1 = f32[24,1024]{1,0:T(8,128)S(1)} collective-permute-done((f32[24,1024]{1,0:T(8,128)S(1)}, f32[24,1024]{1,0:T(8,128)S(1)}, u32[]{:S(2)}, u32[]{:S(2)}) %collective-permute-start.1) | collective-permute-done | bytes 98336 | tf_op jit(solution)/shard_map/ppermute | solution.py:19
  16.2 0.1 fusion.26
  16.3 0.1 fusion.4
  16.4 2.0 %collective-permute-start.2 = (f32[24,1024]{1,0:T(8,128)S(1)}, f32[24,1024]{1,0:T(8,128)S(1)}, u32[]{:S(2)}, u32[]{:S(2)}) collective-permute-start(f32[24,1024]{1,0:T(8,128)S(1)} %fusion.4), channel_id=1, source_target_pairs={{0,3},{1,2},{2,1},{3,0},{4,7},{5,6},{6,5},{7,4},{8,11},{9,10},{10,... | collective-permute-start | bytes 294920 | tf_op jit(solution)/shard_map/ppermute | solution.py:19
  18.4 3.9 %collective-permute-done.2 = f32[24,1024]{1,0:T(8,128)S(1)} collective-permute-done((f32[24,1024]{1,0:T(8,128)S(1)}, f32[24,1024]{1,0:T(8,128)S(1)}, u32[]{:S(2)}, u32[]{:S(2)}) %collective-permute-start.2) | collective-permute-done | bytes 98336 | tf_op jit(solution)/shard_map/ppermute | solution.py:19
  22.3 0.1 fusion.25
  22.4 0.1 fusion.5.own
  22.5 1.7 %collective-permute-start.3 = (f32[24,1024]{1,0:T(8,128)S(1)}, f32[24,1024]{1,0:T(8,128)S(1)}, u32[]{:S(2)}, u32[]{:S(2)}) collective-permute-start(f32[24,1024]{1,0:T(8,128)S(1)} %fusion.5.own), channel_id=1, source_target_pairs={{0,4},{1,5},{2,6},{3,7},{4,0},{5,1},{6,2},{7,3},{8,12},{9,13},{10,... | collective-permute-start | bytes 294920 | tf_op jit(solution)/shard_map/ppermute | solution.py:19
  24.2 0.0 copy-done.1
  24.2 1.1 %own_terms.1.part = f32[176,2048]{1,0:T(8,128)S(1)} custom-call(s32[1]{0:T(128)} %bitcast.place, f32[24,1024]{1,0:T(8,128)S(1)} %fusion.5.own, s32[1,2048]{1,0:T(1,128)S(1)} %bitcast.46, bf16[2048,2048]{1,0:T(8,128)(2,1)S(1)} %get-tuple-element.11.held), custom_call_target="tpu_custom_call" | custom-call | tf_op jit(solution)/shard_map/own_terms/pallas_call | solution.py:216
  25.4 1.8 %collective-permute-done.3.back = f32[24,1024]{1,0:T(8,128)S(1)} collective-permute-done((f32[24,1024]{1,0:T(8,128)S(1)}, f32[24,1024]{1,0:T(8,128)S(1)}, u32[]{:S(2)}, u32[]{:S(2)}) %collective-permute-start.3) | collective-permute-done | bytes 98336 | tf_op jit(solution)/shard_map/ppermute | solution.py:19
  27.2 1.3 %local_terms.1 = (f32[4,4,88,128]{3,2,1,0:T(8,128)S(1)}, f32[4,4,88,128]{3,2,1,0:T(8,128)S(1)}) custom-call(s32[1]{0:T(128)} %bitcast.place, f32[24,1024]{1,0:T(8,128)S(1)} %collective-permute-done.3.back, s32[1,2048]{1,0:T(1,128)S(1)} %bitcast.47, bf16[2048,2048]{1,0:T(8,128)(2,1)S(1)} %get-tuple-element.11.held, f32[176,2048]{1,0:T(8,128)S(1)} %own_terms.1.part), custom_call_target="tpu_custom_call" | custom-call | tf_op jit(solution)/shard_map/local_terms/pallas_call | solution.py:225
  28.6 0.1 collective-permute-start.4
  28.7 2.2 %collective-permute-done.4 = f32[4,4,88,128]{3,2,1,0:T(8,128)S(1)} collective-permute-done((f32[4,4,88,128]{3,2,1,0:T(8,128)S(1)}, f32[4,4,88,128]{3,2,1,0:T(8,128)S(1)}, u32[]{:S(2)}, u32[]{:S(2)}) %collective-permute-start.4) | collective-permute-done | bytes 720928 | tf_op jit(solution)/shard_map/ppermute | solution.py:19
  30.9 0.1 add.88
  31.0 1.7 %collective-permute-start.5 = (f32[4,88,128]{2,1,0:T(8,128)S(1)}, f32[4,88,128]{2,1,0:T(8,128)S(1)}, u32[]{:S(2)}, u32[]{:S(2)}) collective-permute-start(f32[4,88,128]{2,1,0:T(8,128)S(1)} %get-tuple-element.17), channel_id=1, source_target_pairs={{0,64},{8,72},{16,80},{24,88},{32,96},{40,104},{48,112},{56,120},{... | collective-permute-start | bytes 540680 | tf_op jit(solution)/shard_map/ppermute | solution.py:19
  32.7 2.9 %collective-permute-start.7 = (f32[4,88,128]{2,1,0:T(8,128)S(1)}, f32[4,88,128]{2,1,0:T(8,128)S(1)}, u32[]{:S(2)}, u32[]{:S(2)}) collective-permute-start(f32[4,88,128]{2,1,0:T(8,128)S(1)} %get-tuple-element.18), channel_id=1, source_target_pairs={{0,128},{8,136},{16,144},{24,152},{32,160},{40,168},{48,176},{56,1... | collective-permute-start | bytes 540680 | tf_op jit(solution)/shard_map/ppermute | solution.py:19
  35.5 1.3 %collective-permute-start.6 = (f32[4,88,128]{2,1,0:T(8,128)S(1)}, f32[4,88,128]{2,1,0:T(8,128)S(1)}, u32[]{:S(2)}, u32[]{:S(2)}) collective-permute-start(f32[4,88,128]{2,1,0:T(8,128)S(1)} %get-tuple-element.19), channel_id=1, source_target_pairs={{0,192},{8,200},{16,208},{24,216},{32,224},{40,232},{48,240},{56,2... | collective-permute-start | bytes 540680 | tf_op jit(solution)/shard_map/ppermute | solution.py:19
  36.9 2.0 %collective-permute-done.5 = f32[4,88,128]{2,1,0:T(8,128)S(1)} collective-permute-done((f32[4,88,128]{2,1,0:T(8,128)S(1)}, f32[4,88,128]{2,1,0:T(8,128)S(1)}, u32[]{:S(2)}, u32[]{:S(2)}) %collective-permute-start.5) | collective-permute-done | bytes 180256 | tf_op jit(solution)/shard_map/ppermute | solution.py:19
  38.9 5.0 %collective-permute-done.7 = f32[4,88,128]{2,1,0:T(8,128)S(1)} collective-permute-done((f32[4,88,128]{2,1,0:T(8,128)S(1)}, f32[4,88,128]{2,1,0:T(8,128)S(1)}, u32[]{:S(2)}, u32[]{:S(2)}) %collective-permute-start.7) | collective-permute-done | bytes 180256 | tf_op jit(solution)/shard_map/ppermute | solution.py:19
  44.0 0.0 collective-permute-done.6
  44.0 3.4 %collective-permute-start.8 = (f32[88,128]{1,0:T(8,128)S(1)}, f32[88,128]{1,0:T(8,128)S(1)}, u32[]{:S(2)}, u32[]{:S(2)}) collective-permute-start(f32[88,128]{1,0:T(8,128)S(1)} %get-tuple-element.20), channel_id=1, source_target_pairs={{0,16},{8,24},{16,32},{24,40},{32,48},{40,56},{48,0},{56,8},{64,80... | collective-permute-start | bytes 135176 | tf_op jit(solution)/shard_map/ppermute | solution.py:19
  47.4 5.1 %collective-permute-start.10 = (f32[88,128]{1,0:T(8,128)S(1)}, f32[88,128]{1,0:T(8,128)S(1)}, u32[]{:S(2)}, u32[]{:S(2)}) collective-permute-start(f32[88,128]{1,0:T(8,128)S(1)} %get-tuple-element.21), channel_id=1, source_target_pairs={{0,32},{8,40},{16,48},{24,56},{32,0},{40,8},{48,16},{56,24},{64,96... | collective-permute-start | bytes 135176 | tf_op jit(solution)/shard_map/ppermute | solution.py:19
  52.5 2.7 %collective-permute-start.9 = (f32[88,128]{1,0:T(8,128)S(1)}, f32[88,128]{1,0:T(8,128)S(1)}, u32[]{:S(2)}, u32[]{:S(2)}) collective-permute-start(f32[88,128]{1,0:T(8,128)S(1)} %get-tuple-element.22), channel_id=1, source_target_pairs={{0,48},{8,56},{16,0},{24,8},{32,16},{40,24},{48,32},{56,40},{64,11... | collective-permute-start | bytes 135176 | tf_op jit(solution)/shard_map/ppermute | solution.py:19
  55.2 0.0 collective-permute-done.8
  55.2 0.4 collective-permute-done.10
  55.6 1.9 %collective-permute-done.9 = f32[88,128]{1,0:T(8,128)S(1)} collective-permute-done((f32[88,128]{1,0:T(8,128)S(1)}, f32[88,128]{1,0:T(8,128)S(1)}, u32[]{:S(2)}, u32[]{:S(2)}) %collective-permute-start.9) | collective-permute-done | bytes 45088 | tf_op jit(solution)/shard_map/ppermute | solution.py:19
  57.5 0.1 slice.110
  57.6 0.1 fusion.24
  57.7 0.7 %copy.6 = f32[8,21,1,64]{3,2,1,0:T(1,128)} copy(f32[8,21,1,64]{3,0,2,1:T(8,128)S(1)} %fusion.8) | data formatting | bytes 86016 | tf_op jit(solution)/shard_map/reshape | solution.py:256
  (10 shorter events, 0.2 us)
Async XLA Ops:
  0.0 0.9 %copy-start = (bf16[20,2048]{1,0:T(8,128)(2,1)S(1)}, bf16[20,2048]{1,0:T(8,128)(2,1)}, u32[]{:S(2)}) copy-start(bf16[20,2048]{1,0:T(8,128)(2,1)} %probes.1) | copy-start | bytes 245764
  0.9 0.7 %copy-start.2 = (bf16[2048]{0:T(1024)(128)(2,1)S(1)}, bf16[2048]{0:T(1024)(128)(2,1)}, u32[]{:S(2)}) copy-start(bf16[2048]{0:T(1024)(128)(2,1)} %phenotype.1) | copy-start | bytes 12292
  1.6 22.7 %copy-start.1 = (s32[2048]{0:T(1024)S(1)}, s32[2048]{0:T(1024)}, u32[]{:S(2)}) copy-start(s32[2048]{0:T(1024)} %param.5) | copy-start | bytes 24580
  6.4 5.0 %collective-permute-start = (f32[24,1024]{1,0:T(8,128)S(1)}, f32[24,1024]{1,0:T(8,128)S(1)}, u32[]{:S(2)}, u32[]{:S(2)}) collective-permute-start(f32[24,1024]{1,0:T(8,128)S(1)} %get-tuple-element.14), channel_id=1, source_target_pairs={{0,4},{1,5},{2,6},{3,7},{4,0},{5,1},{6,2},{7,3},{8,12},{9,13},{10,... | collective-permute-start | bytes 294920 | tf_op jit(solution)/shard_map/ppermute | solution.py:19
  11.5 4.7 %collective-permute-start.1 = (f32[24,1024]{1,0:T(8,128)S(1)}, f32[24,1024]{1,0:T(8,128)S(1)}, u32[]{:S(2)}, u32[]{:S(2)}) collective-permute-start(f32[24,1024]{1,0:T(8,128)S(1)} %fusion.3), channel_id=1, source_target_pairs={{0,1},{1,0},{2,3},{3,2},{4,5},{5,4},{6,7},{7,6},{8,9},{9,8},{10,11... | collective-permute-start | bytes 294920 | tf_op jit(solution)/shard_map/ppermute | solution.py:19
  16.4 5.9 %collective-permute-start.2 = (f32[24,1024]{1,0:T(8,128)S(1)}, f32[24,1024]{1,0:T(8,128)S(1)}, u32[]{:S(2)}, u32[]{:S(2)}) collective-permute-start(f32[24,1024]{1,0:T(8,128)S(1)} %fusion.4), channel_id=1, source_target_pairs={{0,3},{1,2},{2,1},{3,0},{4,7},{5,6},{6,5},{7,4},{8,11},{9,10},{10,... | collective-permute-start | bytes 294920 | tf_op jit(solution)/shard_map/ppermute | solution.py:19
  22.5 4.7 %collective-permute-start.3 = (f32[24,1024]{1,0:T(8,128)S(1)}, f32[24,1024]{1,0:T(8,128)S(1)}, u32[]{:S(2)}, u32[]{:S(2)}) collective-permute-start(f32[24,1024]{1,0:T(8,128)S(1)} %fusion.5.own), channel_id=1, source_target_pairs={{0,4},{1,5},{2,6},{3,7},{4,0},{5,1},{6,2},{7,3},{8,12},{9,13},{10,... | collective-permute-start | bytes 294920 | tf_op jit(solution)/shard_map/ppermute | solution.py:19
  28.6 2.3 %collective-permute-start.4 = (f32[4,4,88,128]{3,2,1,0:T(8,128)S(1)}, f32[4,4,88,128]{3,2,1,0:T(8,128)S(1)}, u32[]{:S(2)}, u32[]{:S(2)}) collective-permute-start(f32[4,4,88,128]{3,2,1,0:T(8,128)S(1)} %get-tuple-element.16), channel_id=1, source_target_pairs={{0,8},{8,0},{16,24},{24,16},{32,40},{40,32},{48,56},{56,48},{64,72... | collective-permute-start | bytes 2162696 | tf_op jit(solution)/shard_map/ppermute | solution.py:19
  31.0 7.9 %collective-permute-start.5 = (f32[4,88,128]{2,1,0:T(8,128)S(1)}, f32[4,88,128]{2,1,0:T(8,128)S(1)}, u32[]{:S(2)}, u32[]{:S(2)}) collective-permute-start(f32[4,88,128]{2,1,0:T(8,128)S(1)} %get-tuple-element.17), channel_id=1, source_target_pairs={{0,64},{8,72},{16,80},{24,88},{32,96},{40,104},{48,112},{56,120},{... | collective-permute-start | bytes 540680 | tf_op jit(solution)/shard_map/ppermute | solution.py:19
  32.7 11.3 %collective-permute-start.7 = (f32[4,88,128]{2,1,0:T(8,128)S(1)}, f32[4,88,128]{2,1,0:T(8,128)S(1)}, u32[]{:S(2)}, u32[]{:S(2)}) collective-permute-start(f32[4,88,128]{2,1,0:T(8,128)S(1)} %get-tuple-element.18), channel_id=1, source_target_pairs={{0,128},{8,136},{16,144},{24,152},{32,160},{40,168},{48,176},{56,1... | collective-permute-start | bytes 540680 | tf_op jit(solution)/shard_map/ppermute | solution.py:19
  35.5 8.4 %collective-permute-start.6 = (f32[4,88,128]{2,1,0:T(8,128)S(1)}, f32[4,88,128]{2,1,0:T(8,128)S(1)}, u32[]{:S(2)}, u32[]{:S(2)}) collective-permute-start(f32[4,88,128]{2,1,0:T(8,128)S(1)} %get-tuple-element.19), channel_id=1, source_target_pairs={{0,192},{8,200},{16,208},{24,216},{32,224},{40,232},{48,240},{56,2... | collective-permute-start | bytes 540680 | tf_op jit(solution)/shard_map/ppermute | solution.py:19
  44.0 11.1 %collective-permute-start.8 = (f32[88,128]{1,0:T(8,128)S(1)}, f32[88,128]{1,0:T(8,128)S(1)}, u32[]{:S(2)}, u32[]{:S(2)}) collective-permute-start(f32[88,128]{1,0:T(8,128)S(1)} %get-tuple-element.20), channel_id=1, source_target_pairs={{0,16},{8,24},{16,32},{24,40},{32,48},{40,56},{48,0},{56,8},{64,80... | collective-permute-start | bytes 135176 | tf_op jit(solution)/shard_map/ppermute | solution.py:19
  47.4 8.2 %collective-permute-start.10 = (f32[88,128]{1,0:T(8,128)S(1)}, f32[88,128]{1,0:T(8,128)S(1)}, u32[]{:S(2)}, u32[]{:S(2)}) collective-permute-start(f32[88,128]{1,0:T(8,128)S(1)} %get-tuple-element.21), channel_id=1, source_target_pairs={{0,32},{8,40},{16,48},{24,56},{32,0},{40,8},{48,16},{56,24},{64,96... | collective-permute-start | bytes 135176 | tf_op jit(solution)/shard_map/ppermute | solution.py:19
  52.5 5.0 %collective-permute-start.9 = (f32[88,128]{1,0:T(8,128)S(1)}, f32[88,128]{1,0:T(8,128)S(1)}, u32[]{:S(2)}, u32[]{:S(2)}) collective-permute-start(f32[88,128]{1,0:T(8,128)S(1)} %get-tuple-element.22), channel_id=1, source_target_pairs={{0,48},{8,56},{16,0},{24,8},{32,16},{40,24},{48,32},{56,40},{64,11... | collective-permute-start | bytes 135176 | tf_op jit(solution)/shard_map/ppermute | solution.py:19

commit v6 on v5

--- a/solution.py
+++ b/solution.py
@@ -31,11 +31,10 @@
 Z_DOWN = [(i, (i & 25) | ((i - 2) & 6)) for i in range(32)]
 
 
-def block_stats(held, first, vec, vsum):
-    samples = held.shape[1]
-    rows = pl.ds(pl.multiple_of(first, STEP), STEP)
-    acc = jnp.dot(held[rows, :], vec[...], preferred_element_type=jnp.float32)
-    squares, bases = [], []
+def block_side(held, first):
+    samples = held.shape[1]
+    lane = lax.broadcasted_iota(jnp.int32, (64, 128), 1)
+    sides = []
     for r in range(0, STEP, 64):
         part = pl.ds(pl.multiple_of(first + r, 64), 64)
         base = jnp.broadcast_to(held[part, 0:128].astype(jnp.float32)[:, 0:1], (64, 128))
@@ -43,12 +42,16 @@
         for c in range(0, samples, 128):
             dev = held[part, c : c + 128].astype(jnp.float32) - base
             sq = sq + dev * dev
-        squares.append(jnp.sum(sq, axis=1, keepdims=True))
-        bases.append(base)
+        sides.append(jnp.where(lane == SQUARES, jnp.sum(sq, axis=1, keepdims=True), base))
+    return jnp.concatenate(sides, axis=0)
+
+
+def block_stats(held, first, side, vec, vsum):
+    samples = held.shape[1]
+    rows = pl.ds(pl.multiple_of(first, STEP), STEP)
+    acc = jnp.dot(held[rows, :], vec[...], preferred_element_type=jnp.float32)
     lane = lax.broadcasted_iota(jnp.int32, acc.shape, 1)
-    acc = jnp.where(lane == SQUARES, jnp.concatenate(squares, axis=0), acc)
-    acc = jnp.where(lane == VSUM, jnp.concatenate(bases, axis=0), acc)
-    flat = jnp.transpose(acc)[0:ROWS, :]
+    flat = jnp.transpose(jnp.where(lane >= SQUARES, side, acc))[0:ROWS, :]
     mean = flat[MEAN : MEAN + 1] / samples
     apart = mean - flat[VSUM : VSUM + 1]
     spread = jnp.maximum(flat[SQUARES : SQUARES + 1] - samples * apart * apart, 0.0)
@@ -58,7 +61,7 @@
     return jnp.where(row == VSUM, total, flat)
 
 
-def first_kernel(place, probes, phenotype, genotype, held, other, vec, vsum, arrived):
+def hold_kernel(place, genotype, held, side, arrived):
     variants, samples = genotype.shape
     steps = variants // STEP
     ahead = steps // 2
@@ -71,6 +74,21 @@
 
     for i in range(ahead):
         copy(i).start()
+
+    def step(i, carry):
+        copy(i).wait()
+        copy(i + ahead).start()
+        side[pl.ds(pl.multiple_of(i * STEP, STEP), STEP), :] = block_side(held, i * STEP)
+        return carry
+
+    lax.fori_loop(0, ahead, step, 0)
+    for i in range(ahead, steps):
+        copy(i).wait()
+
+
+def first_kernel(held, side, probes, phenotype, other, vec, vsum):
+    samples = held.shape[1]
+    half = held.shape[0] // 2
     row = lax.broadcasted_iota(jnp.int32, (32, samples), 0)
     low = jnp.concatenate([probes[...].astype(jnp.float32), jnp.zeros((12, samples), jnp.float32)], axis=0)
     phen = phenotype[...].astype(jnp.float32).reshape(1, samples)
@@ -80,21 +98,20 @@
     vsum[...] = jnp.dot(jnp.ones((8, samples), jnp.bfloat16), vec[...], preferred_element_type=jnp.float32)
 
     def step(i, carry):
-        copy(i).wait()
-        copy(i + ahead).start()
-        other[:, pl.ds(pl.multiple_of(i * STEP, STEP), STEP)] = block_stats(held, i * STEP, vec, vsum)
+        rows = pl.ds(pl.multiple_of(i * STEP, STEP), STEP)
+        other[:, rows] = block_stats(held, i * STEP, side[rows, :], vec, vsum)
         return carry
 
-    lax.fori_loop(0, ahead, step, 0)
-    for i in range(ahead, steps):
-        copy(i).wait()
+    lax.fori_loop(0, half // STEP, step, 0)
 
 
 def second_kernel(held, vec, vsum, mine):
     half = held.shape[0] // 2
 
     def step(i, carry):
-        mine[:, pl.ds(pl.multiple_of(i * STEP, STEP), STEP)] = block_stats(held, half + i * STEP, vec, vsum)
+        rows = pl.ds(pl.multiple_of(i * STEP, STEP), STEP)
+        first = half + i * STEP
+        mine[:, rows] = block_stats(held, first, block_side(held, first), vec, vsum)
         return carry
 
     lax.fori_loop(0, half // STEP, step, 0)
@@ -104,27 +121,39 @@
     variants, samples = genotype.shape
     vmem = pl.BlockSpec(memory_space=pltpu.VMEM)
     block = jax.ShapeDtypeStruct((ROWS, variants // 2), jnp.float32)
-    held, other, vec, vsum = pl.pallas_call(
-        first_kernel,
-        in_specs=[pl.BlockSpec(memory_space=pltpu.SMEM), vmem, vmem, pl.BlockSpec(memory_space=pltpu.HBM)],
-        out_specs=(vmem, vmem, vmem, vmem),
+    small = pltpu.CompilerParams(vmem_limit_bytes=16 * 1024 * 1024)
+    held, side = pl.pallas_call(
+        hold_kernel,
+        in_specs=[pl.BlockSpec(memory_space=pltpu.SMEM), pl.BlockSpec(memory_space=pltpu.HBM)],
+        out_specs=(vmem, vmem),
         out_shape=(
             jax.ShapeDtypeStruct(genotype.shape, genotype.dtype),
+            jax.ShapeDtypeStruct((variants // 2, 128), jnp.float32),
+        ),
+        scratch_shapes=[pltpu.SemaphoreType.DMA((variants // STEP,))],
+        compiler_params=pltpu.CompilerParams(vmem_limit_bytes=40 * 1024 * 1024),
+        cost_estimate=pl.CostEstimate(flops=40_000_000, bytes_accessed=2 * variants * samples, transcendentals=0),
+        name="hold_genotype",
+    )(place, genotype)
+    other, vec, vsum = pl.pallas_call(
+        first_kernel,
+        in_specs=[vmem, vmem, vmem, vmem],
+        out_specs=(vmem, vmem, vmem),
+        out_shape=(
             block,
             jax.ShapeDtypeStruct((samples, 128), jnp.bfloat16),
             jax.ShapeDtypeStruct((8, 128), jnp.float32),
         ),
-        scratch_shapes=[pltpu.SemaphoreType.DMA((variants // STEP,))],
-        compiler_params=pltpu.CompilerParams(vmem_limit_bytes=40 * 1024 * 1024),
+        compiler_params=small,
         name="first_stats",
-    )(place, probes, phenotype, genotype)
+    )(held, side, probes, phenotype)
     theirs = shifted(other, "smp", ZLO_SWAP)
     mine = pl.pallas_call(
         second_kernel,
         in_specs=[vmem, vmem, vmem],
         out_specs=vmem,
         out_shape=block,
-        compiler_params=pltpu.CompilerParams(vmem_limit_bytes=16 * 1024 * 1024),
+        compiler_params=small,
         name="second_stats",
     )(held, vec, vsum)
     return held, mine, theirs

time: 58.5 us -> 58.4 us (level)
  local copies, waits for them, and re-layouts: 2.51 us -> 0.94 us
  Pallas kernels: 10.2 us -> 11.6 us
    unnamed x6, local copies, waits for them, and re-layouts: 1.58 us -> 0.01 us
    pallas_call x1 -> x2, Pallas kernels: 4.79 us -> 6.34 us  [the longest x1 4.04 us: local_stats(): pl.pallas_call(hold_kernel, in_specs=[pl.BlockSpec(memory_space=pltpu.SME...]
where the time goes in v6:
time: 58.4 us
  starting transfers between devices  24.2 us (41%)
  waiting for transfers between devices  20.8 us (36%)
  Pallas kernels  11.6 us (20%)
  local copies, waits for them, and re-layouts  0.94 us (2%)
  other arithmetic  0.68 us (1%)
    ppermute x11, starting transfers between devices, shifted(): return lax.ppermute(array, axis, perm)  24.2 us
    ppermute x11, waiting for transfers between devices, shifted(): return lax.ppermute(array, axis, perm)  20.8 us
    pallas_call x1, Pallas kernels, local_stats(): pl.pallas_call(hold_kernel, in_specs=[pl.BlockSpec(memory_space=pltpu.SME...  4.04 us
    pallas_call x1, Pallas kernels, local_stats(): pl.pallas_call(second_kernel, in_specs=[vmem, vmem, vmem], out_specs=vmem...  2.8 us
    pallas_call x1, Pallas kernels, local_stats(): pl.pallas_call(first_kernel, in_specs=[vmem, vmem, vmem, vmem], out_specs...  2.3 us
    pallas_call x1, Pallas kernels, local_terms(): pl.pallas_call(terms_kernel, in_specs=[smem, vmem, vmem, vmem, vmem], out...  1.32 us
  transfers between devices with their start and end apart: 11, of which 8 were waited for; matrix products, arithmetic and copies ran while one was open for 0% of the time, Pallas kernels for 7%

profile of v6, /device:TPU:6, one launch (start us, length us, event | category | flops | bytes accessed | tf_op | source)
XLA Modules:
  0.0 58.4 jit_solution(7797654938855707086)
XLA Ops:
  0.0 0.0 copy-start.2
  0.0 0.0 copy-start
  0.0 4.0 %hold_genotype.1 = (bf16[2048,2048]{1,0:T(8,128)(2,1)S(1)}, f32[1024,128]{1,0:T(8,128)S(1)}) custom-call(s32[1]{0:T(128)} %bitcast.place, bf16[2048,2048]{1,0:T(8,128)(2,1)} %genotype.1), custom_call_target="tpu_custom_call" | custom-call | flops 40000000 | bytes 8388608 | tf_op jit(solution)/shard_map/hold_genotype/pallas_call | solution.py:125
  4.1 0.0 copy-done.2
  4.1 0.0 copy-done
  4.1 0.0 copy-start.1
  4.1 2.3 %first_stats.1 = (f32[24,1024]{1,0:T(8,128)S(1)}, bf16[2048,128]{1,0:T(8,128)(2,1)S(1)}, f32[8,128]{1,0:T(8,128)S(1)}) custom-call(bf16[2048,2048]{1,0:T(8,128)(2,1)S(1)} %get-tuple-element.12.held, f32[1024,128]{1,0:T(8,128)S(1)} %get-tuple-element.13.side, bf16[20,2048]{1,0:T(8,128)(2,1)S(1)} %copy-done, bf16[2048]{0:T(1024)(128)(2,1)S(1)} %copy-done.2), custom_call_target="tpu_custom_call" | custom-call | tf_op jit(solution)/shard_map/first_stats/pallas_call | solution.py:138
  6.4 2.0 %collective-permute-start = (f32[24,1024]{1,0:T(8,128)S(1)}, f32[24,1024]{1,0:T(8,128)S(1)}, u32[]{:S(2)}, u32[]{:S(2)}) collective-permute-start(f32[24,1024]{1,0:T(8,128)S(1)} %get-tuple-element.16), channel_id=1, source_target_pairs={{0,4},{1,5},{2,6},{3,7},{4,0},{5,1},{6,2},{7,3},{8,12},{9,13},{10,... | collective-permute-start | bytes 294920 | tf_op jit(solution)/shard_map/ppermute | solution.py:19
  8.4 2.8 %second_stats.1 = f32[24,1024]{1,0:T(8,128)S(1)} custom-call(bf16[2048,2048]{1,0:T(8,128)(2,1)S(1)} %get-tuple-element.12.held, bf16[2048,128]{1,0:T(8,128)(2,1)S(1)} %get-tuple-element.14.vec, f32[8,128]{1,0:T(8,128)S(1)} %get-tuple-element.15.vsum), custom_call_target="tpu_custom_call" | custom-call | tf_op jit(solution)/shard_map/second_stats/pallas_call | solution.py:151
  11.2 0.0 collective-permute-done
  11.3 0.1 fusion.3
  11.3 0.9 %collective-permute-start.1 = (f32[24,1024]{1,0:T(8,128)S(1)}, f32[24,1024]{1,0:T(8,128)S(1)}, u32[]{:S(2)}, u32[]{:S(2)}) collective-permute-start(f32[24,1024]{1,0:T(8,128)S(1)} %fusion.3), channel_id=1, source_target_pairs={{0,1},{1,0},{2,3},{3,2},{4,5},{5,4},{6,7},{7,6},{8,9},{9,8},{10,11... | collective-permute-start | bytes 294920 | tf_op jit(solution)/shard_map/ppermute | solution.py:19
  12.3 3.8 %collective-permute-done.1 = f32[24,1024]{1,0:T(8,128)S(1)} collective-permute-done((f32[24,1024]{1,0:T(8,128)S(1)}, f32[24,1024]{1,0:T(8,128)S(1)}, u32[]{:S(2)}, u32[]{:S(2)}) %collective-permute-start.1) | collective-permute-done | bytes 98336 | tf_op jit(solution)/shard_map/ppermute | solution.py:19
  16.0 0.1 fusion.26
  16.2 0.1 fusion.4
  16.2 2.1 %collective-permute-start.2 = (f32[24,1024]{1,0:T(8,128)S(1)}, f32[24,1024]{1,0:T(8,128)S(1)}, u32[]{:S(2)}, u32[]{:S(2)}) collective-permute-start(f32[24,1024]{1,0:T(8,128)S(1)} %fusion.4), channel_id=1, source_target_pairs={{0,3},{1,2},{2,1},{3,0},{4,7},{5,6},{6,5},{7,4},{8,11},{9,10},{10,... | collective-permute-start | bytes 294920 | tf_op jit(solution)/shard_map/ppermute | solution.py:19
  18.4 3.8 %collective-permute-done.2 = f32[24,1024]{1,0:T(8,128)S(1)} collective-permute-done((f32[24,1024]{1,0:T(8,128)S(1)}, f32[24,1024]{1,0:T(8,128)S(1)}, u32[]{:S(2)}, u32[]{:S(2)}) %collective-permute-start.2) | collective-permute-done | bytes 98336 | tf_op jit(solution)/shard_map/ppermute | solution.py:19
  22.2 0.1 fusion.25
  22.3 0.1 fusion.5.own
  22.4 1.9 %collective-permute-start.3 = (f32[24,1024]{1,0:T(8,128)S(1)}, f32[24,1024]{1,0:T(8,128)S(1)}, u32[]{:S(2)}, u32[]{:S(2)}) collective-permute-start(f32[24,1024]{1,0:T(8,128)S(1)} %fusion.5.own), channel_id=1, source_target_pairs={{0,4},{1,5},{2,6},{3,7},{4,0},{5,1},{6,2},{7,3},{8,12},{9,13},{10,... | collective-permute-start | bytes 294920 | tf_op jit(solution)/shard_map/ppermute | solution.py:19
  24.2 0.0 copy-done.1
  24.2 1.1 %own_terms.1.part = f32[176,2048]{1,0:T(8,128)S(1)} custom-call(s32[1]{0:T(128)} %bitcast.place, f32[24,1024]{1,0:T(8,128)S(1)} %fusion.5.own, s32[1,2048]{1,0:T(1,128)S(1)} %bitcast.46, bf16[2048,2048]{1,0:T(8,128)(2,1)S(1)} %get-tuple-element.12.held), custom_call_target="tpu_custom_call" | custom-call | tf_op jit(solution)/shard_map/own_terms/pallas_call | solution.py:245
  25.4 1.7 %collective-permute-done.3.back = f32[24,1024]{1,0:T(8,128)S(1)} collective-permute-done((f32[24,1024]{1,0:T(8,128)S(1)}, f32[24,1024]{1,0:T(8,128)S(1)}, u32[]{:S(2)}, u32[]{:S(2)}) %collective-permute-start.3) | collective-permute-done | bytes 98336 | tf_op jit(solution)/shard_map/ppermute | solution.py:19
  27.1 1.3 %local_terms.1 = (f32[4,4,88,128]{3,2,1,0:T(8,128)S(1)}, f32[4,4,88,128]{3,2,1,0:T(8,128)S(1)}) custom-call(s32[1]{0:T(128)} %bitcast.place, f32[24,1024]{1,0:T(8,128)S(1)} %collective-permute-done.3.back, s32[1,2048]{1,0:T(1,128)S(1)} %bitcast.47, bf16[2048,2048]{1,0:T(8,128)(2,1)S(1)} %get-tuple-element.12.held, f32[176,2048]{1,0:T(8,128)S(1)} %own_terms.1.part), custom_call_target="tpu_custom_call" | custom-call | tf_op jit(solution)/shard_map/local_terms/pallas_call | solution.py:254
  28.4 0.1 collective-permute-start.4
  28.5 2.2 %collective-permute-done.4 = f32[4,4,88,128]{3,2,1,0:T(8,128)S(1)} collective-permute-done((f32[4,4,88,128]{3,2,1,0:T(8,128)S(1)}, f32[4,4,88,128]{3,2,1,0:T(8,128)S(1)}, u32[]{:S(2)}, u32[]{:S(2)}) %collective-permute-start.4) | collective-permute-done | bytes 720928 | tf_op jit(solution)/shard_map/ppermute | solution.py:19
  30.7 0.1 add.88
  30.8 1.7 %collective-permute-start.5 = (f32[4,88,128]{2,1,0:T(8,128)S(1)}, f32[4,88,128]{2,1,0:T(8,128)S(1)}, u32[]{:S(2)}, u32[]{:S(2)}) collective-permute-start(f32[4,88,128]{2,1,0:T(8,128)S(1)} %get-tuple-element.19), channel_id=1, source_target_pairs={{0,64},{8,72},{16,80},{24,88},{32,96},{40,104},{48,112},{56,120},{... | collective-permute-start | bytes 540680 | tf_op jit(solution)/shard_map/ppermute | solution.py:19
  32.5 2.9 %collective-permute-start.7 = (f32[4,88,128]{2,1,0:T(8,128)S(1)}, f32[4,88,128]{2,1,0:T(8,128)S(1)}, u32[]{:S(2)}, u32[]{:S(2)}) collective-permute-start(f32[4,88,128]{2,1,0:T(8,128)S(1)} %get-tuple-element.20), channel_id=1, source_target_pairs={{0,128},{8,136},{16,144},{24,152},{32,160},{40,168},{48,176},{56,1... | collective-permute-start | bytes 540680 | tf_op jit(solution)/shard_map/ppermute | solution.py:19
  35.4 1.3 %collective-permute-start.6 = (f32[4,88,128]{2,1,0:T(8,128)S(1)}, f32[4,88,128]{2,1,0:T(8,128)S(1)}, u32[]{:S(2)}, u32[]{:S(2)}) collective-permute-start(f32[4,88,128]{2,1,0:T(8,128)S(1)} %get-tuple-element.21), channel_id=1, source_target_pairs={{0,192},{8,200},{16,208},{24,216},{32,224},{40,232},{48,240},{56,2... | collective-permute-start | bytes 540680 | tf_op jit(solution)/shard_map/ppermute | solution.py:19
  36.7 2.0 %collective-permute-done.5 = f32[4,88,128]{2,1,0:T(8,128)S(1)} collective-permute-done((f32[4,88,128]{2,1,0:T(8,128)S(1)}, f32[4,88,128]{2,1,0:T(8,128)S(1)}, u32[]{:S(2)}, u32[]{:S(2)}) %collective-permute-start.5) | collective-permute-done | bytes 180256 | tf_op jit(solution)/shard_map/ppermute | solution.py:19
  38.8 5.0 %collective-permute-done.7 = f32[4,88,128]{2,1,0:T(8,128)S(1)} collective-permute-done((f32[4,88,128]{2,1,0:T(8,128)S(1)}, f32[4,88,128]{2,1,0:T(8,128)S(1)}, u32[]{:S(2)}, u32[]{:S(2)}) %collective-permute-start.7) | collective-permute-done | bytes 180256 | tf_op jit(solution)/shard_map/ppermute | solution.py:19
  43.8 0.0 collective-permute-done.6
  43.9 3.3 %collective-permute-start.8 = (f32[88,128]{1,0:T(8,128)S(1)}, f32[88,128]{1,0:T(8,128)S(1)}, u32[]{:S(2)}, u32[]{:S(2)}) collective-permute-start(f32[88,128]{1,0:T(8,128)S(1)} %get-tuple-element.22), channel_id=1, source_target_pairs={{0,16},{8,24},{16,32},{24,40},{32,48},{40,56},{48,0},{56,8},{64,80... | collective-permute-start | bytes 135176 | tf_op jit(solution)/shard_map/ppermute | solution.py:19
  47.2 5.3 %collective-permute-start.10 = (f32[88,128]{1,0:T(8,128)S(1)}, f32[88,128]{1,0:T(8,128)S(1)}, u32[]{:S(2)}, u32[]{:S(2)}) collective-permute-start(f32[88,128]{1,0:T(8,128)S(1)} %get-tuple-element.23), channel_id=1, source_target_pairs={{0,32},{8,40},{16,48},{24,56},{32,0},{40,8},{48,16},{56,24},{64,96... | collective-permute-start | bytes 135176 | tf_op jit(solution)/shard_map/ppermute | solution.py:19
  52.5 2.7 %collective-permute-start.9 = (f32[88,128]{1,0:T(8,128)S(1)}, f32[88,128]{1,0:T(8,128)S(1)}, u32[]{:S(2)}, u32[]{:S(2)}) collective-permute-start(f32[88,128]{1,0:T(8,128)S(1)} %get-tuple-element.24), channel_id=1, source_target_pairs={{0,48},{8,56},{16,0},{24,8},{32,16},{40,24},{48,32},{56,40},{64,11... | collective-permute-start | bytes 135176 | tf_op jit(solution)/shard_map/ppermute | solution.py:19
  55.1 0.0 collective-permute-done.8
  55.2 0.4 collective-permute-done.10
  55.5 1.9 %collective-permute-done.9 = f32[88,128]{1,0:T(8,128)S(1)} collective-permute-done((f32[88,128]{1,0:T(8,128)S(1)}, f32[88,128]{1,0:T(8,128)S(1)}, u32[]{:S(2)}, u32[]{:S(2)}) %collective-permute-start.9) | collective-permute-done | bytes 45088 | tf_op jit(solution)/shard_map/ppermute | solution.py:19
  57.5 0.1 slice.110
  57.5 0.1 fusion.24
  57.6 0.7 %copy.6 = f32[8,21,1,64]{3,2,1,0:T(1,128)} copy(f32[8,21,1,64]{3,0,2,1:T(8,128)S(1)} %fusion.8) | data formatting | bytes 86016 | tf_op jit(solution)/shard_map/reshape | solution.py:285
  (10 shorter events, 0.2 us)
Async XLA Ops:
  0.0 4.1 %copy-start.2 = (bf16[2048]{0:T(1024)(128)(2,1)S(1)}, bf16[2048]{0:T(1024)(128)(2,1)}, u32[]{:S(2)}) copy-start(bf16[2048]{0:T(1024)(128)(2,1)} %phenotype.1) | copy-start | bytes 12292
  0.0 4.1 %copy-start = (bf16[20,2048]{1,0:T(8,128)(2,1)S(1)}, bf16[20,2048]{1,0:T(8,128)(2,1)}, u32[]{:S(2)}) copy-start(bf16[20,2048]{1,0:T(8,128)(2,1)} %probes.1) | copy-start | bytes 245764
  4.1 20.2 %copy-start.1 = (s32[2048]{0:T(1024)S(1)}, s32[2048]{0:T(1024)}, u32[]{:S(2)}) copy-start(s32[2048]{0:T(1024)} %param.5) | copy-start | bytes 24580
  6.4 4.8 %collective-permute-start = (f32[24,1024]{1,0:T(8,128)S(1)}, f32[24,1024]{1,0:T(8,128)S(1)}, u32[]{:S(2)}, u32[]{:S(2)}) collective-permute-start(f32[24,1024]{1,0:T(8,128)S(1)} %get-tuple-element.16), channel_id=1, source_target_pairs={{0,4},{1,5},{2,6},{3,7},{4,0},{5,1},{6,2},{7,3},{8,12},{9,13},{10,... | collective-permute-start | bytes 294920 | tf_op jit(solution)/shard_map/ppermute | solution.py:19
  11.3 4.7 %collective-permute-start.1 = (f32[24,1024]{1,0:T(8,128)S(1)}, f32[24,1024]{1,0:T(8,128)S(1)}, u32[]{:S(2)}, u32[]{:S(2)}) collective-permute-start(f32[24,1024]{1,0:T(8,128)S(1)} %fusion.3), channel_id=1, source_target_pairs={{0,1},{1,0},{2,3},{3,2},{4,5},{5,4},{6,7},{7,6},{8,9},{9,8},{10,11... | collective-permute-start | bytes 294920 | tf_op jit(solution)/shard_map/ppermute | solution.py:19
  16.2 5.9 %collective-permute-start.2 = (f32[24,1024]{1,0:T(8,128)S(1)}, f32[24,1024]{1,0:T(8,128)S(1)}, u32[]{:S(2)}, u32[]{:S(2)}) collective-permute-start(f32[24,1024]{1,0:T(8,128)S(1)} %fusion.4), channel_id=1, source_target_pairs={{0,3},{1,2},{2,1},{3,0},{4,7},{5,6},{6,5},{7,4},{8,11},{9,10},{10,... | collective-permute-start | bytes 294920 | tf_op jit(solution)/shard_map/ppermute | solution.py:19
  22.4 4.7 %collective-permute-start.3 = (f32[24,1024]{1,0:T(8,128)S(1)}, f32[24,1024]{1,0:T(8,128)S(1)}, u32[]{:S(2)}, u32[]{:S(2)}) collective-permute-start(f32[24,1024]{1,0:T(8,128)S(1)} %fusion.5.own), channel_id=1, source_target_pairs={{0,4},{1,5},{2,6},{3,7},{4,0},{5,1},{6,2},{7,3},{8,12},{9,13},{10,... | collective-permute-start | bytes 294920 | tf_op jit(solution)/shard_map/ppermute | solution.py:19
  28.4 2.3 %collective-permute-start.4 = (f32[4,4,88,128]{3,2,1,0:T(8,128)S(1)}, f32[4,4,88,128]{3,2,1,0:T(8,128)S(1)}, u32[]{:S(2)}, u32[]{:S(2)}) collective-permute-start(f32[4,4,88,128]{3,2,1,0:T(8,128)S(1)} %get-tuple-element.18), channel_id=1, source_target_pairs={{0,8},{8,0},{16,24},{24,16},{32,40},{40,32},{48,56},{56,48},{64,72... | collective-permute-start | bytes 2162696 | tf_op jit(solution)/shard_map/ppermute | solution.py:19
  30.8 7.9 %collective-permute-start.5 = (f32[4,88,128]{2,1,0:T(8,128)S(1)}, f32[4,88,128]{2,1,0:T(8,128)S(1)}, u32[]{:S(2)}, u32[]{:S(2)}) collective-permute-start(f32[4,88,128]{2,1,0:T(8,128)S(1)} %get-tuple-element.19), channel_id=1, source_target_pairs={{0,64},{8,72},{16,80},{24,88},{32,96},{40,104},{48,112},{56,120},{... | collective-permute-start | bytes 540680 | tf_op jit(solution)/shard_map/ppermute | solution.py:19
  32.5 11.3 %collective-permute-start.7 = (f32[4,88,128]{2,1,0:T(8,128)S(1)}, f32[4,88,128]{2,1,0:T(8,128)S(1)}, u32[]{:S(2)}, u32[]{:S(2)}) collective-permute-start(f32[4,88,128]{2,1,0:T(8,128)S(1)} %get-tuple-element.20), channel_id=1, source_target_pairs={{0,128},{8,136},{16,144},{24,152},{32,160},{40,168},{48,176},{56,1... | collective-permute-start | bytes 540680 | tf_op jit(solution)/shard_map/ppermute | solution.py:19
  35.4 8.4 %collective-permute-start.6 = (f32[4,88,128]{2,1,0:T(8,128)S(1)}, f32[4,88,128]{2,1,0:T(8,128)S(1)}, u32[]{:S(2)}, u32[]{:S(2)}) collective-permute-start(f32[4,88,128]{2,1,0:T(8,128)S(1)} %get-tuple-element.21), channel_id=1, source_target_pairs={{0,192},{8,200},{16,208},{24,216},{32,224},{40,232},{48,240},{56,2... | collective-permute-start | bytes 540680 | tf_op jit(solution)/shard_map/ppermute | solution.py:19
  43.9 11.3 %collective-permute-start.8 = (f32[88,128]{1,0:T(8,128)S(1)}, f32[88,128]{1,0:T(8,128)S(1)}, u32[]{:S(2)}, u32[]{:S(2)}) collective-permute-start(f32[88,128]{1,0:T(8,128)S(1)} %get-tuple-element.22), channel_id=1, source_target_pairs={{0,16},{8,24},{16,32},{24,40},{32,48},{40,56},{48,0},{56,8},{64,80... | collective-permute-start | bytes 135176 | tf_op jit(solution)/shard_map/ppermute | solution.py:19
  47.2 8.3 %collective-permute-start.10 = (f32[88,128]{1,0:T(8,128)S(1)}, f32[88,128]{1,0:T(8,128)S(1)}, u32[]{:S(2)}, u32[]{:S(2)}) collective-permute-start(f32[88,128]{1,0:T(8,128)S(1)} %get-tuple-element.23), channel_id=1, source_target_pairs={{0,32},{8,40},{16,48},{24,56},{32,0},{40,8},{48,16},{56,24},{64,96... | collective-permute-start | bytes 135176 | tf_op jit(solution)/shard_map/ppermute | solution.py:19
  52.5 5.0 %collective-permute-start.9 = (f32[88,128]{1,0:T(8,128)S(1)}, f32[88,128]{1,0:T(8,128)S(1)}, u32[]{:S(2)}, u32[]{:S(2)}) collective-permute-start(f32[88,128]{1,0:T(8,128)S(1)} %get-tuple-element.24), channel_id=1, source_target_pairs={{0,48},{8,56},{16,0},{24,8},{32,16},{40,24},{48,32},{56,40},{64,11... | collective-permute-start | bytes 135176 | tf_op jit(solution)/shard_map/ppermute | solution.py:19

commit v7 on v6

--- a/solution.py
+++ b/solution.py
@@ -75,9 +75,15 @@
     for i in range(ahead):
         copy(i).start()
 
+    copy(0).wait()
+    for i in range(ahead, steps):
+        copy(i).start()
+
     def step(i, carry):
-        copy(i).wait()
-        copy(i + ahead).start()
+        @pl.when(i > 0)
+        def _():
+            copy(i).wait()
+
         side[pl.ds(pl.multiple_of(i * STEP, STEP), STEP), :] = block_side(held, i * STEP)
         return carry
 

time: 58.4 us -> 58.2 us (level)
  no operation moved by 1% of the time
where the time goes in v7:
time: 58.2 us; the launch traced here: 58.1 us
  starting transfers between devices  24.2 us (42%)
  waiting for transfers between devices  20.8 us (36%)
  Pallas kernels  11.3 us (19%)
  local copies, waits for them, and re-layouts  0.94 us (2%)
  other arithmetic  0.68 us (1%)
    ppermute x11, starting transfers between devices, shifted(): return lax.ppermute(array, axis, perm)  24.2 us
    ppermute x11, waiting for transfers between devices, shifted(): return lax.ppermute(array, axis, perm)  20.8 us
    pallas_call x1, Pallas kernels, local_stats(): pl.pallas_call(hold_kernel, in_specs=[pl.BlockSpec(memory_space=pltpu.SME...  3.77 us
    pallas_call x1, Pallas kernels, local_stats(): pl.pallas_call(second_kernel, in_specs=[vmem, vmem, vmem], out_specs=vmem...  2.8 us
    pallas_call x1, Pallas kernels, local_stats(): pl.pallas_call(first_kernel, in_specs=[vmem, vmem, vmem, vmem], out_specs...  2.3 us
    pallas_call x1, Pallas kernels, local_terms(): pl.pallas_call(terms_kernel, in_specs=[smem, vmem, vmem, vmem, vmem], out...  1.32 us
  transfers between devices with their start and end apart: 11, of which 8 were waited for; matrix products, arithmetic and copies ran while one was open for 0% of the time, Pallas kernels for 7%

profile of v7, /device:TPU:6, one launch (start us, length us, event | category | flops | bytes accessed | tf_op | source)
XLA Modules:
  0.0 58.1 jit_solution(5038290807868319696)
XLA Ops:
  0.0 0.0 copy-start.2
  0.0 0.0 copy-start
  0.0 3.8 %hold_genotype.1 = (bf16[2048,2048]{1,0:T(8,128)(2,1)S(1)}, f32[1024,128]{1,0:T(8,128)S(1)}) custom-call(s32[1]{0:T(128)} %bitcast.place, bf16[2048,2048]{1,0:T(8,128)(2,1)} %genotype.1), custom_call_target="tpu_custom_call" | custom-call | flops 40000000 | bytes 8388608 | tf_op jit(solution)/shard_map/hold_genotype/pallas_call | solution.py:131
  3.8 0.0 copy-done.2
  3.8 0.0 copy-done
  3.8 0.0 copy-start.1
  3.8 2.3 %first_stats.1 = (f32[24,1024]{1,0:T(8,128)S(1)}, bf16[2048,128]{1,0:T(8,128)(2,1)S(1)}, f32[8,128]{1,0:T(8,128)S(1)}) custom-call(bf16[2048,2048]{1,0:T(8,128)(2,1)S(1)} %get-tuple-element.12.held, f32[1024,128]{1,0:T(8,128)S(1)} %get-tuple-element.13.side, bf16[20,2048]{1,0:T(8,128)(2,1)S(1)} %copy-done, bf16[2048]{0:T(1024)(128)(2,1)S(1)} %copy-done.2), custom_call_target="tpu_custom_call" | custom-call | tf_op jit(solution)/shard_map/first_stats/pallas_call | solution.py:144
  6.1 2.0 %collective-permute-start = (f32[24,1024]{1,0:T(8,128)S(1)}, f32[24,1024]{1,0:T(8,128)S(1)}, u32[]{:S(2)}, u32[]{:S(2)}) collective-permute-start(f32[24,1024]{1,0:T(8,128)S(1)} %get-tuple-element.16), channel_id=1, source_target_pairs={{0,4},{1,5},{2,6},{3,7},{4,0},{5,1},{6,2},{7,3},{8,12},{9,13},{10,... | collective-permute-start | bytes 294920 | tf_op jit(solution)/shard_map/ppermute | solution.py:19
  8.1 2.8 %second_stats.1 = f32[24,1024]{1,0:T(8,128)S(1)} custom-call(bf16[2048,2048]{1,0:T(8,128)(2,1)S(1)} %get-tuple-element.12.held, bf16[2048,128]{1,0:T(8,128)(2,1)S(1)} %get-tuple-element.14.vec, f32[8,128]{1,0:T(8,128)S(1)} %get-tuple-element.15.vsum), custom_call_target="tpu_custom_call" | custom-call | tf_op jit(solution)/shard_map/second_stats/pallas_call | solution.py:157
  10.9 0.0 collective-permute-done
  11.0 0.1 fusion.3
  11.1 0.9 %collective-permute-start.1 = (f32[24,1024]{1,0:T(8,128)S(1)}, f32[24,1024]{1,0:T(8,128)S(1)}, u32[]{:S(2)}, u32[]{:S(2)}) collective-permute-start(f32[24,1024]{1,0:T(8,128)S(1)} %fusion.3), channel_id=1, source_target_pairs={{0,1},{1,0},{2,3},{3,2},{4,5},{5,4},{6,7},{7,6},{8,9},{9,8},{10,11... | collective-permute-start | bytes 294920 | tf_op jit(solution)/shard_map/ppermute | solution.py:19
  12.0 3.8 %collective-permute-done.1 = f32[24,1024]{1,0:T(8,128)S(1)} collective-permute-done((f32[24,1024]{1,0:T(8,128)S(1)}, f32[24,1024]{1,0:T(8,128)S(1)}, u32[]{:S(2)}, u32[]{:S(2)}) %collective-permute-start.1) | collective-permute-done | bytes 98336 | tf_op jit(solution)/shard_map/ppermute | solution.py:19
  15.8 0.1 fusion.26
  15.9 0.1 fusion.4
  16.0 2.1 %collective-permute-start.2 = (f32[24,1024]{1,0:T(8,128)S(1)}, f32[24,1024]{1,0:T(8,128)S(1)}, u32[]{:S(2)}, u32[]{:S(2)}) collective-permute-start(f32[24,1024]{1,0:T(8,128)S(1)} %fusion.4), channel_id=1, source_target_pairs={{0,3},{1,2},{2,1},{3,0},{4,7},{5,6},{6,5},{7,4},{8,11},{9,10},{10,... | collective-permute-start | bytes 294920 | tf_op jit(solution)/shard_map/ppermute | solution.py:19
  18.1 3.8 %collective-permute-done.2 = f32[24,1024]{1,0:T(8,128)S(1)} collective-permute-done((f32[24,1024]{1,0:T(8,128)S(1)}, f32[24,1024]{1,0:T(8,128)S(1)}, u32[]{:S(2)}, u32[]{:S(2)}) %collective-permute-start.2) | collective-permute-done | bytes 98336 | tf_op jit(solution)/shard_map/ppermute | solution.py:19
  21.9 0.1 fusion.25
  22.0 0.1 fusion.5.own
  22.1 1.9 %collective-permute-start.3 = (f32[24,1024]{1,0:T(8,128)S(1)}, f32[24,1024]{1,0:T(8,128)S(1)}, u32[]{:S(2)}, u32[]{:S(2)}) collective-permute-start(f32[24,1024]{1,0:T(8,128)S(1)} %fusion.5.own), channel_id=1, source_target_pairs={{0,4},{1,5},{2,6},{3,7},{4,0},{5,1},{6,2},{7,3},{8,12},{9,13},{10,... | collective-permute-start | bytes 294920 | tf_op jit(solution)/shard_map/ppermute | solution.py:19
  24.0 0.0 copy-done.1
  24.0 1.1 %own_terms.1.part = f32[176,2048]{1,0:T(8,128)S(1)} custom-call(s32[1]{0:T(128)} %bitcast.place, f32[24,1024]{1,0:T(8,128)S(1)} %fusion.5.own, s32[1,2048]{1,0:T(1,128)S(1)} %bitcast.46, bf16[2048,2048]{1,0:T(8,128)(2,1)S(1)} %get-tuple-element.12.held), custom_call_target="tpu_custom_call" | custom-call | tf_op jit(solution)/shard_map/own_terms/pallas_call | solution.py:251
  25.1 1.7 %collective-permute-done.3.back = f32[24,1024]{1,0:T(8,128)S(1)} collective-permute-done((f32[24,1024]{1,0:T(8,128)S(1)}, f32[24,1024]{1,0:T(8,128)S(1)}, u32[]{:S(2)}, u32[]{:S(2)}) %collective-permute-start.3) | collective-permute-done | bytes 98336 | tf_op jit(solution)/shard_map/ppermute | solution.py:19
  26.8 1.3 %local_terms.1 = (f32[4,4,88,128]{3,2,1,0:T(8,128)S(1)}, f32[4,4,88,128]{3,2,1,0:T(8,128)S(1)}) custom-call(s32[1]{0:T(128)} %bitcast.place, f32[24,1024]{1,0:T(8,128)S(1)} %collective-permute-done.3.back, s32[1,2048]{1,0:T(1,128)S(1)} %bitcast.47, bf16[2048,2048]{1,0:T(8,128)(2,1)S(1)} %get-tuple-element.12.held, f32[176,2048]{1,0:T(8,128)S(1)} %own_terms.1.part), custom_call_target="tpu_custom_call" | custom-call | tf_op jit(solution)/shard_map/local_terms/pallas_call | solution.py:260
  28.1 0.1 collective-permute-start.4
  28.2 2.2 %collective-permute-done.4 = f32[4,4,88,128]{3,2,1,0:T(8,128)S(1)} collective-permute-done((f32[4,4,88,128]{3,2,1,0:T(8,128)S(1)}, f32[4,4,88,128]{3,2,1,0:T(8,128)S(1)}, u32[]{:S(2)}, u32[]{:S(2)}) %collective-permute-start.4) | collective-permute-done | bytes 720928 | tf_op jit(solution)/shard_map/ppermute | solution.py:19
  30.4 0.1 add.88
  30.5 1.7 %collective-permute-start.5 = (f32[4,88,128]{2,1,0:T(8,128)S(1)}, f32[4,88,128]{2,1,0:T(8,128)S(1)}, u32[]{:S(2)}, u32[]{:S(2)}) collective-permute-start(f32[4,88,128]{2,1,0:T(8,128)S(1)} %get-tuple-element.19), channel_id=1, source_target_pairs={{0,64},{8,72},{16,80},{24,88},{32,96},{40,104},{48,112},{56,120},{... | collective-permute-start | bytes 540680 | tf_op jit(solution)/shard_map/ppermute | solution.py:19
  32.2 2.9 %collective-permute-start.7 = (f32[4,88,128]{2,1,0:T(8,128)S(1)}, f32[4,88,128]{2,1,0:T(8,128)S(1)}, u32[]{:S(2)}, u32[]{:S(2)}) collective-permute-start(f32[4,88,128]{2,1,0:T(8,128)S(1)} %get-tuple-element.20), channel_id=1, source_target_pairs={{0,128},{8,136},{16,144},{24,152},{32,160},{40,168},{48,176},{56,1... | collective-permute-start | bytes 540680 | tf_op jit(solution)/shard_map/ppermute | solution.py:19
  35.1 1.3 %collective-permute-start.6 = (f32[4,88,128]{2,1,0:T(8,128)S(1)}, f32[4,88,128]{2,1,0:T(8,128)S(1)}, u32[]{:S(2)}, u32[]{:S(2)}) collective-permute-start(f32[4,88,128]{2,1,0:T(8,128)S(1)} %get-tuple-element.21), channel_id=1, source_target_pairs={{0,192},{8,200},{16,208},{24,216},{32,224},{40,232},{48,240},{56,2... | collective-permute-start | bytes 540680 | tf_op jit(solution)/shard_map/ppermute | solution.py:19
  36.4 2.0 %collective-permute-done.5 = f32[4,88,128]{2,1,0:T(8,128)S(1)} collective-permute-done((f32[4,88,128]{2,1,0:T(8,128)S(1)}, f32[4,88,128]{2,1,0:T(8,128)S(1)}, u32[]{:S(2)}, u32[]{:S(2)}) %collective-permute-start.5) | collective-permute-done | bytes 180256 | tf_op jit(solution)/shard_map/ppermute | solution.py:19
  38.5 5.0 %collective-permute-done.7 = f32[4,88,128]{2,1,0:T(8,128)S(1)} collective-permute-done((f32[4,88,128]{2,1,0:T(8,128)S(1)}, f32[4,88,128]{2,1,0:T(8,128)S(1)}, u32[]{:S(2)}, u32[]{:S(2)}) %collective-permute-start.7) | collective-permute-done | bytes 180256 | tf_op jit(solution)/shard_map/ppermute | solution.py:19
  43.5 0.0 collective-permute-done.6
  43.6 3.3 %collective-permute-start.8 = (f32[88,128]{1,0:T(8,128)S(1)}, f32[88,128]{1,0:T(8,128)S(1)}, u32[]{:S(2)}, u32[]{:S(2)}) collective-permute-start(f32[88,128]{1,0:T(8,128)S(1)} %get-tuple-element.22), channel_id=1, source_target_pairs={{0,16},{8,24},{16,32},{24,40},{32,48},{40,56},{48,0},{56,8},{64,80... | collective-permute-start | bytes 135176 | tf_op jit(solution)/shard_map/ppermute | solution.py:19
  47.0 5.3 %collective-permute-start.10 = (f32[88,128]{1,0:T(8,128)S(1)}, f32[88,128]{1,0:T(8,128)S(1)}, u32[]{:S(2)}, u32[]{:S(2)}) collective-permute-start(f32[88,128]{1,0:T(8,128)S(1)} %get-tuple-element.23), channel_id=1, source_target_pairs={{0,32},{8,40},{16,48},{24,56},{32,0},{40,8},{48,16},{56,24},{64,96... | collective-permute-start | bytes 135176 | tf_op jit(solution)/shard_map/ppermute | solution.py:19
  52.2 2.7 %collective-permute-start.9 = (f32[88,128]{1,0:T(8,128)S(1)}, f32[88,128]{1,0:T(8,128)S(1)}, u32[]{:S(2)}, u32[]{:S(2)}) collective-permute-start(f32[88,128]{1,0:T(8,128)S(1)} %get-tuple-element.24), channel_id=1, source_target_pairs={{0,48},{8,56},{16,0},{24,8},{32,16},{40,24},{48,32},{56,40},{64,11... | collective-permute-start | bytes 135176 | tf_op jit(solution)/shard_map/ppermute | solution.py:19
  54.9 0.0 collective-permute-done.8
  54.9 0.4 collective-permute-done.10
  55.3 1.9 %collective-permute-done.9 = f32[88,128]{1,0:T(8,128)S(1)} collective-permute-done((f32[88,128]{1,0:T(8,128)S(1)}, f32[88,128]{1,0:T(8,128)S(1)}, u32[]{:S(2)}, u32[]{:S(2)}) %collective-permute-start.9) | collective-permute-done | bytes 45088 | tf_op jit(solution)/shard_map/ppermute | solution.py:19
  57.2 0.1 slice.110
  57.3 0.1 fusion.24
  57.4 0.7 %copy.6 = f32[8,21,1,64]{3,2,1,0:T(1,128)} copy(f32[8,21,1,64]{3,0,2,1:T(8,128)S(1)} %fusion.8) | data formatting | bytes 86016 | tf_op jit(solution)/shard_map/reshape | solution.py:291
  (10 shorter events, 0.2 us)
Async XLA Ops:
  0.0 3.8 %copy-start.2 = (bf16[2048]{0:T(1024)(128)(2,1)S(1)}, bf16[2048]{0:T(1024)(128)(2,1)}, u32[]{:S(2)}) copy-start(bf16[2048]{0:T(1024)(128)(2,1)} %phenotype.1) | copy-start | bytes 12292
  0.0 3.8 %copy-start = (bf16[20,2048]{1,0:T(8,128)(2,1)S(1)}, bf16[20,2048]{1,0:T(8,128)(2,1)}, u32[]{:S(2)}) copy-start(bf16[20,2048]{1,0:T(8,128)(2,1)} %probes.1) | copy-start | bytes 245764
  3.8 20.2 %copy-start.1 = (s32[2048]{0:T(1024)S(1)}, s32[2048]{0:T(1024)}, u32[]{:S(2)}) copy-start(s32[2048]{0:T(1024)} %param.5) | copy-start | bytes 24580
  6.1 4.8 %collective-permute-start = (f32[24,1024]{1,0:T(8,128)S(1)}, f32[24,1024]{1,0:T(8,128)S(1)}, u32[]{:S(2)}, u32[]{:S(2)}) collective-permute-start(f32[24,1024]{1,0:T(8,128)S(1)} %get-tuple-element.16), channel_id=1, source_target_pairs={{0,4},{1,5},{2,6},{3,7},{4,0},{5,1},{6,2},{7,3},{8,12},{9,13},{10,... | collective-permute-start | bytes 294920 | tf_op jit(solution)/shard_map/ppermute | solution.py:19
  11.1 4.7 %collective-permute-start.1 = (f32[24,1024]{1,0:T(8,128)S(1)}, f32[24,1024]{1,0:T(8,128)S(1)}, u32[]{:S(2)}, u32[]{:S(2)}) collective-permute-start(f32[24,1024]{1,0:T(8,128)S(1)} %fusion.3), channel_id=1, source_target_pairs={{0,1},{1,0},{2,3},{3,2},{4,5},{5,4},{6,7},{7,6},{8,9},{9,8},{10,11... | collective-permute-start | bytes 294920 | tf_op jit(solution)/shard_map/ppermute | solution.py:19
  16.0 5.9 %collective-permute-start.2 = (f32[24,1024]{1,0:T(8,128)S(1)}, f32[24,1024]{1,0:T(8,128)S(1)}, u32[]{:S(2)}, u32[]{:S(2)}) collective-permute-start(f32[24,1024]{1,0:T(8,128)S(1)} %fusion.4), channel_id=1, source_target_pairs={{0,3},{1,2},{2,1},{3,0},{4,7},{5,6},{6,5},{7,4},{8,11},{9,10},{10,... | collective-permute-start | bytes 294920 | tf_op jit(solution)/shard_map/ppermute | solution.py:19
  22.1 4.7 %collective-permute-start.3 = (f32[24,1024]{1,0:T(8,128)S(1)}, f32[24,1024]{1,0:T(8,128)S(1)}, u32[]{:S(2)}, u32[]{:S(2)}) collective-permute-start(f32[24,1024]{1,0:T(8,128)S(1)} %fusion.5.own), channel_id=1, source_target_pairs={{0,4},{1,5},{2,6},{3,7},{4,0},{5,1},{6,2},{7,3},{8,12},{9,13},{10,... | collective-permute-start | bytes 294920 | tf_op jit(solution)/shard_map/ppermute | solution.py:19
  28.1 2.3 %collective-permute-start.4 = (f32[4,4,88,128]{3,2,1,0:T(8,128)S(1)}, f32[4,4,88,128]{3,2,1,0:T(8,128)S(1)}, u32[]{:S(2)}, u32[]{:S(2)}) collective-permute-start(f32[4,4,88,128]{3,2,1,0:T(8,128)S(1)} %get-tuple-element.18), channel_id=1, source_target_pairs={{0,8},{8,0},{16,24},{24,16},{32,40},{40,32},{48,56},{56,48},{64,72... | collective-permute-start | bytes 2162696 | tf_op jit(solution)/shard_map/ppermute | solution.py:19
  30.5 7.9 %collective-permute-start.5 = (f32[4,88,128]{2,1,0:T(8,128)S(1)}, f32[4,88,128]{2,1,0:T(8,128)S(1)}, u32[]{:S(2)}, u32[]{:S(2)}) collective-permute-start(f32[4,88,128]{2,1,0:T(8,128)S(1)} %get-tuple-element.19), channel_id=1, source_target_pairs={{0,64},{8,72},{16,80},{24,88},{32,96},{40,104},{48,112},{56,120},{... | collective-permute-start | bytes 540680 | tf_op jit(solution)/shard_map/ppermute | solution.py:19
  32.2 11.3 %collective-permute-start.7 = (f32[4,88,128]{2,1,0:T(8,128)S(1)}, f32[4,88,128]{2,1,0:T(8,128)S(1)}, u32[]{:S(2)}, u32[]{:S(2)}) collective-permute-start(f32[4,88,128]{2,1,0:T(8,128)S(1)} %get-tuple-element.20), channel_id=1, source_target_pairs={{0,128},{8,136},{16,144},{24,152},{32,160},{40,168},{48,176},{56,1... | collective-permute-start | bytes 540680 | tf_op jit(solution)/shard_map/ppermute | solution.py:19
  35.1 8.4 %collective-permute-start.6 = (f32[4,88,128]{2,1,0:T(8,128)S(1)}, f32[4,88,128]{2,1,0:T(8,128)S(1)}, u32[]{:S(2)}, u32[]{:S(2)}) collective-permute-start(f32[4,88,128]{2,1,0:T(8,128)S(1)} %get-tuple-element.21), channel_id=1, source_target_pairs={{0,192},{8,200},{16,208},{24,216},{32,224},{40,232},{48,240},{56,2... | collective-permute-start | bytes 540680 | tf_op jit(solution)/shard_map/ppermute | solution.py:19
  43.6 11.3 %collective-permute-start.8 = (f32[88,128]{1,0:T(8,128)S(1)}, f32[88,128]{1,0:T(8,128)S(1)}, u32[]{:S(2)}, u32[]{:S(2)}) collective-permute-start(f32[88,128]{1,0:T(8,128)S(1)} %get-tuple-element.22), channel_id=1, source_target_pairs={{0,16},{8,24},{16,32},{24,40},{32,48},{40,56},{48,0},{56,8},{64,80... | collective-permute-start | bytes 135176 | tf_op jit(solution)/shard_map/ppermute | solution.py:19
  47.0 8.3 %collective-permute-start.10 = (f32[88,128]{1,0:T(8,128)S(1)}, f32[88,128]{1,0:T(8,128)S(1)}, u32[]{:S(2)}, u32[]{:S(2)}) collective-permute-start(f32[88,128]{1,0:T(8,128)S(1)} %get-tuple-element.23), channel_id=1, source_target_pairs={{0,32},{8,40},{16,48},{24,56},{32,0},{40,8},{48,16},{56,24},{64,96... | collective-permute-start | bytes 135176 | tf_op jit(solution)/shard_map/ppermute | solution.py:19
  52.2 5.0 %collective-permute-start.9 = (f32[88,128]{1,0:T(8,128)S(1)}, f32[88,128]{1,0:T(8,128)S(1)}, u32[]{:S(2)}, u32[]{:S(2)}) collective-permute-start(f32[88,128]{1,0:T(8,128)S(1)} %get-tuple-element.24), channel_id=1, source_target_pairs={{0,48},{8,56},{16,0},{24,8},{32,16},{40,24},{48,32},{56,40},{64,11... | collective-permute-start | bytes 135176 | tf_op jit(solution)/shard_map/ppermute | solution.py:19
